TPU v7x, 256 devices: a whole 4x4x8 slice. The times are simulated.
256 devices in a mesh: depth: 16 (over z, core), gx: 16 (over y, x).
Axes of the slice: x: 4, y: 4, z: 8, core: 2. Of those that a mesh axis runs over, the one named last changes fastest.
Arguments:
- pressure_now: float32 [4, 512, 512, 128], P(None, 'gx', 'depth'), may hold values from -6 to 6
- pressure_before: float32 [4, 512, 512, 128], P(None, 'gx', 'depth'), may hold values from -6 to 6
- class_map: int32 [512, 512, 128], P('gx', 'depth'), may hold values from 0 to 7
- courant_sq: float32 [8], replicated, may hold values from 0.02 to 0.12
- source_cells: int32 [4, 3], replicated, may hold values from 0 to 511, as said below
- source_wavelet: float32 [8, 4], replicated, may hold values from -6 to 6
- layer_start: int32 [1], replicated, may hold values from 488 to 496
Outputs:
- pressure_final: float32 [4, 512, 512, 128], P(None, 'gx', 'depth')
- pressure_prior: float32 [4, 512, 512, 128], P(None, 'gx', 'depth')
Inputs may be any that keep to these rules, and one draw needn't show every extreme that they name: `source_cells`: each row holds a cell inside the grid: x below 512, depth below 512, y below 128; shot 0 sits at the last cell along every dimension and shot 1 at cell (0, 0, 0).
All inputs are finite; a program needn't handle non-finite values.
Results may differ from a plain program's by a relative error of at most 0.00002.
Values sent between devices are 32-bit elements; how exact they have to be, the bound alone decides.
No kernel may reach another device: no remote copies, remote signals or barrier semaphores. Data moves between devices by JAX's collectives and lax.ppermute only.
A program may use at most 128 MiB of HBM per device.

v0:
```python
import jax
import jax.numpy as jnp
from jax import lax
from jax.sharding import PartitionSpec as P

ITERS = 8


COEFFS = (-205.0 / 72.0, 8.0 / 5.0, -1.0 / 5.0, 8.0 / 315.0, -1.0 / 560.0)
DAMPING = 0.3


def padded_2(shard, sides, width):
    edges = {}
    for axis, dim in sides:
        peers, length = (lax.axis_size(axis), shard.shape[dim])
        up = [(i, (i + 1) % peers) for i in range(peers - 1)]
        last = lax.slice_in_dim(shard, length - width, length, axis=dim)
        leading = lax.slice_in_dim(shard, 0, width, axis=dim)
        edges[dim] = (
            lax.ppermute(last, axis, up),
            lax.ppermute(leading, axis, [(b, a) for a, b in up]),
        )
    done = []
    for _, dim in sides:
        low, high = edges[dim]
        around = [(width, width) if d in done else (0, 0) for d in range(shard.ndim)]
        shard = jnp.concatenate([jnp.pad(low, around), shard, jnp.pad(high, around)], axis=dim)
        done.append(dim)
    return shard


def laplace(padded, rows, depth):
    center = padded[:, 4 : 4 + rows, 4 : 4 + depth, :]
    total = 3.0 * COEFFS[0] * center
    side_y = jnp.pad(center, ((0, 0), (0, 0), (0, 0), (4, 4)))
    width = center.shape[3]
    for k in range(1, 5):
        pair = (
            padded[:, 4 + k : 4 + k + rows, 4 : 4 + depth, :]
            + padded[:, 4 - k : 4 - k + rows, 4 : 4 + depth, :]
        )
        pair = (
            pair
            + padded[:, 4 : 4 + rows, 4 + k : 4 + k + depth, :]
            + padded[:, 4 : 4 + rows, 4 - k : 4 - k + depth, :]
        )
        pair = (
            pair + side_y[:, :, :, 4 + k : 4 + k + width] + side_y[:, :, :, 4 - k : 4 - k + width]
        )
        total = total + COEFFS[k] * pair
    return total


def advance(current, before, padded, speed, damping, source):
    lap = laplace(padded, current.shape[1], current.shape[2])
    return (2.0 * current - (1.0 - damping) * before + speed * lap + source) / (1.0 + damping)


def profile(global_z, start, total):
    ratio = (global_z - start + 1).astype(jnp.float32) / (total - start).astype(jnp.float32)
    return jnp.where(global_z >= start, DAMPING * ratio * ratio, jnp.float32(0.0))


def point_mask(cells, column, anchor, count):
    index = anchor + jnp.arange(count, dtype=jnp.int32)
    return (index[None, :] == cells[:, column][:, None]).astype(jnp.float32)


def lookup_speed(class_map, courant_sq):
    speed = jnp.zeros(class_map.shape, jnp.float32)
    for klass in range(courant_sq.shape[0]):
        speed = speed + jnp.where(class_map == klass, courant_sq[klass], jnp.float32(0.0))
    return speed


def local(
    pressure_now, pressure_before, class_map, courant_sq, source_cells, source_wavelet, layer_start
):
    rows = pressure_now.shape[1]
    depth = pressure_now.shape[2]
    width = pressure_now.shape[3]
    x_anchor = lax.axis_index("gx") * rows
    z_anchor = lax.axis_index("depth") * depth
    total_z = jnp.int32(depth * lax.axis_size("depth"))
    speed = lookup_speed(class_map, courant_sq)
    mask_y = point_mask(source_cells, 2, jnp.int32(0), width)
    current, before = (pressure_now, pressure_before)
    mask_x = point_mask(source_cells, 0, x_anchor, rows)
    depth_index = z_anchor + jnp.arange(depth, dtype=jnp.int32)
    damping = profile(depth_index, layer_start[0], total_z)[None, None, :, None]
    mask_z = point_mask(source_cells, 1, z_anchor, depth)
    onehot = mask_x[:, :, None, None] * mask_z[:, None, :, None] * mask_y[:, None, None, :]
    for step in range(ITERS):
        padded = padded_2(current, (("depth", 2), ("gx", 1)), 4)
        source = source_wavelet[step][:, None, None, None] * onehot
        nxt = advance(current, before, padded, speed, damping, source)
        before, current = (current, nxt)
    return (current, before)


def solution(mesh):
    placed = (
        P(None, "gx", "depth", None),
        P(None, "gx", "depth", None),
        P("gx", "depth", None),
        P(),
        P(),
        P(),
        P(),
    )
    return jax.shard_map(
        local,
        mesh=mesh,
        in_specs=placed,
        out_specs=(P(None, "gx", "depth", None), P(None, "gx", "depth", None)),
        check_vma=False,
    )
```

profile of v0, /device:TPU:217, one launch (start us, length us, event | category | flops | bytes accessed | tf_op | source)
XLA Modules:
  0.0 227.8 jit_solution(8181226835160092627)
XLA Ops:
  0.7 2.1 fusion.281
  2.8 2.6 %collective-permute-start.1 = (f32[4,32,4,128]{3,2,1,0:T(4,128)}, f32[4,32,4,128]{3,2,1,0:T(4,128)S(1)}, u32[]{:S(2)}, u32[]{:S(2)}) collective-permute-start(f32[4,32,4,128]{3,2,1,0:T(4,128)} %get-tuple-element.59), channel_id=1, source_target_pairs={{16,0},{32,16},{48,32},{64,48},{80,64},{96,80},{112,96},{128,112},... | collective-permute-start | bytes 786440 | tf_op jit(solution)/shard_map/ppermute | solution.py:22
  5.4 3.0 %collective-permute-start = (f32[4,32,4,128]{3,2,1,0:T(4,128)S(1)}, f32[4,32,4,128]{3,2,1,0:T(4,128)S(1)}, u32[]{:S(2)}, u32[]{:S(2)}) collective-permute-start(f32[4,32,4,128]{3,2,1,0:T(4,128)S(1)} %get-tuple-element.60), channel_id=1, source_target_pairs={{0,16},{16,32},{32,48},{48,64},{64,80},{80,96},{96,112},{112,128},... | collective-permute-start | bytes 786440 | tf_op jit(solution)/shard_map/ppermute | solution.py:21
  8.4 1.8 fusion.280
  10.2 4.6 %collective-permute-start.2 = (f32[4,4,32,128]{3,2,1,0:T(8,128)}, f32[4,4,32,128]{3,2,1,0:T(8,128)S(1)}, u32[]{:S(2)}, u32[]{:S(2)}) collective-permute-start(f32[4,4,32,128]{3,2,1,0:T(8,128)} %get-tuple-element.57), channel_id=1, source_target_pairs={{1,0},{2,1},{3,2},{4,3},{5,4},{6,5},{7,6},{8,7},{9,8},{10,9},{11,1... | collective-permute-start | bytes 786440 | tf_op jit(solution)/shard_map/ppermute | solution.py:22
  14.8 1.9 collective-permute-start.3
  18.8 6.4 %select_add_fusion = f32[32,32,128]{2,1,0:T(8,128)S(1)} fusion(s32[32,32,128]{2,1,0:T(8,128)} %param.9, f32[]{:T(128)} %bitcast.8, f32[]{:T(128)} %bitcast.7, f32[]{:T(128)} %bitcast.6, f32[]{:T(128)} %bitcast.5, f32[]{:T(128)} %bitcast.4, f32[]{:T(128)} %bitcast.3, f32[]{:T(128)} %bitcast.2, f32[]{:T(128)} %bitcast.1), kind=kLoop, calls=%fused_computation.496 | loop fusion | flops 3014656 | bytes 1048608 | tf_op jit(solution)/shard_map/add | solution.py:73
  25.6 1.6 collective-permute-done.3
  27.2 0.9 select_maximum_fusion.15
  28.1 6.2 %fusion.213 = f32[4,32,32,128]{3,2,1,0:T(8,128)S(1)} fusion(f32[4,32,32,128]{3,2,1,0:T(8,128)S(1)} %copy-done, f32[4,32,4,128]{3,2,1,0:T(4,128)S(1)} %collective-permute-done, f32[4,32,36,128]{3,2,1,0:T(8,128)S(1)} %constant_dynamic-update-slice_fusion, f32[4,36,40,128]{3,2,1,0:T(8,128)S(1)} %get-tuple-element.28, ...), kind=kLoop, calls=%fused_computation.393 | loop fusion | flops 22020096 | bytes 32262416 | tf_op jit(solution)/shard_map/div | solution.py:57
  34.5 2.5 %collective-permute-start.5 = (f32[4,32,4,128]{3,2,1,0:T(4,128)S(1)}, f32[4,32,4,128]{3,2,1,0:T(4,128)S(1)}, u32[]{:S(2)}, u32[]{:S(2)}) collective-permute-start(f32[4,32,4,128]{3,2,1,0:T(4,128)S(1)} %get-tuple-element.55), channel_id=1, source_target_pairs={{16,0},{32,16},{48,32},{64,48},{80,64},{96,80},{112,96},{128,112},... | collective-permute-start | bytes 786440 | tf_op jit(solution)/shard_map/ppermute | solution.py:22
  37.0 3.1 %collective-permute-start.4 = (f32[4,32,4,128]{3,2,1,0:T(4,128)S(1)}, f32[4,32,4,128]{3,2,1,0:T(4,128)S(1)}, u32[]{:S(2)}, u32[]{:S(2)}) collective-permute-start(f32[4,32,4,128]{3,2,1,0:T(4,128)S(1)} %get-tuple-element.56), channel_id=1, source_target_pairs={{0,16},{16,32},{32,48},{48,64},{64,80},{80,96},{96,112},{112,128},... | collective-permute-start | bytes 786440 | tf_op jit(solution)/shard_map/ppermute | solution.py:21
  40.1 4.5 %collective-permute-start.6 = (f32[4,4,32,128]{3,2,1,0:T(8,128)S(1)}, f32[4,4,32,128]{3,2,1,0:T(8,128)S(1)}, u32[]{:S(2)}, u32[]{:S(2)}) collective-permute-start(f32[4,4,32,128]{3,2,1,0:T(8,128)S(1)} %get-tuple-element.53), channel_id=1, source_target_pairs={{1,0},{2,1},{3,2},{4,3},{5,4},{6,5},{7,6},{8,7},{9,8},{10,9},{11,1... | collective-permute-start | bytes 786440 | tf_op jit(solution)/shard_map/ppermute | solution.py:22
  44.5 1.9 collective-permute-start.7
  46.5 4.0 %collective-permute-done.6 = f32[4,4,32,128]{3,2,1,0:T(8,128)S(1)} collective-permute-done((f32[4,4,32,128]{3,2,1,0:T(8,128)S(1)}, f32[4,4,32,128]{3,2,1,0:T(8,128)S(1)}, u32[]{:S(2)}, u32[]{:S(2)}) %collective-permute-start.6) | collective-permute-done | bytes 262176 | tf_op jit(solution)/shard_map/ppermute | solution.py:22
  50.5 6.2 %collective-permute-done.7 = f32[4,4,32,128]{3,2,1,0:T(8,128)S(1)} collective-permute-done((f32[4,4,32,128]{3,2,1,0:T(8,128)S(1)}, f32[4,4,32,128]{3,2,1,0:T(8,128)S(1)}, u32[]{:S(2)}, u32[]{:S(2)}) %collective-permute-start.7) | collective-permute-done | bytes 262176 | tf_op jit(solution)/shard_map/ppermute | solution.py:21
  56.7 0.9 select_maximum_fusion.13
  57.7 6.7 %fusion.184 = f32[4,32,32,128]{3,2,1,0:T(8,128)S(1)} fusion(f32[4,32,32,128]{3,2,1,0:T(8,128)S(1)} %fusion.213, f32[4,32,4,128]{3,2,1,0:T(4,128)S(1)} %collective-permute-done.4, f32[4,32,4,128]{3,2,1,0:T(4,128)S(1)} %collective-permute-done.5, f32[4,36,40,128]{3,2,1,0:T(8,128)S(1)} %get-tuple-element.26, f32[4,36,40,128]{3,2,1,0:T(8,128)S(1)} %get-tuple-element.25, ...), kind=kLoop, calls=%fused_computation.364 | loop fusion | flops 24117248 | bytes 24135952 | tf_op jit(solution)/shard_map/div | solution.py:57
  64.5 2.4 %collective-permute-start.9 = (f32[4,32,4,128]{3,2,1,0:T(4,128)S(1)}, f32[4,32,4,128]{3,2,1,0:T(4,128)S(1)}, u32[]{:S(2)}, u32[]{:S(2)}) collective-permute-start(f32[4,32,4,128]{3,2,1,0:T(4,128)S(1)} %get-tuple-element.51), channel_id=1, source_target_pairs={{16,0},{32,16},{48,32},{64,48},{80,64},{96,80},{112,96},{128,112},... | collective-permute-start | bytes 786440 | tf_op jit(solution)/shard_map/ppermute | solution.py:22
  66.9 3.1 %collective-permute-start.8 = (f32[4,32,4,128]{3,2,1,0:T(4,128)S(1)}, f32[4,32,4,128]{3,2,1,0:T(4,128)S(1)}, u32[]{:S(2)}, u32[]{:S(2)}) collective-permute-start(f32[4,32,4,128]{3,2,1,0:T(4,128)S(1)} %get-tuple-element.52), channel_id=1, source_target_pairs={{0,16},{16,32},{32,48},{48,64},{64,80},{80,96},{96,112},{112,128},... | collective-permute-start | bytes 786440 | tf_op jit(solution)/shard_map/ppermute | solution.py:21
  70.1 1.9 collective-permute-start.10
  72.0 3.4 %collective-permute-start.11 = (f32[4,4,32,128]{3,2,1,0:T(8,128)S(1)}, f32[4,4,32,128]{3,2,1,0:T(8,128)S(1)}, u32[]{:S(2)}, u32[]{:S(2)}) collective-permute-start(f32[4,4,32,128]{3,2,1,0:T(8,128)S(1)} %get-tuple-element.50), channel_id=1, source_target_pairs={{0,1},{1,2},{2,3},{3,4},{4,5},{5,6},{6,7},{7,8},{8,9},{9,10},{10,1... | collective-permute-start | bytes 786440 | tf_op jit(solution)/shard_map/ppermute | solution.py:21
  75.4 4.7 %collective-permute-done.10 = f32[4,4,32,128]{3,2,1,0:T(8,128)S(1)} collective-permute-done((f32[4,4,32,128]{3,2,1,0:T(8,128)S(1)}, f32[4,4,32,128]{3,2,1,0:T(8,128)S(1)}, u32[]{:S(2)}, u32[]{:S(2)}) %collective-permute-start.10) | collective-permute-done | bytes 262176 | tf_op jit(solution)/shard_map/ppermute | solution.py:22
  80.1 3.9 %collective-permute-done.11 = f32[4,4,32,128]{3,2,1,0:T(8,128)S(1)} collective-permute-done((f32[4,4,32,128]{3,2,1,0:T(8,128)S(1)}, f32[4,4,32,128]{3,2,1,0:T(8,128)S(1)}, u32[]{:S(2)}, u32[]{:S(2)}) %collective-permute-start.11) | collective-permute-done | bytes 262176 | tf_op jit(solution)/shard_map/ppermute | solution.py:21
  84.0 0.9 select_maximum_fusion.11
  85.0 6.7 %fusion.155 = f32[4,32,32,128]{3,2,1,0:T(8,128)S(1)} fusion(f32[4,32,32,128]{3,2,1,0:T(8,128)S(1)} %fusion.184, f32[4,32,4,128]{3,2,1,0:T(4,128)S(1)} %collective-permute-done.8, f32[4,32,4,128]{3,2,1,0:T(4,128)S(1)} %collective-permute-done.9, f32[4,36,40,128]{3,2,1,0:T(8,128)S(1)} %get-tuple-element.24, f32[4,36,40,128]{3,2,1,0:T(8,128)S(1)} %get-tuple-element.23, ...), kind=kLoop, calls=%fused_computation.335 | loop fusion | flops 24117248 | bytes 24135952 | tf_op jit(solution)/shard_map/div | solution.py:57
  91.8 2.3 %collective-permute-start.13 = (f32[4,32,4,128]{3,2,1,0:T(4,128)S(1)}, f32[4,32,4,128]{3,2,1,0:T(4,128)S(1)}, u32[]{:S(2)}, u32[]{:S(2)}) collective-permute-start(f32[4,32,4,128]{3,2,1,0:T(4,128)S(1)} %get-tuple-element.47), channel_id=1, source_target_pairs={{16,0},{32,16},{48,32},{64,48},{80,64},{96,80},{112,96},{128,112},... | collective-permute-start | bytes 786440 | tf_op jit(solution)/shard_map/ppermute | solution.py:22
  94.1 3.3 %collective-permute-start.12 = (f32[4,32,4,128]{3,2,1,0:T(4,128)S(1)}, f32[4,32,4,128]{3,2,1,0:T(4,128)S(1)}, u32[]{:S(2)}, u32[]{:S(2)}) collective-permute-start(f32[4,32,4,128]{3,2,1,0:T(4,128)S(1)} %get-tuple-element.48), channel_id=1, source_target_pairs={{0,16},{16,32},{32,48},{48,64},{64,80},{80,96},{96,112},{112,128},... | collective-permute-start | bytes 786440 | tf_op jit(solution)/shard_map/ppermute | solution.py:21
  97.3 1.9 collective-permute-start.14
  99.3 3.4 %collective-permute-start.15 = (f32[4,4,32,128]{3,2,1,0:T(8,128)S(1)}, f32[4,4,32,128]{3,2,1,0:T(8,128)S(1)}, u32[]{:S(2)}, u32[]{:S(2)}) collective-permute-start(f32[4,4,32,128]{3,2,1,0:T(8,128)S(1)} %get-tuple-element.46), channel_id=1, source_target_pairs={{0,1},{1,2},{2,3},{3,4},{4,5},{5,6},{6,7},{7,8},{8,9},{9,10},{10,1... | collective-permute-start | bytes 786440 | tf_op jit(solution)/shard_map/ppermute | solution.py:21
  102.7 4.6 %collective-permute-done.14 = f32[4,4,32,128]{3,2,1,0:T(8,128)S(1)} collective-permute-done((f32[4,4,32,128]{3,2,1,0:T(8,128)S(1)}, f32[4,4,32,128]{3,2,1,0:T(8,128)S(1)}, u32[]{:S(2)}, u32[]{:S(2)}) %collective-permute-start.14) | collective-permute-done | bytes 262176 | tf_op jit(solution)/shard_map/ppermute | solution.py:22
  107.2 3.7 %collective-permute-done.15 = f32[4,4,32,128]{3,2,1,0:T(8,128)S(1)} collective-permute-done((f32[4,4,32,128]{3,2,1,0:T(8,128)S(1)}, f32[4,4,32,128]{3,2,1,0:T(8,128)S(1)}, u32[]{:S(2)}, u32[]{:S(2)}) %collective-permute-start.15) | collective-permute-done | bytes 262176 | tf_op jit(solution)/shard_map/ppermute | solution.py:21
  111.0 0.9 select_maximum_fusion.9
  111.9 6.7 %fusion.126 = f32[4,32,32,128]{3,2,1,0:T(8,128)S(1)} fusion(f32[4,32,32,128]{3,2,1,0:T(8,128)S(1)} %fusion.155, f32[4,32,4,128]{3,2,1,0:T(4,128)S(1)} %collective-permute-done.12, f32[4,32,4,128]{3,2,1,0:T(4,128)S(1)} %collective-permute-done.13, f32[4,36,40,128]{3,2,1,0:T(8,128)S(1)} %get-tuple-element.22, f32[4,36,40,128]{3,2,1,0:T(8,128)S(1)} %get-tuple-element.21, ...), kind=kLoop, calls=%fused_computation.306 | loop fusion | flops 24117248 | bytes 24135952 | tf_op jit(solution)/shard_map/div | solution.py:57
  118.7 2.2 collective-permute-start.17
  121.0 3.3 %collective-permute-start.16 = (f32[4,32,4,128]{3,2,1,0:T(4,128)S(1)}, f32[4,32,4,128]{3,2,1,0:T(4,128)S(1)}, u32[]{:S(2)}, u32[]{:S(2)}) collective-permute-start(f32[4,32,4,128]{3,2,1,0:T(4,128)S(1)} %get-tuple-element.44), channel_id=1, source_target_pairs={{0,16},{16,32},{32,48},{48,64},{64,80},{80,96},{96,112},{112,128},... | collective-permute-start | bytes 786440 | tf_op jit(solution)/shard_map/ppermute | solution.py:21
  124.3 1.9 collective-permute-start.18
  126.2 3.5 %collective-permute-start.19 = (f32[4,4,32,128]{3,2,1,0:T(8,128)S(1)}, f32[4,4,32,128]{3,2,1,0:T(8,128)S(1)}, u32[]{:S(2)}, u32[]{:S(2)}) collective-permute-start(f32[4,4,32,128]{3,2,1,0:T(8,128)S(1)} %get-tuple-element.42), channel_id=1, source_target_pairs={{0,1},{1,2},{2,3},{3,4},{4,5},{5,6},{6,7},{7,8},{8,9},{9,10},{10,1... | collective-permute-start | bytes 786440 | tf_op jit(solution)/shard_map/ppermute | solution.py:21
  129.8 4.3 %collective-permute-done.18 = f32[4,4,32,128]{3,2,1,0:T(8,128)S(1)} collective-permute-done((f32[4,4,32,128]{3,2,1,0:T(8,128)S(1)}, f32[4,4,32,128]{3,2,1,0:T(8,128)S(1)}, u32[]{:S(2)}, u32[]{:S(2)}) %collective-permute-start.18) | collective-permute-done | bytes 262176 | tf_op jit(solution)/shard_map/ppermute | solution.py:22
  134.1 3.7 %collective-permute-done.19 = f32[4,4,32,128]{3,2,1,0:T(8,128)S(1)} collective-permute-done((f32[4,4,32,128]{3,2,1,0:T(8,128)S(1)}, f32[4,4,32,128]{3,2,1,0:T(8,128)S(1)}, u32[]{:S(2)}, u32[]{:S(2)}) %collective-permute-start.19) | collective-permute-done | bytes 262176 | tf_op jit(solution)/shard_map/ppermute | solution.py:21
  138.8 6.7 %fusion.97 = f32[4,32,32,128]{3,2,1,0:T(8,128)S(1)} fusion(f32[4,32,32,128]{3,2,1,0:T(8,128)S(1)} %fusion.126, f32[4,32,4,128]{3,2,1,0:T(4,128)S(1)} %collective-permute-done.16, f32[4,32,4,128]{3,2,1,0:T(4,128)S(1)} %collective-permute-done.17, f32[4,36,40,128]{3,2,1,0:T(8,128)S(1)} %get-tuple-element.20, f32[4,36,40,128]{3,2,1,0:T(8,128)S(1)} %get-tuple-element.19, ...), kind=kLoop, calls=%fused_computation.277 | loop fusion | flops 24117248 | bytes 24135952 | tf_op jit(solution)/shard_map/div | solution.py:57
  145.6 2.2 collective-permute-start.21
  147.8 3.3 %collective-permute-start.20 = (f32[4,32,4,128]{3,2,1,0:T(4,128)S(1)}, f32[4,32,4,128]{3,2,1,0:T(4,128)S(1)}, u32[]{:S(2)}, u32[]{:S(2)}) collective-permute-start(f32[4,32,4,128]{3,2,1,0:T(4,128)S(1)} %get-tuple-element.40), channel_id=1, source_target_pairs={{0,16},{16,32},{32,48},{48,64},{64,80},{80,96},{96,112},{112,128},... | collective-permute-start | bytes 786440 | tf_op jit(solution)/shard_map/ppermute | solution.py:21
  151.2 1.9 collective-permute-start.22
  153.1 3.4 %collective-permute-start.23 = (f32[4,4,32,128]{3,2,1,0:T(8,128)S(1)}, f32[4,4,32,128]{3,2,1,0:T(8,128)S(1)}, u32[]{:S(2)}, u32[]{:S(2)}) collective-permute-start(f32[4,4,32,128]{3,2,1,0:T(8,128)S(1)} %get-tuple-element.38), channel_id=1, source_target_pairs={{0,1},{1,2},{2,3},{3,4},{4,5},{5,6},{6,7},{7,8},{8,9},{9,10},{10,1... | collective-permute-start | bytes 786440 | tf_op jit(solution)/shard_map/ppermute | solution.py:21
  156.5 4.6 %collective-permute-done.22 = f32[4,4,32,128]{3,2,1,0:T(8,128)S(1)} collective-permute-done((f32[4,4,32,128]{3,2,1,0:T(8,128)S(1)}, f32[4,4,32,128]{3,2,1,0:T(8,128)S(1)}, u32[]{:S(2)}, u32[]{:S(2)}) %collective-permute-start.22) | collective-permute-done | bytes 262176 | tf_op jit(solution)/shard_map/ppermute | solution.py:22
  161.1 3.7 %collective-permute-done.23 = f32[4,4,32,128]{3,2,1,0:T(8,128)S(1)} collective-permute-done((f32[4,4,32,128]{3,2,1,0:T(8,128)S(1)}, f32[4,4,32,128]{3,2,1,0:T(8,128)S(1)}, u32[]{:S(2)}, u32[]{:S(2)}) %collective-permute-start.23) | collective-permute-done | bytes 262176 | tf_op jit(solution)/shard_map/ppermute | solution.py:21
  164.8 0.9 select_maximum_fusion.5
  165.8 6.7 %fusion.68 = f32[4,32,32,128]{3,2,1,0:T(8,128)S(1)} fusion(f32[4,32,32,128]{3,2,1,0:T(8,128)S(1)} %fusion.97, f32[4,32,4,128]{3,2,1,0:T(4,128)S(1)} %collective-permute-done.20, f32[4,32,4,128]{3,2,1,0:T(4,128)S(1)} %collective-permute-done.21, f32[4,36,40,128]{3,2,1,0:T(8,128)S(1)} %get-tuple-element.18, f32[4,36,40,128]{3,2,1,0:T(8,128)S(1)} %get-tuple-element.17, ...), kind=kLoop, calls=%fused_computation.248 | loop fusion | flops 24117248 | bytes 24135952 | tf_op jit(solution)/shard_map/div | solution.py:57
  172.6 2.3 %collective-permute-start.25 = (f32[4,32,4,128]{3,2,1,0:T(4,128)S(1)}, f32[4,32,4,128]{3,2,1,0:T(4,128)S(1)}, u32[]{:S(2)}, u32[]{:S(2)}) collective-permute-start(f32[4,32,4,128]{3,2,1,0:T(4,128)S(1)} %get-tuple-element.35), channel_id=1, source_target_pairs={{16,0},{32,16},{48,32},{64,48},{80,64},{96,80},{112,96},{128,112},... | collective-permute-start | bytes 786440 | tf_op jit(solution)/shard_map/ppermute | solution.py:22
  174.9 3.3 %collective-permute-start.24 = (f32[4,32,4,128]{3,2,1,0:T(4,128)S(1)}, f32[4,32,4,128]{3,2,1,0:T(4,128)S(1)}, u32[]{:S(2)}, u32[]{:S(2)}) collective-permute-start(f32[4,32,4,128]{3,2,1,0:T(4,128)S(1)} %get-tuple-element.36), channel_id=1, source_target_pairs={{0,16},{16,32},{32,48},{48,64},{64,80},{80,96},{96,112},{112,128},... | collective-permute-start | bytes 786440 | tf_op jit(solution)/shard_map/ppermute | solution.py:21
  178.2 1.9 collective-permute-start.26
  180.1 3.4 %collective-permute-start.27 = (f32[4,4,32,128]{3,2,1,0:T(8,128)S(1)}, f32[4,4,32,128]{3,2,1,0:T(8,128)S(1)}, u32[]{:S(2)}, u32[]{:S(2)}) collective-permute-start(f32[4,4,32,128]{3,2,1,0:T(8,128)S(1)} %get-tuple-element.34), channel_id=1, source_target_pairs={{0,1},{1,2},{2,3},{3,4},{4,5},{5,6},{6,7},{7,8},{8,9},{9,10},{10,1... | collective-permute-start | bytes 786440 | tf_op jit(solution)/shard_map/ppermute | solution.py:21
  183.5 4.8 %collective-permute-done.26 = f32[4,4,32,128]{3,2,1,0:T(8,128)S(1)} collective-permute-done((f32[4,4,32,128]{3,2,1,0:T(8,128)S(1)}, f32[4,4,32,128]{3,2,1,0:T(8,128)S(1)}, u32[]{:S(2)}, u32[]{:S(2)}) %collective-permute-start.26) | collective-permute-done | bytes 262176 | tf_op jit(solution)/shard_map/ppermute | solution.py:22
  188.3 4.0 %collective-permute-done.27 = f32[4,4,32,128]{3,2,1,0:T(8,128)S(1)} collective-permute-done((f32[4,4,32,128]{3,2,1,0:T(8,128)S(1)}, f32[4,4,32,128]{3,2,1,0:T(8,128)S(1)}, u32[]{:S(2)}, u32[]{:S(2)}) %collective-permute-start.27) | collective-permute-done | bytes 262176 | tf_op jit(solution)/shard_map/ppermute | solution.py:21
  193.2 6.7 %fusion.39 = f32[4,32,32,128]{3,2,1,0:T(8,128)S(1)} fusion(f32[4,32,32,128]{3,2,1,0:T(8,128)S(1)} %fusion.68, f32[4,32,4,128]{3,2,1,0:T(4,128)S(1)} %collective-permute-done.24, f32[4,32,4,128]{3,2,1,0:T(4,128)S(1)} %collective-permute-done.25, f32[4,36,40,128]{3,2,1,0:T(8,128)S(1)} %get-tuple-element.16, f32[4,36,40,128]{3,2,1,0:T(8,128)S(1)} %get-tuple-element.15, ...), kind=kLoop, calls=%fused_computation.219 | loop fusion | flops 24117248 | bytes 24135952 | tf_op jit(solution)/shard_map/div | solution.py:57
  200.1 2.4 %collective-permute-start.29 = (f32[4,32,4,128]{3,2,1,0:T(4,128)S(1)}, f32[4,32,4,128]{3,2,1,0:T(4,128)S(1)}, u32[]{:S(2)}, u32[]{:S(2)}) collective-permute-start(f32[4,32,4,128]{3,2,1,0:T(4,128)S(1)} %get-tuple-element.31), channel_id=1, source_target_pairs={{16,0},{32,16},{48,32},{64,48},{80,64},{96,80},{112,96},{128,112},... | collective-permute-start | bytes 786440 | tf_op jit(solution)/shard_map/ppermute | solution.py:22
  202.5 3.2 %collective-permute-start.28 = (f32[4,32,4,128]{3,2,1,0:T(4,128)S(1)}, f32[4,32,4,128]{3,2,1,0:T(4,128)S(1)}, u32[]{:S(2)}, u32[]{:S(2)}) collective-permute-start(f32[4,32,4,128]{3,2,1,0:T(4,128)S(1)} %get-tuple-element.32), channel_id=1, source_target_pairs={{0,16},{16,32},{32,48},{48,64},{64,80},{80,96},{96,112},{112,128},... | collective-permute-start | bytes 786440 | tf_op jit(solution)/shard_map/ppermute | solution.py:21
  205.6 1.9 collective-permute-start.30
  207.6 3.4 %collective-permute-start.31 = (f32[4,4,32,128]{3,2,1,0:T(8,128)S(1)}, f32[4,4,32,128]{3,2,1,0:T(8,128)S(1)}, u32[]{:S(2)}, u32[]{:S(2)}) collective-permute-start(f32[4,4,32,128]{3,2,1,0:T(8,128)S(1)} %get-tuple-element.30), channel_id=1, source_target_pairs={{0,1},{1,2},{2,3},{3,4},{4,5},{5,6},{6,7},{7,8},{8,9},{9,10},{10,1... | collective-permute-start | bytes 786440 | tf_op jit(solution)/shard_map/ppermute | solution.py:21
  211.0 4.6 %collective-permute-done.30 = f32[4,4,32,128]{3,2,1,0:T(8,128)S(1)} collective-permute-done((f32[4,4,32,128]{3,2,1,0:T(8,128)S(1)}, f32[4,4,32,128]{3,2,1,0:T(8,128)S(1)}, u32[]{:S(2)}, u32[]{:S(2)}) %collective-permute-start.30) | collective-permute-done | bytes 262176 | tf_op jit(solution)/shard_map/ppermute | solution.py:22
  215.6 3.8 %collective-permute-done.31 = f32[4,4,32,128]{3,2,1,0:T(8,128)S(1)} collective-permute-done((f32[4,4,32,128]{3,2,1,0:T(8,128)S(1)}, f32[4,4,32,128]{3,2,1,0:T(8,128)S(1)}, u32[]{:S(2)}, u32[]{:S(2)}) %collective-permute-start.31) | collective-permute-done | bytes 262176 | tf_op jit(solution)/shard_map/ppermute | solution.py:21
  219.3 0.9 select_maximum_fusion.1
  220.3 7.5 %fusion.10 = f32[4,32,32,128]{3,2,1,0:T(8,128)} fusion(f32[4,32,32,128]{3,2,1,0:T(8,128)S(1)} %fusion.39, f32[4,32,4,128]{3,2,1,0:T(4,128)S(1)} %collective-permute-done.28, f32[4,32,4,128]{3,2,1,0:T(4,128)S(1)} %collective-permute-done.29, f32[4,36,40,128]{3,2,1,0:T(8,128)S(1)} %get-tuple-element.14, f32[4,36,40,128]{3,2,1,0:T(8,128)S(1)} %get-tuple-element.13, ...), kind=kLoop, calls=%fused_computation.190 | loop fusion | flops 24117248 | bytes 24135952 | tf_op jit(solution)/shard_map/div | solution.py:57
  (56 shorter events, 4.5 us)
Async XLA Ops:
  0.6 24.6 %copy-start = (f32[4,32,32,128]{3,2,1,0:T(8,128)S(1)}, f32[4,32,32,128]{3,2,1,0:T(8,128)}, u32[]{:S(2)}) copy-start(f32[4,32,32,128]{3,2,1,0:T(8,128)} %param.7) | copy-start | bytes 6291460
  0.6 16.8 %copy-start.5 = (s32[4,3]{1,0:T(4,128)S(1)}, s32[4,3]{1,0:T(4,128)}, u32[]{:S(2)}) copy-start(s32[4,3]{1,0:T(4,128)} %param.11) | copy-start | bytes 148
  0.7 17.0 %copy-start.4 = (f32[8]{0:T(128)S(1)}, f32[8]{0:T(128)}, u32[]{:S(2)}) copy-start(f32[8]{0:T(128)} %param.10) | copy-start | bytes 100
  0.7 17.7 %copy-start.3 = (f32[8,4]{0,1:T(4,128)S(1)}, f32[8,4]{0,1:T(4,128)}, u32[]{:S(2)}) copy-start(f32[8,4]{0,1:T(4,128)} %param.12) | copy-start | bytes 388
  2.8 22.6 %collective-permute-start.1 = (f32[4,32,4,128]{3,2,1,0:T(4,128)}, f32[4,32,4,128]{3,2,1,0:T(4,128)S(1)}, u32[]{:S(2)}, u32[]{:S(2)}) collective-permute-start(f32[4,32,4,128]{3,2,1,0:T(4,128)} %get-tuple-element.59), channel_id=1, source_target_pairs={{16,0},{32,16},{48,32},{64,48},{80,64},{96,80},{112,96},{128,112},... | collective-permute-start | bytes 786440 | tf_op jit(solution)/shard_map/ppermute | solution.py:22
  5.4 20.2 %collective-permute-start = (f32[4,32,4,128]{3,2,1,0:T(4,128)S(1)}, f32[4,32,4,128]{3,2,1,0:T(4,128)S(1)}, u32[]{:S(2)}, u32[]{:S(2)}) collective-permute-start(f32[4,32,4,128]{3,2,1,0:T(4,128)S(1)} %get-tuple-element.60), channel_id=1, source_target_pairs={{0,16},{16,32},{32,48},{48,64},{64,80},{80,96},{96,112},{112,128},... | collective-permute-start | bytes 786440 | tf_op jit(solution)/shard_map/ppermute | solution.py:21
  10.2 15.3 %collective-permute-start.2 = (f32[4,4,32,128]{3,2,1,0:T(8,128)}, f32[4,4,32,128]{3,2,1,0:T(8,128)S(1)}, u32[]{:S(2)}, u32[]{:S(2)}) collective-permute-start(f32[4,4,32,128]{3,2,1,0:T(8,128)} %get-tuple-element.57), channel_id=1, source_target_pairs={{1,0},{2,1},{3,2},{4,3},{5,4},{6,5},{7,6},{8,7},{9,8},{10,9},{11,1... | collective-permute-start | bytes 786440 | tf_op jit(solution)/shard_map/ppermute | solution.py:22
  14.8 12.4 %collective-permute-start.3 = (f32[4,4,32,128]{3,2,1,0:T(8,128)}, f32[4,4,32,128]{3,2,1,0:T(8,128)S(1)}, u32[]{:S(2)}, u32[]{:S(2)}) collective-permute-start(f32[4,4,32,128]{3,2,1,0:T(8,128)} %get-tuple-element.58), channel_id=1, source_target_pairs={{0,1},{1,2},{2,3},{3,4},{4,5},{5,6},{6,7},{7,8},{8,9},{9,10},{10,1... | collective-permute-start | bytes 786440 | tf_op jit(solution)/shard_map/ppermute | solution.py:21
  25.5 2.5 %copy-start.2 = (f32[4,32,32,128]{3,2,1,0:T(8,128)S(1)}, f32[4,32,32,128]{3,2,1,0:T(8,128)}, u32[]{:S(2)}) copy-start(f32[4,32,32,128]{3,2,1,0:T(8,128)} %param.8) | copy-start | bytes 6291460
  34.5 12.0 %collective-permute-start.5 = (f32[4,32,4,128]{3,2,1,0:T(4,128)S(1)}, f32[4,32,4,128]{3,2,1,0:T(4,128)S(1)}, u32[]{:S(2)}, u32[]{:S(2)}) collective-permute-start(f32[4,32,4,128]{3,2,1,0:T(4,128)S(1)} %get-tuple-element.55), channel_id=1, source_target_pairs={{16,0},{32,16},{48,32},{64,48},{80,64},{96,80},{112,96},{128,112},... | collective-permute-start | bytes 786440 | tf_op jit(solution)/shard_map/ppermute | solution.py:22
  37.0 9.5 %collective-permute-start.4 = (f32[4,32,4,128]{3,2,1,0:T(4,128)S(1)}, f32[4,32,4,128]{3,2,1,0:T(4,128)S(1)}, u32[]{:S(2)}, u32[]{:S(2)}) collective-permute-start(f32[4,32,4,128]{3,2,1,0:T(4,128)S(1)} %get-tuple-element.56), channel_id=1, source_target_pairs={{0,16},{16,32},{32,48},{48,64},{64,80},{80,96},{96,112},{112,128},... | collective-permute-start | bytes 786440 | tf_op jit(solution)/shard_map/ppermute | solution.py:21
  40.1 10.5 %collective-permute-start.6 = (f32[4,4,32,128]{3,2,1,0:T(8,128)S(1)}, f32[4,4,32,128]{3,2,1,0:T(8,128)S(1)}, u32[]{:S(2)}, u32[]{:S(2)}) collective-permute-start(f32[4,4,32,128]{3,2,1,0:T(8,128)S(1)} %get-tuple-element.53), channel_id=1, source_target_pairs={{1,0},{2,1},{3,2},{4,3},{5,4},{6,5},{7,6},{8,7},{9,8},{10,9},{11,1... | collective-permute-start | bytes 786440 | tf_op jit(solution)/shard_map/ppermute | solution.py:22
  44.5 12.2 %collective-permute-start.7 = (f32[4,4,32,128]{3,2,1,0:T(8,128)S(1)}, f32[4,4,32,128]{3,2,1,0:T(8,128)S(1)}, u32[]{:S(2)}, u32[]{:S(2)}) collective-permute-start(f32[4,4,32,128]{3,2,1,0:T(8,128)S(1)} %get-tuple-element.54), channel_id=1, source_target_pairs={{0,1},{1,2},{2,3},{3,4},{4,5},{5,6},{6,7},{7,8},{8,9},{9,10},{10,1... | collective-permute-start | bytes 786440 | tf_op jit(solution)/shard_map/ppermute | solution.py:21
  64.5 10.9 %collective-permute-start.9 = (f32[4,32,4,128]{3,2,1,0:T(4,128)S(1)}, f32[4,32,4,128]{3,2,1,0:T(4,128)S(1)}, u32[]{:S(2)}, u32[]{:S(2)}) collective-permute-start(f32[4,32,4,128]{3,2,1,0:T(4,128)S(1)} %get-tuple-element.51), channel_id=1, source_target_pairs={{16,0},{32,16},{48,32},{64,48},{80,64},{96,80},{112,96},{128,112},... | collective-permute-start | bytes 786440 | tf_op jit(solution)/shard_map/ppermute | solution.py:22
  66.9 8.4 %collective-permute-start.8 = (f32[4,32,4,128]{3,2,1,0:T(4,128)S(1)}, f32[4,32,4,128]{3,2,1,0:T(4,128)S(1)}, u32[]{:S(2)}, u32[]{:S(2)}) collective-permute-start(f32[4,32,4,128]{3,2,1,0:T(4,128)S(1)} %get-tuple-element.52), channel_id=1, source_target_pairs={{0,16},{16,32},{32,48},{48,64},{64,80},{80,96},{96,112},{112,128},... | collective-permute-start | bytes 786440 | tf_op jit(solution)/shard_map/ppermute | solution.py:21
  70.1 10.1 %collective-permute-start.10 = (f32[4,4,32,128]{3,2,1,0:T(8,128)S(1)}, f32[4,4,32,128]{3,2,1,0:T(8,128)S(1)}, u32[]{:S(2)}, u32[]{:S(2)}) collective-permute-start(f32[4,4,32,128]{3,2,1,0:T(8,128)S(1)} %get-tuple-element.49), channel_id=1, source_target_pairs={{1,0},{2,1},{3,2},{4,3},{5,4},{6,5},{7,6},{8,7},{9,8},{10,9},{11,1... | collective-permute-start | bytes 786440 | tf_op jit(solution)/shard_map/ppermute | solution.py:22
  72.0 12.0 %collective-permute-start.11 = (f32[4,4,32,128]{3,2,1,0:T(8,128)S(1)}, f32[4,4,32,128]{3,2,1,0:T(8,128)S(1)}, u32[]{:S(2)}, u32[]{:S(2)}) collective-permute-start(f32[4,4,32,128]{3,2,1,0:T(8,128)S(1)} %get-tuple-element.50), channel_id=1, source_target_pairs={{0,1},{1,2},{2,3},{3,4},{4,5},{5,6},{6,7},{7,8},{8,9},{9,10},{10,1... | collective-permute-start | bytes 786440 | tf_op jit(solution)/shard_map/ppermute | solution.py:21
  91.8 10.9 %collective-permute-start.13 = (f32[4,32,4,128]{3,2,1,0:T(4,128)S(1)}, f32[4,32,4,128]{3,2,1,0:T(4,128)S(1)}, u32[]{:S(2)}, u32[]{:S(2)}) collective-permute-start(f32[4,32,4,128]{3,2,1,0:T(4,128)S(1)} %get-tuple-element.47), channel_id=1, source_target_pairs={{16,0},{32,16},{48,32},{64,48},{80,64},{96,80},{112,96},{128,112},... | collective-permute-start | bytes 786440 | tf_op jit(solution)/shard_map/ppermute | solution.py:22
  94.1 8.6 %collective-permute-start.12 = (f32[4,32,4,128]{3,2,1,0:T(4,128)S(1)}, f32[4,32,4,128]{3,2,1,0:T(4,128)S(1)}, u32[]{:S(2)}, u32[]{:S(2)}) collective-permute-start(f32[4,32,4,128]{3,2,1,0:T(4,128)S(1)} %get-tuple-element.48), channel_id=1, source_target_pairs={{0,16},{16,32},{32,48},{48,64},{64,80},{80,96},{96,112},{112,128},... | collective-permute-start | bytes 786440 | tf_op jit(solution)/shard_map/ppermute | solution.py:21
  97.3 9.9 %collective-permute-start.14 = (f32[4,4,32,128]{3,2,1,0:T(8,128)S(1)}, f32[4,4,32,128]{3,2,1,0:T(8,128)S(1)}, u32[]{:S(2)}, u32[]{:S(2)}) collective-permute-start(f32[4,4,32,128]{3,2,1,0:T(8,128)S(1)} %get-tuple-element.45), channel_id=1, source_target_pairs={{1,0},{2,1},{3,2},{4,3},{5,4},{6,5},{7,6},{8,7},{9,8},{10,9},{11,1... | collective-permute-start | bytes 786440 | tf_op jit(solution)/shard_map/ppermute | solution.py:22
  99.3 11.7 %collective-permute-start.15 = (f32[4,4,32,128]{3,2,1,0:T(8,128)S(1)}, f32[4,4,32,128]{3,2,1,0:T(8,128)S(1)}, u32[]{:S(2)}, u32[]{:S(2)}) collective-permute-start(f32[4,4,32,128]{3,2,1,0:T(8,128)S(1)} %get-tuple-element.46), channel_id=1, source_target_pairs={{0,1},{1,2},{2,3},{3,4},{4,5},{5,6},{6,7},{7,8},{8,9},{9,10},{10,1... | collective-permute-start | bytes 786440 | tf_op jit(solution)/shard_map/ppermute | solution.py:21
  118.7 11.1 %collective-permute-start.17 = (f32[4,32,4,128]{3,2,1,0:T(4,128)S(1)}, f32[4,32,4,128]{3,2,1,0:T(4,128)S(1)}, u32[]{:S(2)}, u32[]{:S(2)}) collective-permute-start(f32[4,32,4,128]{3,2,1,0:T(4,128)S(1)} %get-tuple-element.43), channel_id=1, source_target_pairs={{16,0},{32,16},{48,32},{64,48},{80,64},{96,80},{112,96},{128,112},... | collective-permute-start | bytes 786440 | tf_op jit(solution)/shard_map/ppermute | solution.py:22
  121.0 8.8 %collective-permute-start.16 = (f32[4,32,4,128]{3,2,1,0:T(4,128)S(1)}, f32[4,32,4,128]{3,2,1,0:T(4,128)S(1)}, u32[]{:S(2)}, u32[]{:S(2)}) collective-permute-start(f32[4,32,4,128]{3,2,1,0:T(4,128)S(1)} %get-tuple-element.44), channel_id=1, source_target_pairs={{0,16},{16,32},{32,48},{48,64},{64,80},{80,96},{96,112},{112,128},... | collective-permute-start | bytes 786440 | tf_op jit(solution)/shard_map/ppermute | solution.py:21
  124.3 9.8 %collective-permute-start.18 = (f32[4,4,32,128]{3,2,1,0:T(8,128)S(1)}, f32[4,4,32,128]{3,2,1,0:T(8,128)S(1)}, u32[]{:S(2)}, u32[]{:S(2)}) collective-permute-start(f32[4,4,32,128]{3,2,1,0:T(8,128)S(1)} %get-tuple-element.41), channel_id=1, source_target_pairs={{1,0},{2,1},{3,2},{4,3},{5,4},{6,5},{7,6},{8,7},{9,8},{10,9},{11,1... | collective-permute-start | bytes 786440 | tf_op jit(solution)/shard_map/ppermute | solution.py:22
  126.2 11.7 %collective-permute-start.19 = (f32[4,4,32,128]{3,2,1,0:T(8,128)S(1)}, f32[4,4,32,128]{3,2,1,0:T(8,128)S(1)}, u32[]{:S(2)}, u32[]{:S(2)}) collective-permute-start(f32[4,4,32,128]{3,2,1,0:T(8,128)S(1)} %get-tuple-element.42), channel_id=1, source_target_pairs={{0,1},{1,2},{2,3},{3,4},{4,5},{5,6},{6,7},{7,8},{8,9},{9,10},{10,1... | collective-permute-start | bytes 786440 | tf_op jit(solution)/shard_map/ppermute | solution.py:21
  145.6 10.9 %collective-permute-start.21 = (f32[4,32,4,128]{3,2,1,0:T(4,128)S(1)}, f32[4,32,4,128]{3,2,1,0:T(4,128)S(1)}, u32[]{:S(2)}, u32[]{:S(2)}) collective-permute-start(f32[4,32,4,128]{3,2,1,0:T(4,128)S(1)} %get-tuple-element.39), channel_id=1, source_target_pairs={{16,0},{32,16},{48,32},{64,48},{80,64},{96,80},{112,96},{128,112},... | collective-permute-start | bytes 786440 | tf_op jit(solution)/shard_map/ppermute | solution.py:22
  147.8 8.7 %collective-permute-start.20 = (f32[4,32,4,128]{3,2,1,0:T(4,128)S(1)}, f32[4,32,4,128]{3,2,1,0:T(4,128)S(1)}, u32[]{:S(2)}, u32[]{:S(2)}) collective-permute-start(f32[4,32,4,128]{3,2,1,0:T(4,128)S(1)} %get-tuple-element.40), channel_id=1, source_target_pairs={{0,16},{16,32},{32,48},{48,64},{64,80},{80,96},{96,112},{112,128},... | collective-permute-start | bytes 786440 | tf_op jit(solution)/shard_map/ppermute | solution.py:21
  151.2 9.9 %collective-permute-start.22 = (f32[4,4,32,128]{3,2,1,0:T(8,128)S(1)}, f32[4,4,32,128]{3,2,1,0:T(8,128)S(1)}, u32[]{:S(2)}, u32[]{:S(2)}) collective-permute-start(f32[4,4,32,128]{3,2,1,0:T(8,128)S(1)} %get-tuple-element.37), channel_id=1, source_target_pairs={{1,0},{2,1},{3,2},{4,3},{5,4},{6,5},{7,6},{8,7},{9,8},{10,9},{11,1... | collective-permute-start | bytes 786440 | tf_op jit(solution)/shard_map/ppermute | solution.py:22
  153.1 11.7 %collective-permute-start.23 = (f32[4,4,32,128]{3,2,1,0:T(8,128)S(1)}, f32[4,4,32,128]{3,2,1,0:T(8,128)S(1)}, u32[]{:S(2)}, u32[]{:S(2)}) collective-permute-start(f32[4,4,32,128]{3,2,1,0:T(8,128)S(1)} %get-tuple-element.38), channel_id=1, source_target_pairs={{0,1},{1,2},{2,3},{3,4},{4,5},{5,6},{6,7},{7,8},{8,9},{9,10},{10,1... | collective-permute-start | bytes 786440 | tf_op jit(solution)/shard_map/ppermute | solution.py:21
  172.6 10.9 %collective-permute-start.25 = (f32[4,32,4,128]{3,2,1,0:T(4,128)S(1)}, f32[4,32,4,128]{3,2,1,0:T(4,128)S(1)}, u32[]{:S(2)}, u32[]{:S(2)}) collective-permute-start(f32[4,32,4,128]{3,2,1,0:T(4,128)S(1)} %get-tuple-element.35), channel_id=1, source_target_pairs={{16,0},{32,16},{48,32},{64,48},{80,64},{96,80},{112,96},{128,112},... | collective-permute-start | bytes 786440 | tf_op jit(solution)/shard_map/ppermute | solution.py:22
  174.9 8.6 %collective-permute-start.24 = (f32[4,32,4,128]{3,2,1,0:T(4,128)S(1)}, f32[4,32,4,128]{3,2,1,0:T(4,128)S(1)}, u32[]{:S(2)}, u32[]{:S(2)}) collective-permute-start(f32[4,32,4,128]{3,2,1,0:T(4,128)S(1)} %get-tuple-element.36), channel_id=1, source_target_pairs={{0,16},{16,32},{32,48},{48,64},{64,80},{80,96},{96,112},{112,128},... | collective-permute-start | bytes 786440 | tf_op jit(solution)/shard_map/ppermute | solution.py:21
  178.2 10.1 %collective-permute-start.26 = (f32[4,4,32,128]{3,2,1,0:T(8,128)S(1)}, f32[4,4,32,128]{3,2,1,0:T(8,128)S(1)}, u32[]{:S(2)}, u32[]{:S(2)}) collective-permute-start(f32[4,4,32,128]{3,2,1,0:T(8,128)S(1)} %get-tuple-element.33), channel_id=1, source_target_pairs={{1,0},{2,1},{3,2},{4,3},{5,4},{6,5},{7,6},{8,7},{9,8},{10,9},{11,1... | collective-permute-start | bytes 786440 | tf_op jit(solution)/shard_map/ppermute | solution.py:22
  180.1 12.2 %collective-permute-start.27 = (f32[4,4,32,128]{3,2,1,0:T(8,128)S(1)}, f32[4,4,32,128]{3,2,1,0:T(8,128)S(1)}, u32[]{:S(2)}, u32[]{:S(2)}) collective-permute-start(f32[4,4,32,128]{3,2,1,0:T(8,128)S(1)} %get-tuple-element.34), channel_id=1, source_target_pairs={{0,1},{1,2},{2,3},{3,4},{4,5},{5,6},{6,7},{7,8},{8,9},{9,10},{10,1... | collective-permute-start | bytes 786440 | tf_op jit(solution)/shard_map/ppermute | solution.py:21
  199.9 20.4 %copy-start.1 = (f32[4,32,32,128]{3,2,1,0:T(8,128)}, f32[4,32,32,128]{3,2,1,0:T(8,128)S(1)}, u32[]{:S(2)}) copy-start(f32[4,32,32,128]{3,2,1,0:T(8,128)S(1)} %fusion.39) | copy-start | bytes 6291460
  200.1 10.9 %collective-permute-start.29 = (f32[4,32,4,128]{3,2,1,0:T(4,128)S(1)}, f32[4,32,4,128]{3,2,1,0:T(4,128)S(1)}, u32[]{:S(2)}, u32[]{:S(2)}) collective-permute-start(f32[4,32,4,128]{3,2,1,0:T(4,128)S(1)} %get-tuple-element.31), channel_id=1, source_target_pairs={{16,0},{32,16},{48,32},{64,48},{80,64},{96,80},{112,96},{128,112},... | collective-permute-start | bytes 786440 | tf_op jit(solution)/shard_map/ppermute | solution.py:22
  202.5 8.5 %collective-permute-start.28 = (f32[4,32,4,128]{3,2,1,0:T(4,128)S(1)}, f32[4,32,4,128]{3,2,1,0:T(4,128)S(1)}, u32[]{:S(2)}, u32[]{:S(2)}) collective-permute-start(f32[4,32,4,128]{3,2,1,0:T(4,128)S(1)} %get-tuple-element.32), channel_id=1, source_target_pairs={{0,16},{16,32},{32,48},{48,64},{64,80},{80,96},{96,112},{112,128},... | collective-permute-start | bytes 786440 | tf_op jit(solution)/shard_map/ppermute | solution.py:21
  205.6 9.9 %collective-permute-start.30 = (f32[4,4,32,128]{3,2,1,0:T(8,128)S(1)}, f32[4,4,32,128]{3,2,1,0:T(8,128)S(1)}, u32[]{:S(2)}, u32[]{:S(2)}) collective-permute-start(f32[4,4,32,128]{3,2,1,0:T(8,128)S(1)} %get-tuple-element.29), channel_id=1, source_target_pairs={{1,0},{2,1},{3,2},{4,3},{5,4},{6,5},{7,6},{8,7},{9,8},{10,9},{11,1... | collective-permute-start | bytes 786440 | tf_op jit(solution)/shard_map/ppermute | solution.py:22
  207.6 11.8 %collective-permute-start.31 = (f32[4,4,32,128]{3,2,1,0:T(8,128)S(1)}, f32[4,4,32,128]{3,2,1,0:T(8,128)S(1)}, u32[]{:S(2)}, u32[]{:S(2)}) collective-permute-start(f32[4,4,32,128]{3,2,1,0:T(8,128)S(1)} %get-tuple-element.30), channel_id=1, source_target_pairs={{0,1},{1,2},{2,3},{3,4},{4,5},{5,6},{6,7},{7,8},{8,9},{9,10},{10,1... | collective-permute-start | bytes 786440 | tf_op jit(solution)/shard_map/ppermute | solution.py:21
where the time goes:
time: 229 us; the launch traced here: 228 us
  starting transfers between devices  89.2 us (39%)
  other arithmetic  67.7 us (30%)
  waiting for transfers between devices  62.4 us (27%)
  local copies, waits for them, and re-layouts  6.31 us (3%)
    div x8, other arithmetic, advance(): (2.0 * current - (1.0 - damping) * before + speed * lap + source) / (1.0...  53.6 us
    ppermute x16, starting transfers between devices, padded_2(): lax.ppermute(last, axis, up)  49.7 us
    ppermute x16, starting transfers between devices, padded_2(): lax.ppermute(leading, axis, [(b, a) for a, b in up])  39.5 us
    ppermute x16, waiting for transfers between devices, padded_2(): lax.ppermute(leading, axis, [(b, a) for a, b in up])  31.7 us
    ppermute x16, waiting for transfers between devices, padded_2(): lax.ppermute(last, axis, up)  30.7 us
    concatenate x8, other arithmetic, padded_2(): jnp.concatenate([jnp.pad(low, around), shard, jnp.pad(high, around)], axi...  7.41 us
    add x1, other arithmetic, lookup_speed(): speed + jnp.where(class_map == klass, courant_sq[klass], jnp.float32(0.0))  6.45 us
    slice x16, local copies, waits for them, and re-layouts, padded_2(): leading = lax.slice_in_dim(shard, 0, width, axis=dim)  4.9 us
  transfers between devices with their start and end apart: 32, of which 15 were waited for; matrix products, arithmetic and copies ran while one was open for 4% of the time, Pallas kernels for 0%

commit v1 on v0

--- a/solution.py
+++ b/solution.py
@@ -14,12 +14,15 @@
     edges = {}
     for axis, dim in sides:
         peers, length = (lax.axis_size(axis), shard.shape[dim])
-        up = [(i, (i + 1) % peers) for i in range(peers - 1)]
+        up = [(i, (i + 1) % peers) for i in range(peers)]
         last = lax.slice_in_dim(shard, length - width, length, axis=dim)
         leading = lax.slice_in_dim(shard, 0, width, axis=dim)
+        place = lax.axis_index(axis)
+        low = lax.ppermute(last, axis, up)
+        high = lax.ppermute(leading, axis, [(b, a) for a, b in up])
         edges[dim] = (
-            lax.ppermute(last, axis, up),
-            lax.ppermute(leading, axis, [(b, a) for a, b in up]),
+            jnp.where(place > 0, low, 0.0),
+            jnp.where(place < peers - 1, high, 0.0),
         )
     done = []
     for _, dim in sides:
@@ -92,7 +95,7 @@
     mask_z = point_mask(source_cells, 1, z_anchor, depth)
     onehot = mask_x[:, :, None, None] * mask_z[:, None, :, None] * mask_y[:, None, None, :]
     for step in range(ITERS):
-        padded = padded_2(current, (("depth", 2), ("gx", 1)), 4)
+        padded = padded_2(current, (("gx", 1), ("depth", 2)), 4)
         source = source_wavelet[step][:, None, None, None] * onehot
         nxt = advance(current, before, padded, speed, damping, source)
         before, current = (current, nxt)

time: 229 us -> 178 us (0.78)
  the two profiles are of different devices: /device:TPU:217 before, /device:TPU:0 now
where the time goes in v1:
time: 178 us
  other arithmetic  70.8 us (40%)
  waiting for transfers between devices  61.1 us (34%)
  starting transfers between devices  37.3 us (21%)
  local copies, waits for them, and re-layouts  6.9 us (4%)
  between operations  1.98 us (1%)
    div x8, other arithmetic, advance(): (2.0 * current - (1.0 - damping) * before + speed * lap + source) / (1.0...  54.6 us
    ppermute x16, waiting for transfers between devices, padded_2(): low = lax.ppermute(last, axis, up)  40.4 us
    ppermute x16, starting transfers between devices, padded_2(): high = lax.ppermute(leading, axis, [(b, a) for a, b in up])  35 us
    ppermute x16, waiting for transfers between devices, padded_2(): high = lax.ppermute(leading, axis, [(b, a) for a, b in up])  20.7 us
    concatenate x8, other arithmetic, padded_2(): jnp.concatenate([jnp.pad(low, around), shard, jnp.pad(high, around)], axi...  7.36 us
    add x1, other arithmetic, lookup_speed(): speed + jnp.where(class_map == klass, courant_sq[klass], jnp.float32(0.0))  5.36 us
    slice x16, local copies, waits for them, and re-layouts, padded_2(): leading = lax.slice_in_dim(shard, 0, width, axis=dim)  5.06 us
  transfers between devices with their start and end apart: 32, of which 14 were waited for; matrix products, arithmetic and copies ran while one was open for 7% of the time, Pallas kernels for 0%

profile of v1, /device:TPU:0, one launch (start us, length us, event | category | flops | bytes accessed | tf_op | source)
XLA Modules:
  0.0 178.1 jit_solution(7989025066254416256)
XLA Ops:
  0.7 1.9 %fusion.304 = (f32[4,4,32,128]{3,2,1,0:T(8,128)}, f32[4,4,32,128]{3,2,1,0:T(8,128)}) fusion(f32[4,32,32,128]{3,2,1,0:T(8,128)} %param.7), kind=kLoop, calls=%fused_computation.576 | loop fusion | bytes 1048576 | tf_op jit(solution)/shard_map/slice | solution.py:19
  2.6 3.5 %collective-permute-start = (f32[4,4,32,128]{3,2,1,0:T(8,128)}, f32[4,4,32,128]{3,2,1,0:T(8,128)}, u32[]{:S(2)}, u32[]{:S(2)}) collective-permute-start(f32[4,4,32,128]{3,2,1,0:T(8,128)} %get-tuple-element.59), channel_id=1, source_target_pairs={{1,0},{2,1},{3,2},{4,3},{5,4},{6,5},{7,6},{8,7},{9,8},{10,9},{11,1... | collective-permute-start | bytes 786440 | tf_op jit(solution)/shard_map/ppermute | solution.py:22
  6.1 2.2 %fusion.303 = (f32[4,32,4,128]{3,2,1,0:T(4,128)}, f32[4,32,4,128]{3,2,1,0:T(4,128)}) fusion(f32[4,32,32,128]{3,2,1,0:T(8,128)} %param.7), kind=kLoop, calls=%fused_computation.575 | loop fusion | bytes 1048576 | tf_op jit(solution)/shard_map/slice | solution.py:19
  8.3 5.0 %collective-permute-start.2 = (f32[4,32,4,128]{3,2,1,0:T(4,128)}, f32[4,32,4,128]{3,2,1,0:T(4,128)}, u32[]{:S(2)}, u32[]{:S(2)}) collective-permute-start(f32[4,32,4,128]{3,2,1,0:T(4,128)} %get-tuple-element.57), channel_id=1, source_target_pairs={{16,0},{32,16},{48,32},{64,48},{80,64},{96,80},{112,96},{128,112},... | collective-permute-start | bytes 786440 | tf_op jit(solution)/shard_map/ppermute | solution.py:22
  13.4 0.2 slice_reduce_fusion.9
  13.6 0.7 fusion.305
  14.3 0.1 broadcast_multiply_fusion
  14.4 5.4 %select_add_fusion = f32[32,32,128]{2,1,0:T(8,128)S(1)} fusion(s32[32,32,128]{2,1,0:T(8,128)S(1)} %copy-done.3, f32[]{:T(128)} %bitcast.8, f32[]{:T(128)} %bitcast.7, f32[]{:T(128)} %bitcast.6, f32[]{:T(128)} %bitcast.5, f32[]{:T(128)} %bitcast.4, f32[]{:T(128)} %bitcast.3, f32[]{:T(128)} %bitcast.2, f32[]{:T(128)} %bitcast.1), kind=kLoop, calls=%fused_computation.506 | loop fusion | flops 3014656 | bytes 1048608 | tf_op jit(solution)/shard_map/add | solution.py:76
  20.5 0.3 slice_reduce_fusion
  20.9 1.0 broadcast_select_fusion.31
  21.9 1.0 broadcast_select_fusion.15
  23.0 0.9 select_maximum_fusion.15
  24.0 0.7 copy-done.2
  24.6 6.7 %fusion.236 = f32[4,32,32,128]{3,2,1,0:T(8,128)S(1)} fusion(f32[4,32,32,128]{3,2,1,0:T(8,128)S(1)} %copy-done, f32[4,4,32,128]{3,2,1,0:T(8,128)S(1)} %broadcast_select_fusion.30, f32[4,4,32,128]{3,2,1,0:T(8,128)S(1)} %broadcast_select_fusion.31, f32[4,40,36,128]{3,2,1,0:T(8,128)S(1)} %get-tuple-element.28, f32[4,40,36,128]{3,2,1,0:T(8,128)S(1)} %get-tuple-element.27, ...), kind=kLoop, calls=%fused_computation.422 | loop fusion | flops 24117248 | bytes 24135952 | tf_op jit(solution)/shard_map/div | solution.py:60
  31.4 4.0 %collective-permute-start.4 = (f32[4,4,32,128]{3,2,1,0:T(8,128)S(1)}, f32[4,4,32,128]{3,2,1,0:T(8,128)S(1)}, u32[]{:S(2)}, u32[]{:S(2)}) collective-permute-start(f32[4,4,32,128]{3,2,1,0:T(8,128)S(1)} %get-tuple-element.55), channel_id=1, source_target_pairs={{1,0},{2,1},{3,2},{4,3},{5,4},{6,5},{7,6},{8,7},{9,8},{10,9},{11,1... | collective-permute-start | bytes 786440 | tf_op jit(solution)/shard_map/ppermute | solution.py:22
  35.5 0.1 fusion.301
  35.6 2.7 %collective-permute-start.6 = (f32[4,32,4,128]{3,2,1,0:T(4,128)S(1)}, f32[4,32,4,128]{3,2,1,0:T(4,128)S(1)}, u32[]{:S(2)}, u32[]{:S(2)}) collective-permute-start(f32[4,32,4,128]{3,2,1,0:T(4,128)S(1)} %get-tuple-element.53), channel_id=1, source_target_pairs={{16,0},{32,16},{48,32},{64,48},{80,64},{96,80},{112,96},{128,112},... | collective-permute-start | bytes 786440 | tf_op jit(solution)/shard_map/ppermute | solution.py:22
  38.2 1.2 collective-permute-done.4
  39.4 5.7 %collective-permute-done.5 = f32[4,4,32,128]{3,2,1,0:T(8,128)S(1)} collective-permute-done((f32[4,4,32,128]{3,2,1,0:T(8,128)S(1)}, f32[4,4,32,128]{3,2,1,0:T(8,128)S(1)}, u32[]{:S(2)}, u32[]{:S(2)}) %collective-permute-start.5) | collective-permute-done | bytes 262176 | tf_op jit(solution)/shard_map/ppermute | solution.py:21
  45.3 0.9 select_maximum_fusion.13
  46.3 6.7 %fusion.204 = f32[4,32,32,128]{3,2,1,0:T(8,128)S(1)} fusion(f32[4,32,32,128]{3,2,1,0:T(8,128)S(1)} %fusion.236, f32[4,4,32,128]{3,2,1,0:T(8,128)S(1)} %broadcast_select_fusion.28, f32[4,4,32,128]{3,2,1,0:T(8,128)S(1)} %broadcast_select_fusion.29, f32[4,40,36,128]{3,2,1,0:T(8,128)S(1)} %get-tuple-element.26, f32[4,40,36,128]{3,2,1,0:T(8,128)S(1)} %get-tuple-element.25, ...), kind=kLoop, calls=%fused_computation.390 | loop fusion | flops 24117248 | bytes 24135952 | tf_op jit(solution)/shard_map/div | solution.py:60
  53.1 5.1 %collective-permute-start.8 = (f32[4,4,32,128]{3,2,1,0:T(8,128)S(1)}, f32[4,4,32,128]{3,2,1,0:T(8,128)S(1)}, u32[]{:S(2)}, u32[]{:S(2)}) collective-permute-start(f32[4,4,32,128]{3,2,1,0:T(8,128)S(1)} %get-tuple-element.51), channel_id=1, source_target_pairs={{1,0},{2,1},{3,2},{4,3},{5,4},{6,5},{7,6},{8,7},{9,8},{10,9},{11,1... | collective-permute-start | bytes 786440 | tf_op jit(solution)/shard_map/ppermute | solution.py:22
  58.2 0.1 fusion.299
  58.3 0.6 collective-permute-start.10
  58.9 3.2 %collective-permute-done.8 = f32[4,4,32,128]{3,2,1,0:T(8,128)S(1)} collective-permute-done((f32[4,4,32,128]{3,2,1,0:T(8,128)S(1)}, f32[4,4,32,128]{3,2,1,0:T(8,128)S(1)}, u32[]{:S(2)}, u32[]{:S(2)}) %collective-permute-start.8) | collective-permute-done | bytes 262176 | tf_op jit(solution)/shard_map/ppermute | solution.py:22
  62.1 5.8 %collective-permute-done.9 = f32[4,4,32,128]{3,2,1,0:T(8,128)S(1)} collective-permute-done((f32[4,4,32,128]{3,2,1,0:T(8,128)S(1)}, f32[4,4,32,128]{3,2,1,0:T(8,128)S(1)}, u32[]{:S(2)}, u32[]{:S(2)}) %collective-permute-start.9) | collective-permute-done | bytes 262176 | tf_op jit(solution)/shard_map/ppermute | solution.py:21
  68.0 0.9 select_maximum_fusion.11
  69.0 6.7 %fusion.172 = f32[4,32,32,128]{3,2,1,0:T(8,128)S(1)} fusion(f32[4,32,32,128]{3,2,1,0:T(8,128)S(1)} %fusion.204, f32[4,4,32,128]{3,2,1,0:T(8,128)S(1)} %broadcast_select_fusion.26, f32[4,4,32,128]{3,2,1,0:T(8,128)S(1)} %broadcast_select_fusion.27, f32[4,40,36,128]{3,2,1,0:T(8,128)S(1)} %get-tuple-element.24, f32[4,40,36,128]{3,2,1,0:T(8,128)S(1)} %get-tuple-element.23, ...), kind=kLoop, calls=%fused_computation.358 | loop fusion | flops 24117248 | bytes 24135952 | tf_op jit(solution)/shard_map/div | solution.py:60
  75.7 2.8 %collective-permute-start.12 = (f32[4,4,32,128]{3,2,1,0:T(8,128)S(1)}, f32[4,4,32,128]{3,2,1,0:T(8,128)S(1)}, u32[]{:S(2)}, u32[]{:S(2)}) collective-permute-start(f32[4,4,32,128]{3,2,1,0:T(8,128)S(1)} %get-tuple-element.47), channel_id=1, source_target_pairs={{1,0},{2,1},{3,2},{4,3},{5,4},{6,5},{7,6},{8,7},{9,8},{10,9},{11,1... | collective-permute-start | bytes 786440 | tf_op jit(solution)/shard_map/ppermute | solution.py:22
  78.5 0.1 fusion.297
  78.6 0.5 collective-permute-start.15
  79.1 3.3 %collective-permute-done.12 = f32[4,4,32,128]{3,2,1,0:T(8,128)S(1)} collective-permute-done((f32[4,4,32,128]{3,2,1,0:T(8,128)S(1)}, f32[4,4,32,128]{3,2,1,0:T(8,128)S(1)}, u32[]{:S(2)}, u32[]{:S(2)}) %collective-permute-start.12) | collective-permute-done | bytes 262176 | tf_op jit(solution)/shard_map/ppermute | solution.py:22
  82.4 5.8 %collective-permute-done.13 = f32[4,4,32,128]{3,2,1,0:T(8,128)S(1)} collective-permute-done((f32[4,4,32,128]{3,2,1,0:T(8,128)S(1)}, f32[4,4,32,128]{3,2,1,0:T(8,128)S(1)}, u32[]{:S(2)}, u32[]{:S(2)}) %collective-permute-start.13) | collective-permute-done | bytes 262176 | tf_op jit(solution)/shard_map/ppermute | solution.py:21
  88.4 0.9 select_maximum_fusion.9
  89.3 6.7 %fusion.140 = f32[4,32,32,128]{3,2,1,0:T(8,128)S(1)} fusion(f32[4,32,32,128]{3,2,1,0:T(8,128)S(1)} %fusion.172, f32[4,4,32,128]{3,2,1,0:T(8,128)S(1)} %broadcast_select_fusion.24, f32[4,4,32,128]{3,2,1,0:T(8,128)S(1)} %broadcast_select_fusion.25, f32[4,40,36,128]{3,2,1,0:T(8,128)S(1)} %get-tuple-element.22, f32[4,40,36,128]{3,2,1,0:T(8,128)S(1)} %get-tuple-element.21, ...), kind=kLoop, calls=%fused_computation.326 | loop fusion | flops 24117248 | bytes 24135952 | tf_op jit(solution)/shard_map/div | solution.py:60
  96.1 2.8 %collective-permute-start.16 = (f32[4,4,32,128]{3,2,1,0:T(8,128)S(1)}, f32[4,4,32,128]{3,2,1,0:T(8,128)S(1)}, u32[]{:S(2)}, u32[]{:S(2)}) collective-permute-start(f32[4,4,32,128]{3,2,1,0:T(8,128)S(1)} %get-tuple-element.43), channel_id=1, source_target_pairs={{1,0},{2,1},{3,2},{4,3},{5,4},{6,5},{7,6},{8,7},{9,8},{10,9},{11,1... | collective-permute-start | bytes 786440 | tf_op jit(solution)/shard_map/ppermute | solution.py:22
  98.8 0.1 fusion.295
  99.0 0.5 collective-permute-start.19
  99.5 3.3 %collective-permute-done.16 = f32[4,4,32,128]{3,2,1,0:T(8,128)S(1)} collective-permute-done((f32[4,4,32,128]{3,2,1,0:T(8,128)S(1)}, f32[4,4,32,128]{3,2,1,0:T(8,128)S(1)}, u32[]{:S(2)}, u32[]{:S(2)}) %collective-permute-start.16) | collective-permute-done | bytes 262176 | tf_op jit(solution)/shard_map/ppermute | solution.py:22
  102.7 5.8 %collective-permute-done.17 = f32[4,4,32,128]{3,2,1,0:T(8,128)S(1)} collective-permute-done((f32[4,4,32,128]{3,2,1,0:T(8,128)S(1)}, f32[4,4,32,128]{3,2,1,0:T(8,128)S(1)}, u32[]{:S(2)}, u32[]{:S(2)}) %collective-permute-start.17) | collective-permute-done | bytes 262176 | tf_op jit(solution)/shard_map/ppermute | solution.py:21
  108.7 0.9 select_maximum_fusion.7
  109.6 6.7 %fusion.108 = f32[4,32,32,128]{3,2,1,0:T(8,128)S(1)} fusion(f32[4,32,32,128]{3,2,1,0:T(8,128)S(1)} %fusion.140, f32[4,4,32,128]{3,2,1,0:T(8,128)S(1)} %broadcast_select_fusion.22, f32[4,4,32,128]{3,2,1,0:T(8,128)S(1)} %broadcast_select_fusion.23, f32[4,40,36,128]{3,2,1,0:T(8,128)S(1)} %get-tuple-element.20, f32[4,40,36,128]{3,2,1,0:T(8,128)S(1)} %get-tuple-element.19, ...), kind=kLoop, calls=%fused_computation.294 | loop fusion | flops 24117248 | bytes 24135952 | tf_op jit(solution)/shard_map/div | solution.py:60
  116.4 2.8 %collective-permute-start.20 = (f32[4,4,32,128]{3,2,1,0:T(8,128)S(1)}, f32[4,4,32,128]{3,2,1,0:T(8,128)S(1)}, u32[]{:S(2)}, u32[]{:S(2)}) collective-permute-start(f32[4,4,32,128]{3,2,1,0:T(8,128)S(1)} %get-tuple-element.39), channel_id=1, source_target_pairs={{1,0},{2,1},{3,2},{4,3},{5,4},{6,5},{7,6},{8,7},{9,8},{10,9},{11,1... | collective-permute-start | bytes 786440 | tf_op jit(solution)/shard_map/ppermute | solution.py:22
  119.2 0.1 fusion.293
  119.3 0.4 collective-permute-start.23
  119.8 3.3 %collective-permute-done.20 = f32[4,4,32,128]{3,2,1,0:T(8,128)S(1)} collective-permute-done((f32[4,4,32,128]{3,2,1,0:T(8,128)S(1)}, f32[4,4,32,128]{3,2,1,0:T(8,128)S(1)}, u32[]{:S(2)}, u32[]{:S(2)}) %collective-permute-start.20) | collective-permute-done | bytes 262176 | tf_op jit(solution)/shard_map/ppermute | solution.py:22
  123.1 5.8 %collective-permute-done.21 = f32[4,4,32,128]{3,2,1,0:T(8,128)S(1)} collective-permute-done((f32[4,4,32,128]{3,2,1,0:T(8,128)S(1)}, f32[4,4,32,128]{3,2,1,0:T(8,128)S(1)}, u32[]{:S(2)}, u32[]{:S(2)}) %collective-permute-start.21) | collective-permute-done | bytes 262176 | tf_op jit(solution)/shard_map/ppermute | solution.py:21
  129.0 0.9 select_maximum_fusion.5
  130.0 6.7 %fusion.76 = f32[4,32,32,128]{3,2,1,0:T(8,128)S(1)} fusion(f32[4,32,32,128]{3,2,1,0:T(8,128)S(1)} %fusion.108, f32[4,4,32,128]{3,2,1,0:T(8,128)S(1)} %broadcast_select_fusion.20, f32[4,4,32,128]{3,2,1,0:T(8,128)S(1)} %broadcast_select_fusion.21, f32[4,40,36,128]{3,2,1,0:T(8,128)S(1)} %get-tuple-element.18, f32[4,40,36,128]{3,2,1,0:T(8,128)S(1)} %get-tuple-element.17, ...), kind=kLoop, calls=%fused_computation.262 | loop fusion | flops 24117248 | bytes 24135952 | tf_op jit(solution)/shard_map/div | solution.py:60
  136.7 2.8 %collective-permute-start.24 = (f32[4,4,32,128]{3,2,1,0:T(8,128)S(1)}, f32[4,4,32,128]{3,2,1,0:T(8,128)S(1)}, u32[]{:S(2)}, u32[]{:S(2)}) collective-permute-start(f32[4,4,32,128]{3,2,1,0:T(8,128)S(1)} %get-tuple-element.35), channel_id=1, source_target_pairs={{1,0},{2,1},{3,2},{4,3},{5,4},{6,5},{7,6},{8,7},{9,8},{10,9},{11,1... | collective-permute-start | bytes 786440 | tf_op jit(solution)/shard_map/ppermute | solution.py:22
  139.5 0.1 fusion.291
  139.7 0.4 collective-permute-start.27
  140.1 3.3 %collective-permute-done.24 = f32[4,4,32,128]{3,2,1,0:T(8,128)S(1)} collective-permute-done((f32[4,4,32,128]{3,2,1,0:T(8,128)S(1)}, f32[4,4,32,128]{3,2,1,0:T(8,128)S(1)}, u32[]{:S(2)}, u32[]{:S(2)}) %collective-permute-start.24) | collective-permute-done | bytes 262176 | tf_op jit(solution)/shard_map/ppermute | solution.py:22
  143.4 5.8 %collective-permute-done.25 = f32[4,4,32,128]{3,2,1,0:T(8,128)S(1)} collective-permute-done((f32[4,4,32,128]{3,2,1,0:T(8,128)S(1)}, f32[4,4,32,128]{3,2,1,0:T(8,128)S(1)}, u32[]{:S(2)}, u32[]{:S(2)}) %collective-permute-start.25) | collective-permute-done | bytes 262176 | tf_op jit(solution)/shard_map/ppermute | solution.py:21
  149.4 0.9 select_maximum_fusion.3
  150.3 6.7 %fusion.44 = f32[4,32,32,128]{3,2,1,0:T(8,128)S(1)} fusion(f32[4,32,32,128]{3,2,1,0:T(8,128)S(1)} %fusion.76, f32[4,4,32,128]{3,2,1,0:T(8,128)S(1)} %broadcast_select_fusion.18, f32[4,4,32,128]{3,2,1,0:T(8,128)S(1)} %broadcast_select_fusion.19, f32[4,40,36,128]{3,2,1,0:T(8,128)S(1)} %get-tuple-element.16, f32[4,40,36,128]{3,2,1,0:T(8,128)S(1)} %get-tuple-element.15, ...), kind=kLoop, calls=%fused_computation.230 | loop fusion | flops 24117248 | bytes 24135952 | tf_op jit(solution)/shard_map/div | solution.py:60
  157.1 2.8 %collective-permute-start.28 = (f32[4,4,32,128]{3,2,1,0:T(8,128)S(1)}, f32[4,4,32,128]{3,2,1,0:T(8,128)S(1)}, u32[]{:S(2)}, u32[]{:S(2)}) collective-permute-start(f32[4,4,32,128]{3,2,1,0:T(8,128)S(1)} %get-tuple-element.31), channel_id=1, source_target_pairs={{1,0},{2,1},{3,2},{4,3},{5,4},{6,5},{7,6},{8,7},{9,8},{10,9},{11,1... | collective-permute-start | bytes 786440 | tf_op jit(solution)/shard_map/ppermute | solution.py:22
  159.9 0.1 fusion.289
  159.9 0.1 collective-permute-start.30
  160.0 0.4 collective-permute-start.31
  160.5 3.3 %collective-permute-done.28 = f32[4,4,32,128]{3,2,1,0:T(8,128)S(1)} collective-permute-done((f32[4,4,32,128]{3,2,1,0:T(8,128)S(1)}, f32[4,4,32,128]{3,2,1,0:T(8,128)S(1)}, u32[]{:S(2)}, u32[]{:S(2)}) %collective-permute-start.28) | collective-permute-done | bytes 262176 | tf_op jit(solution)/shard_map/ppermute | solution.py:22
  163.8 5.8 %collective-permute-done.29 = f32[4,4,32,128]{3,2,1,0:T(8,128)S(1)} collective-permute-done((f32[4,4,32,128]{3,2,1,0:T(8,128)S(1)}, f32[4,4,32,128]{3,2,1,0:T(8,128)S(1)}, u32[]{:S(2)}, u32[]{:S(2)}) %collective-permute-start.29) | collective-permute-done | bytes 262176 | tf_op jit(solution)/shard_map/ppermute | solution.py:21
  169.7 0.9 select_maximum_fusion.1
  170.7 7.5 %fusion.12 = f32[4,32,32,128]{3,2,1,0:T(8,128)} fusion(f32[4,32,32,128]{3,2,1,0:T(8,128)S(1)} %fusion.44, f32[4,4,32,128]{3,2,1,0:T(8,128)S(1)} %broadcast_select_fusion.16, f32[4,4,32,128]{3,2,1,0:T(8,128)S(1)} %broadcast_select_fusion.17, f32[4,40,36,128]{3,2,1,0:T(8,128)S(1)} %get-tuple-element.14, f32[4,40,36,128]{3,2,1,0:T(8,128)S(1)} %get-tuple-element.13, ...), kind=kLoop, calls=%fused_computation.198 | loop fusion | flops 24117248 | bytes 24135952 | tf_op jit(solution)/shard_map/div | solution.py:60
  (88 shorter events, 2.0 us)
Async XLA Ops:
  0.6 12.7 %copy-start.6 = (s32[4,3]{1,0:T(4,128)S(1)}, s32[4,3]{1,0:T(4,128)}, u32[]{:S(2)}) copy-start(s32[4,3]{1,0:T(4,128)} %param.11) | copy-start | bytes 148
  0.6 12.9 %copy-start.5 = (f32[8]{0:T(128)S(1)}, f32[8]{0:T(128)}, u32[]{:S(2)}) copy-start(f32[8]{0:T(128)} %param.10) | copy-start | bytes 100
  0.7 13.8 %copy-start.3 = (s32[32,32,128]{2,1,0:T(8,128)S(1)}, s32[32,32,128]{2,1,0:T(8,128)}, u32[]{:S(2)}) copy-start(s32[32,32,128]{2,1,0:T(8,128)} %param.9) | copy-start | bytes 1572868
  0.7 19.9 %copy-start.4 = (f32[8,4]{0,1:T(4,128)S(1)}, f32[8,4]{0,1:T(4,128)}, u32[]{:S(2)}) copy-start(f32[8,4]{0,1:T(4,128)} %param.12) | copy-start | bytes 388
  2.6 18.3 %collective-permute-start = (f32[4,4,32,128]{3,2,1,0:T(8,128)}, f32[4,4,32,128]{3,2,1,0:T(8,128)}, u32[]{:S(2)}, u32[]{:S(2)}) collective-permute-start(f32[4,4,32,128]{3,2,1,0:T(8,128)} %get-tuple-element.59), channel_id=1, source_target_pairs={{1,0},{2,1},{3,2},{4,3},{5,4},{6,5},{7,6},{8,7},{9,8},{10,9},{11,1... | collective-permute-start | bytes 786440 | tf_op jit(solution)/shard_map/ppermute | solution.py:22
  6.1 16.9 %copy-start = (f32[4,32,32,128]{3,2,1,0:T(8,128)S(1)}, f32[4,32,32,128]{3,2,1,0:T(8,128)}, u32[]{:S(2)}) copy-start(f32[4,32,32,128]{3,2,1,0:T(8,128)} %param.7) | copy-start | bytes 6291460
  6.1 15.8 %collective-permute-start.1 = (f32[4,4,32,128]{3,2,1,0:T(8,128)}, f32[4,4,32,128]{3,2,1,0:T(8,128)S(1)}, u32[]{:S(2)}, u32[]{:S(2)}) collective-permute-start(f32[4,4,32,128]{3,2,1,0:T(8,128)} %get-tuple-element.60), channel_id=1, source_target_pairs={{0,1},{1,2},{2,3},{3,4},{4,5},{5,6},{6,7},{7,8},{8,9},{9,10},{10,1... | collective-permute-start | bytes 786440 | tf_op jit(solution)/shard_map/ppermute | solution.py:21
  8.3 13.5 %collective-permute-start.2 = (f32[4,32,4,128]{3,2,1,0:T(4,128)}, f32[4,32,4,128]{3,2,1,0:T(4,128)}, u32[]{:S(2)}, u32[]{:S(2)}) collective-permute-start(f32[4,32,4,128]{3,2,1,0:T(4,128)} %get-tuple-element.57), channel_id=1, source_target_pairs={{16,0},{32,16},{48,32},{64,48},{80,64},{96,80},{112,96},{128,112},... | collective-permute-start | bytes 786440 | tf_op jit(solution)/shard_map/ppermute | solution.py:22
  13.4 9.6 %collective-permute-start.3 = (f32[4,32,4,128]{3,2,1,0:T(4,128)}, f32[4,32,4,128]{3,2,1,0:T(4,128)}, u32[]{:S(2)}, u32[]{:S(2)}) collective-permute-start(f32[4,32,4,128]{3,2,1,0:T(4,128)} %get-tuple-element.58), channel_id=1, source_target_pairs={{0,16},{16,32},{32,48},{48,64},{64,80},{80,96},{96,112},{112,128},... | collective-permute-start | bytes 786440 | tf_op jit(solution)/shard_map/ppermute | solution.py:21
  23.0 1.6 copy-start.2
  31.4 8.0 %collective-permute-start.4 = (f32[4,4,32,128]{3,2,1,0:T(8,128)S(1)}, f32[4,4,32,128]{3,2,1,0:T(8,128)S(1)}, u32[]{:S(2)}, u32[]{:S(2)}) collective-permute-start(f32[4,4,32,128]{3,2,1,0:T(8,128)S(1)} %get-tuple-element.55), channel_id=1, source_target_pairs={{1,0},{2,1},{3,2},{4,3},{5,4},{6,5},{7,6},{8,7},{9,8},{10,9},{11,1... | collective-permute-start | bytes 786440 | tf_op jit(solution)/shard_map/ppermute | solution.py:22
  35.5 9.7 %collective-permute-start.5 = (f32[4,4,32,128]{3,2,1,0:T(8,128)S(1)}, f32[4,4,32,128]{3,2,1,0:T(8,128)S(1)}, u32[]{:S(2)}, u32[]{:S(2)}) collective-permute-start(f32[4,4,32,128]{3,2,1,0:T(8,128)S(1)} %get-tuple-element.56), channel_id=1, source_target_pairs={{0,1},{1,2},{2,3},{3,4},{4,5},{5,6},{6,7},{7,8},{8,9},{9,10},{10,1... | collective-permute-start | bytes 786440 | tf_op jit(solution)/shard_map/ppermute | solution.py:21
  35.6 9.6 %collective-permute-start.6 = (f32[4,32,4,128]{3,2,1,0:T(4,128)S(1)}, f32[4,32,4,128]{3,2,1,0:T(4,128)S(1)}, u32[]{:S(2)}, u32[]{:S(2)}) collective-permute-start(f32[4,32,4,128]{3,2,1,0:T(4,128)S(1)} %get-tuple-element.53), channel_id=1, source_target_pairs={{16,0},{32,16},{48,32},{64,48},{80,64},{96,80},{112,96},{128,112},... | collective-permute-start | bytes 786440 | tf_op jit(solution)/shard_map/ppermute | solution.py:22
  38.2 7.0 %collective-permute-start.7 = (f32[4,32,4,128]{3,2,1,0:T(4,128)S(1)}, f32[4,32,4,128]{3,2,1,0:T(4,128)S(1)}, u32[]{:S(2)}, u32[]{:S(2)}) collective-permute-start(f32[4,32,4,128]{3,2,1,0:T(4,128)S(1)} %get-tuple-element.54), channel_id=1, source_target_pairs={{0,16},{16,32},{32,48},{48,64},{64,80},{80,96},{96,112},{112,128},... | collective-permute-start | bytes 786440 | tf_op jit(solution)/shard_map/ppermute | solution.py:21
  53.1 9.0 %collective-permute-start.8 = (f32[4,4,32,128]{3,2,1,0:T(8,128)S(1)}, f32[4,4,32,128]{3,2,1,0:T(8,128)S(1)}, u32[]{:S(2)}, u32[]{:S(2)}) collective-permute-start(f32[4,4,32,128]{3,2,1,0:T(8,128)S(1)} %get-tuple-element.51), channel_id=1, source_target_pairs={{1,0},{2,1},{3,2},{4,3},{5,4},{6,5},{7,6},{8,7},{9,8},{10,9},{11,1... | collective-permute-start | bytes 786440 | tf_op jit(solution)/shard_map/ppermute | solution.py:22
  58.2 9.7 %collective-permute-start.9 = (f32[4,4,32,128]{3,2,1,0:T(8,128)S(1)}, f32[4,4,32,128]{3,2,1,0:T(8,128)S(1)}, u32[]{:S(2)}, u32[]{:S(2)}) collective-permute-start(f32[4,4,32,128]{3,2,1,0:T(8,128)S(1)} %get-tuple-element.52), channel_id=1, source_target_pairs={{0,1},{1,2},{2,3},{3,4},{4,5},{5,6},{6,7},{7,8},{8,9},{9,10},{10,1... | collective-permute-start | bytes 786440 | tf_op jit(solution)/shard_map/ppermute | solution.py:21
  58.3 9.6 %collective-permute-start.10 = (f32[4,32,4,128]{3,2,1,0:T(4,128)S(1)}, f32[4,32,4,128]{3,2,1,0:T(4,128)S(1)}, u32[]{:S(2)}, u32[]{:S(2)}) collective-permute-start(f32[4,32,4,128]{3,2,1,0:T(4,128)S(1)} %get-tuple-element.49), channel_id=1, source_target_pairs={{16,0},{32,16},{48,32},{64,48},{80,64},{96,80},{112,96},{128,112},... | collective-permute-start | bytes 786440 | tf_op jit(solution)/shard_map/ppermute | solution.py:22
  58.9 9.1 %collective-permute-start.11 = (f32[4,32,4,128]{3,2,1,0:T(4,128)S(1)}, f32[4,32,4,128]{3,2,1,0:T(4,128)S(1)}, u32[]{:S(2)}, u32[]{:S(2)}) collective-permute-start(f32[4,32,4,128]{3,2,1,0:T(4,128)S(1)} %get-tuple-element.50), channel_id=1, source_target_pairs={{0,16},{16,32},{32,48},{48,64},{64,80},{80,96},{96,112},{112,128},... | collective-permute-start | bytes 786440 | tf_op jit(solution)/shard_map/ppermute | solution.py:21
  75.7 6.6 %collective-permute-start.12 = (f32[4,4,32,128]{3,2,1,0:T(8,128)S(1)}, f32[4,4,32,128]{3,2,1,0:T(8,128)S(1)}, u32[]{:S(2)}, u32[]{:S(2)}) collective-permute-start(f32[4,4,32,128]{3,2,1,0:T(8,128)S(1)} %get-tuple-element.47), channel_id=1, source_target_pairs={{1,0},{2,1},{3,2},{4,3},{5,4},{6,5},{7,6},{8,7},{9,8},{10,9},{11,1... | collective-permute-start | bytes 786440 | tf_op jit(solution)/shard_map/ppermute | solution.py:22
  78.5 9.7 %collective-permute-start.13 = (f32[4,4,32,128]{3,2,1,0:T(8,128)S(1)}, f32[4,4,32,128]{3,2,1,0:T(8,128)S(1)}, u32[]{:S(2)}, u32[]{:S(2)}) collective-permute-start(f32[4,4,32,128]{3,2,1,0:T(8,128)S(1)} %get-tuple-element.48), channel_id=1, source_target_pairs={{0,1},{1,2},{2,3},{3,4},{4,5},{5,6},{6,7},{7,8},{8,9},{9,10},{10,1... | collective-permute-start | bytes 786440 | tf_op jit(solution)/shard_map/ppermute | solution.py:21
  78.6 9.6 %collective-permute-start.14 = (f32[4,32,4,128]{3,2,1,0:T(4,128)S(1)}, f32[4,32,4,128]{3,2,1,0:T(4,128)S(1)}, u32[]{:S(2)}, u32[]{:S(2)}) collective-permute-start(f32[4,32,4,128]{3,2,1,0:T(4,128)S(1)} %get-tuple-element.45), channel_id=1, source_target_pairs={{16,0},{32,16},{48,32},{64,48},{80,64},{96,80},{112,96},{128,112},... | collective-permute-start | bytes 786440 | tf_op jit(solution)/shard_map/ppermute | solution.py:22
  78.6 9.7 %collective-permute-start.15 = (f32[4,32,4,128]{3,2,1,0:T(4,128)S(1)}, f32[4,32,4,128]{3,2,1,0:T(4,128)S(1)}, u32[]{:S(2)}, u32[]{:S(2)}) collective-permute-start(f32[4,32,4,128]{3,2,1,0:T(4,128)S(1)} %get-tuple-element.46), channel_id=1, source_target_pairs={{0,16},{16,32},{32,48},{48,64},{64,80},{80,96},{96,112},{112,128},... | collective-permute-start | bytes 786440 | tf_op jit(solution)/shard_map/ppermute | solution.py:21
  96.1 6.6 %collective-permute-start.16 = (f32[4,4,32,128]{3,2,1,0:T(8,128)S(1)}, f32[4,4,32,128]{3,2,1,0:T(8,128)S(1)}, u32[]{:S(2)}, u32[]{:S(2)}) collective-permute-start(f32[4,4,32,128]{3,2,1,0:T(8,128)S(1)} %get-tuple-element.43), channel_id=1, source_target_pairs={{1,0},{2,1},{3,2},{4,3},{5,4},{6,5},{7,6},{8,7},{9,8},{10,9},{11,1... | collective-permute-start | bytes 786440 | tf_op jit(solution)/shard_map/ppermute | solution.py:22
  98.8 9.7 %collective-permute-start.17 = (f32[4,4,32,128]{3,2,1,0:T(8,128)S(1)}, f32[4,4,32,128]{3,2,1,0:T(8,128)S(1)}, u32[]{:S(2)}, u32[]{:S(2)}) collective-permute-start(f32[4,4,32,128]{3,2,1,0:T(8,128)S(1)} %get-tuple-element.44), channel_id=1, source_target_pairs={{0,1},{1,2},{2,3},{3,4},{4,5},{5,6},{6,7},{7,8},{8,9},{9,10},{10,1... | collective-permute-start | bytes 786440 | tf_op jit(solution)/shard_map/ppermute | solution.py:21
  98.9 9.6 %collective-permute-start.18 = (f32[4,32,4,128]{3,2,1,0:T(4,128)S(1)}, f32[4,32,4,128]{3,2,1,0:T(4,128)S(1)}, u32[]{:S(2)}, u32[]{:S(2)}) collective-permute-start(f32[4,32,4,128]{3,2,1,0:T(4,128)S(1)} %get-tuple-element.41), channel_id=1, source_target_pairs={{16,0},{32,16},{48,32},{64,48},{80,64},{96,80},{112,96},{128,112},... | collective-permute-start | bytes 786440 | tf_op jit(solution)/shard_map/ppermute | solution.py:22
  99.0 9.6 %collective-permute-start.19 = (f32[4,32,4,128]{3,2,1,0:T(4,128)S(1)}, f32[4,32,4,128]{3,2,1,0:T(4,128)S(1)}, u32[]{:S(2)}, u32[]{:S(2)}) collective-permute-start(f32[4,32,4,128]{3,2,1,0:T(4,128)S(1)} %get-tuple-element.42), channel_id=1, source_target_pairs={{0,16},{16,32},{32,48},{48,64},{64,80},{80,96},{96,112},{112,128},... | collective-permute-start | bytes 786440 | tf_op jit(solution)/shard_map/ppermute | solution.py:21
  116.4 6.6 %collective-permute-start.20 = (f32[4,4,32,128]{3,2,1,0:T(8,128)S(1)}, f32[4,4,32,128]{3,2,1,0:T(8,128)S(1)}, u32[]{:S(2)}, u32[]{:S(2)}) collective-permute-start(f32[4,4,32,128]{3,2,1,0:T(8,128)S(1)} %get-tuple-element.39), channel_id=1, source_target_pairs={{1,0},{2,1},{3,2},{4,3},{5,4},{6,5},{7,6},{8,7},{9,8},{10,9},{11,1... | collective-permute-start | bytes 786440 | tf_op jit(solution)/shard_map/ppermute | solution.py:22
  119.2 9.7 %collective-permute-start.21 = (f32[4,4,32,128]{3,2,1,0:T(8,128)S(1)}, f32[4,4,32,128]{3,2,1,0:T(8,128)S(1)}, u32[]{:S(2)}, u32[]{:S(2)}) collective-permute-start(f32[4,4,32,128]{3,2,1,0:T(8,128)S(1)} %get-tuple-element.40), channel_id=1, source_target_pairs={{0,1},{1,2},{2,3},{3,4},{4,5},{5,6},{6,7},{7,8},{8,9},{9,10},{10,1... | collective-permute-start | bytes 786440 | tf_op jit(solution)/shard_map/ppermute | solution.py:21
  119.3 9.6 %collective-permute-start.22 = (f32[4,32,4,128]{3,2,1,0:T(4,128)S(1)}, f32[4,32,4,128]{3,2,1,0:T(4,128)S(1)}, u32[]{:S(2)}, u32[]{:S(2)}) collective-permute-start(f32[4,32,4,128]{3,2,1,0:T(4,128)S(1)} %get-tuple-element.37), channel_id=1, source_target_pairs={{16,0},{32,16},{48,32},{64,48},{80,64},{96,80},{112,96},{128,112},... | collective-permute-start | bytes 786440 | tf_op jit(solution)/shard_map/ppermute | solution.py:22
  119.3 9.6 %collective-permute-start.23 = (f32[4,32,4,128]{3,2,1,0:T(4,128)S(1)}, f32[4,32,4,128]{3,2,1,0:T(4,128)S(1)}, u32[]{:S(2)}, u32[]{:S(2)}) collective-permute-start(f32[4,32,4,128]{3,2,1,0:T(4,128)S(1)} %get-tuple-element.38), channel_id=1, source_target_pairs={{0,16},{16,32},{32,48},{48,64},{64,80},{80,96},{96,112},{112,128},... | collective-permute-start | bytes 786440 | tf_op jit(solution)/shard_map/ppermute | solution.py:21
  136.7 6.6 %collective-permute-start.24 = (f32[4,4,32,128]{3,2,1,0:T(8,128)S(1)}, f32[4,4,32,128]{3,2,1,0:T(8,128)S(1)}, u32[]{:S(2)}, u32[]{:S(2)}) collective-permute-start(f32[4,4,32,128]{3,2,1,0:T(8,128)S(1)} %get-tuple-element.35), channel_id=1, source_target_pairs={{1,0},{2,1},{3,2},{4,3},{5,4},{6,5},{7,6},{8,7},{9,8},{10,9},{11,1... | collective-permute-start | bytes 786440 | tf_op jit(solution)/shard_map/ppermute | solution.py:22
  139.5 9.7 %collective-permute-start.25 = (f32[4,4,32,128]{3,2,1,0:T(8,128)S(1)}, f32[4,4,32,128]{3,2,1,0:T(8,128)S(1)}, u32[]{:S(2)}, u32[]{:S(2)}) collective-permute-start(f32[4,4,32,128]{3,2,1,0:T(8,128)S(1)} %get-tuple-element.36), channel_id=1, source_target_pairs={{0,1},{1,2},{2,3},{3,4},{4,5},{5,6},{6,7},{7,8},{8,9},{9,10},{10,1... | collective-permute-start | bytes 786440 | tf_op jit(solution)/shard_map/ppermute | solution.py:21
  139.6 9.6 %collective-permute-start.26 = (f32[4,32,4,128]{3,2,1,0:T(4,128)S(1)}, f32[4,32,4,128]{3,2,1,0:T(4,128)S(1)}, u32[]{:S(2)}, u32[]{:S(2)}) collective-permute-start(f32[4,32,4,128]{3,2,1,0:T(4,128)S(1)} %get-tuple-element.33), channel_id=1, source_target_pairs={{16,0},{32,16},{48,32},{64,48},{80,64},{96,80},{112,96},{128,112},... | collective-permute-start | bytes 786440 | tf_op jit(solution)/shard_map/ppermute | solution.py:22
  139.7 9.6 %collective-permute-start.27 = (f32[4,32,4,128]{3,2,1,0:T(4,128)S(1)}, f32[4,32,4,128]{3,2,1,0:T(4,128)S(1)}, u32[]{:S(2)}, u32[]{:S(2)}) collective-permute-start(f32[4,32,4,128]{3,2,1,0:T(4,128)S(1)} %get-tuple-element.34), channel_id=1, source_target_pairs={{0,16},{16,32},{32,48},{48,64},{64,80},{80,96},{96,112},{112,128},... | collective-permute-start | bytes 786440 | tf_op jit(solution)/shard_map/ppermute | solution.py:21
  157.0 13.6 %copy-start.1 = (f32[4,32,32,128]{3,2,1,0:T(8,128)}, f32[4,32,32,128]{3,2,1,0:T(8,128)S(1)}, u32[]{:S(2)}) copy-start(f32[4,32,32,128]{3,2,1,0:T(8,128)S(1)} %fusion.44) | copy-start | bytes 6291460
  157.1 6.6 %collective-permute-start.28 = (f32[4,4,32,128]{3,2,1,0:T(8,128)S(1)}, f32[4,4,32,128]{3,2,1,0:T(8,128)S(1)}, u32[]{:S(2)}, u32[]{:S(2)}) collective-permute-start(f32[4,4,32,128]{3,2,1,0:T(8,128)S(1)} %get-tuple-element.31), channel_id=1, source_target_pairs={{1,0},{2,1},{3,2},{4,3},{5,4},{6,5},{7,6},{8,7},{9,8},{10,9},{11,1... | collective-permute-start | bytes 786440 | tf_op jit(solution)/shard_map/ppermute | solution.py:22
  159.8 9.7 %collective-permute-start.29 = (f32[4,4,32,128]{3,2,1,0:T(8,128)S(1)}, f32[4,4,32,128]{3,2,1,0:T(8,128)S(1)}, u32[]{:S(2)}, u32[]{:S(2)}) collective-permute-start(f32[4,4,32,128]{3,2,1,0:T(8,128)S(1)} %get-tuple-element.32), channel_id=1, source_target_pairs={{0,1},{1,2},{2,3},{3,4},{4,5},{5,6},{6,7},{7,8},{8,9},{9,10},{10,1... | collective-permute-start | bytes 786440 | tf_op jit(solution)/shard_map/ppermute | solution.py:21
  159.9 9.6 %collective-permute-start.30 = (f32[4,32,4,128]{3,2,1,0:T(4,128)S(1)}, f32[4,32,4,128]{3,2,1,0:T(4,128)S(1)}, u32[]{:S(2)}, u32[]{:S(2)}) collective-permute-start(f32[4,32,4,128]{3,2,1,0:T(4,128)S(1)} %get-tuple-element.29), channel_id=1, source_target_pairs={{16,0},{32,16},{48,32},{64,48},{80,64},{96,80},{112,96},{128,112},... | collective-permute-start | bytes 786440 | tf_op jit(solution)/shard_map/ppermute | solution.py:22
  160.0 9.6 %collective-permute-start.31 = (f32[4,32,4,128]{3,2,1,0:T(4,128)S(1)}, f32[4,32,4,128]{3,2,1,0:T(4,128)S(1)}, u32[]{:S(2)}, u32[]{:S(2)}) collective-permute-start(f32[4,32,4,128]{3,2,1,0:T(4,128)S(1)} %get-tuple-element.30), channel_id=1, source_target_pairs={{0,16},{16,32},{32,48},{48,64},{64,80},{80,96},{96,112},{112,128},... | collective-permute-start | bytes 786440 | tf_op jit(solution)/shard_map/ppermute | solution.py:21

commit v2 on v0

v2 whole, which is shorter than its diff:
```python
import jax
import jax.numpy as jnp
from jax import lax
from jax.experimental import pallas as pl
from jax.experimental.pallas import tpu as pltpu
from jax.sharding import PartitionSpec as P


ITERS = 8
COEFFS = (-205.0 / 72.0, 8.0 / 5.0, -1.0 / 5.0, 8.0 / 315.0, -1.0 / 560.0)
DAMPING = 0.3
HALO = 4
ZO = 8
F32 = jnp.float32


def lanes(rows, width):
    return lax.broadcasted_iota(jnp.int32, (rows, width), 1)


def stencil(u, v, w, sa, bc, s, x, z, count):
    width = u.shape[3]
    at = ZO + z
    center = u[s, HALO + x, at : at + count, :]
    lane = lanes(count, width)
    total = None
    for k in range(1, HALO + 1):
        pair = u[s, HALO + x + k, at : at + count, :] + u[s, HALO + x - k, at : at + count, :]
        pair = pair + (u[s, HALO + x, at + k : at + k + count, :] + u[s, HALO + x, at - k : at - k + count, :])
        low = jnp.where(lane >= k, pltpu.roll(center, k, 1), 0.0)
        high = jnp.where(lane < width - k, pltpu.roll(center, width - k, 1), 0.0)
        pair = pair + (low + high)
        total = COEFFS[k] * pair if total is None else total + COEFFS[k] * pair
    return (
        w[x, z : z + count, :] * center
        + sa[x, z : z + count, :] * total
        - bc[z : z + count, :] * v[s, HALO + x, at : at + count, :]
    )


def inject(step, spot, amp, v, spans, send=None, send_at=None):
    shots, width = v.shape[0], v.shape[3]
    depth = v.shape[2] - 2 * ZO

    @pl.when(spot[shots : shots + 1, :][0, 0] >= 0)
    def _():
        for s in range(shots):
            flat = spot[s : s + 1, :][0, 0]
            x = lax.div(flat, depth * width)
            z = lax.rem(lax.div(flat, width), depth)
            y = lax.rem(flat, width)
            for x_low, x_high, z_low, z_high in spans:

                @pl.when((flat >= 0) & (x >= x_low) & (x < x_high) & (z >= z_low) & (z < z_high))
                def _():
                    at = step * shots + s
                    add = jnp.where(lanes(1, width) == y, amp[at : at + 1, :], 0.0)
                    row = v[s, HALO + x, pl.ds(ZO + z, 1), :] + add
                    v[s, HALO + x, pl.ds(ZO + z, 1), :] = row
                    if send is not None:
                        send[s, x - send_at, pl.ds(z, 1), :] = row


def at_high_x(side):
    odd = lax.rem(lax.axis_index("gx"), 2)
    return odd if side == 0 else 1 - odd


def at_end(axis):
    place = lax.axis_index(axis)
    return (place == 0) | (place == lax.axis_size(axis) - 1)


def fill_depth(u, z_near, z_far, columns, depth):
    odd = lax.rem(lax.axis_index("depth"), 2) == 1
    inside = jnp.where(at_end("depth"), 0.0, 1.0).astype(F32)

    def some(x, carry):
        for s in range(u.shape[0]):
            far = z_far[s, x]
            near = z_near[s, x] * inside
            u[s, HALO + x, ZO - HALO : ZO, :] = jnp.where(odd, far, near)
            u[s, HALO + x, ZO + depth : ZO + depth + HALO, :] = jnp.where(odd, near, far)
        return carry

    lax.fori_loop(0, columns, some, 0, unroll=8)


def fill_x(side, u, got, columns, depth):
    at = at_high_x(side) * (columns + HALO)
    inside = jnp.where(at_end("gx"), 0.0, 1.0).astype(F32)
    for s in range(u.shape[0]):
        for x in range(HALO):
            row = got[s, x]
            u[s, at + x, ZO : ZO + depth, :] = row * inside if side == 0 else row


def depth_faces(v, send_near, send_far, columns, depth):
    odd = lax.rem(lax.axis_index("depth"), 2) == 1

    def face(x, carry):
        for s in range(v.shape[0]):
            low = v[s, HALO + x, ZO : ZO + HALO, :]
            high = v[s, HALO + x, ZO + depth - HALO : ZO + depth, :]
            send_near[s, x] = jnp.where(odd, high, low)
            send_far[s, x] = jnp.where(odd, low, high)
        return carry

    lax.fori_loop(0, columns, face, 0, unroll=8)


def span_loop(u, v, w, sa, bc, tiles, group):
    inner = w.shape[0] - 2 * HALO

    def some(i, carry):
        s, x = i // (inner // group), HALO + group * lax.rem(i, inner // group)
        for j in range(group):
            for z, count in tiles:
                v[s, HALO + x + j, ZO + z : ZO + z + count, :] = stencil(u, v, w, sa, bc, s, x + j, z, count)
        return carry

    lax.fori_loop(0, v.shape[0] * (inner // group), some, 0)


def ends_kernel(step, spot, amp, u_in, v_in, z_near, z_far, w, sa, bc, u, v, *out):
    del u_in, v_in
    columns, depth = w.shape[0], w.shape[1]
    fill_depth(u, z_near, z_far, columns, depth)
    span_loop(u, v, w, sa, bc, ((0, 8), (depth - 8, 8)), 12)
    inject(step, spot, amp, v, ((HALO, columns - HALO, 0, 8), (HALO, columns - HALO, depth - 8, depth)))
    if step == ITERS - 1:
        to_hbm(v, *out, ((HALO, columns - 2 * HALO),))


def middle_kernel(step, spot, amp, u, v_in, w, sa, bc, v):
    del v_in
    columns, depth = w.shape[0], w.shape[1]
    span_loop(u, v, w, sa, bc, ((8, depth - 16),), 12)
    inject(step, spot, amp, v, ((HALO, columns - HALO, 8, depth - 8),))


def edge_kernel(step, spot, amp, u_in, v_in, got_b, got_a, w, sa, bc, u, v, near, far, send_b, send_a):
    del u_in, v_in
    columns, depth = w.shape[0], w.shape[1]
    fill_x(0, u, got_b, columns, depth)
    fill_x(1, u, got_a, columns, depth)
    for s in range(u.shape[0]):
        for x in range(HALO):
            for side, send in ((0, send_b), (1, send_a)):
                at = at_high_x(side) * (columns - HALO) + x
                new = stencil(u, v, w, sa, bc, s, at, 0, depth)
                v[s, HALO + at, ZO : ZO + depth, :] = new
                send[s, x] = new
    for side, send in ((0, send_b), (1, send_a)):
        face = at_high_x(side) * (columns - HALO)
        inject(step, spot, amp, v, ((face, face + HALO, 0, depth),), send, face)
    depth_faces(v, near, far, columns, depth)


def last_kernel(step, spot, amp, u_in, v_in, out_in, got_b, got_a, w, sa, bc, u, v, out, sem):
    del u_in, v_in, out_in
    columns, depth = w.shape[0], w.shape[1]
    fill_x(0, u, got_b, columns, depth)
    fill_x(1, u, got_a, columns, depth)
    for s in range(u.shape[0]):
        for x in range(HALO):
            for at in (x, columns - HALO + x):
                v[s, HALO + at, ZO : ZO + depth, :] = stencil(u, v, w, sa, bc, s, at, 0, depth)
    inject(step, spot, amp, v, ((0, HALO, 0, depth), (columns - HALO, columns, 0, depth)))
    to_hbm(v, out, sem, ((0, HALO), (columns - HALO, HALO)))


def to_hbm(v, out, sem, spans):
    shots, depth = out.shape[0], out.shape[2]
    copies = []
    for i, (first, count) in enumerate(spans):
        for s in range(shots):
            source = v.at[s, pl.ds(HALO + first, count), pl.ds(ZO, depth), :]
            copies.append(pltpu.make_async_copy(source, out.at[s, pl.ds(first, count)], sem.at[i * shots + s]))
    for c in copies:
        c.start()
    for c in copies:
        c.wait()


def prior_kernel(u, out, sem):
    to_hbm(u, out, sem, ((0, out.shape[1]),))


def open_kernel(now, send_b, send_a, send_near, send_far, low, high, sem):
    shots, columns, depth = now.shape[0], now.shape[1], now.shape[2]
    copies = []
    for target, source in (
        (low, now.at[:, :, pl.ds(0, 8)]),
        (high, now.at[:, :, pl.ds(depth - 8, 8)]),
        (send_b, now.at[:, pl.ds(at_high_x(0) * (columns - HALO), HALO)]),
        (send_a, now.at[:, pl.ds(at_high_x(1) * (columns - HALO), HALO)]),
    ):
        copies.append(pltpu.make_async_copy(source, target, sem.at[len(copies)]))
    for c in copies:
        c.start()
    odd = lax.rem(lax.axis_index("depth"), 2) == 1
    copies[0].wait()
    copies[1].wait()

    def face(x, carry):
        for s in range(shots):
            first, last = low[s, x, 0:HALO, :], high[s, x, 8 - HALO : 8, :]
            send_near[s, x] = jnp.where(odd, last, first)
            send_far[s, x] = jnp.where(odd, first, last)
        return carry

    lax.fori_loop(0, columns, face, 0, unroll=8)
    copies[2].wait()
    copies[3].wait()


def begin_kernel(speeds, start, cells, wavelet, now, before, classes, u, v, w, sa, bc, spot, amp, kinds, sem):
    shots, columns, depth, width = now.shape
    copies = [pltpu.make_async_copy(classes, kinds, sem.at[2 * shots])]
    for i, (source, state) in enumerate(((now, u), (before, v))):
        for s in range(shots):
            target = state.at[s, pl.ds(HALO, columns), pl.ds(ZO, depth), :]
            copies.append(pltpu.make_async_copy(source.at[s], target, sem.at[i * shots + s]))
    for c in copies:
        c.start()
    total = depth * lax.axis_size("depth")
    first_x, first_z = lax.axis_index("gx") * columns, lax.axis_index("depth") * depth
    begin = start[0]

    def damping_at(z):
        ratio = (z - begin + 1).astype(F32) / jnp.broadcast_to((total - begin).astype(F32), z.shape)
        return jnp.where(z >= begin, DAMPING * ratio * ratio, 0.0)

    damping = damping_at(first_z + lax.broadcasted_iota(jnp.int32, (depth, width), 0))
    inverse = 1.0 / (1.0 + damping)
    bc[...] = (1.0 - damping) * inverse
    some = jnp.int32(-1)
    for s in range(shots):
        x, z, y = cells[s, 0] - first_x, cells[s, 1] - first_z, cells[s, 2]
        mine = (x >= 0) & (x < columns) & (z >= 0) & (z < depth)
        flat = jnp.where(mine, (x * depth + z) * width + y, -1)
        some = jnp.maximum(some, flat)
        spot[s : s + 1, :] = jnp.broadcast_to(flat, (1, width))
        scale = 1.0 / (1.0 + damping_at(jnp.broadcast_to(cells[s, 1], (1, width))))
        for step in range(wavelet.shape[0]):
            amp[step * shots + s : step * shots + s + 1, :] = wavelet[step, s] * scale
    spot[shots : shots + 1, :] = jnp.broadcast_to(some, (1, width))
    copies[0].wait()

    def column(x, carry):
        kind = kinds[x]
        speed = jnp.zeros((depth, width), F32)
        for c in range(speeds.shape[0]):
            speed = jnp.where(kind == c, speeds[c], speed)
        scaled = speed * inverse
        sa[x] = scaled
        w[x] = 2.0 * inverse + (3.0 * COEFFS[0]) * scaled
        return carry

    lax.fori_loop(0, columns, column, 0, unroll=2)
    for c in copies[1:]:
        c.wait()


VMEM = pl.BlockSpec(memory_space=pltpu.VMEM)
SMEM = pl.BlockSpec(memory_space=pltpu.SMEM)
ANY = pl.BlockSpec(memory_space=pl.ANY)


def call(kernel, out_shape, args, specs, aliases=None, flops=1_000_000, scratch=(), out_specs=None):
    return pl.pallas_call(
        kernel,
        out_shape=out_shape,
        in_specs=specs,
        out_specs=out_specs if out_specs is not None else [VMEM] * len(out_shape),
        input_output_aliases=aliases or {},
        scratch_shapes=list(scratch),
        cost_estimate=pl.CostEstimate(flops=flops, bytes_accessed=4_000_000, transcendentals=0),
        compiler_params=pltpu.CompilerParams(vmem_limit_bytes=16 * 1024 * 1024),
    )(*args)


def pairs(count):
    b = [(i, (i - 1) % count if i % 2 == 0 else (i + 1) % count) for i in range(count)]
    return b, [(i, i ^ 1) for i in range(count)]


def local(
    pressure_now, pressure_before, class_map, courant_sq, source_cells, source_wavelet, layer_start
):
    shots, columns, depth, width = pressure_now.shape
    x_b, x_a = pairs(lax.axis_size("gx"))
    z_b, z_a = pairs(lax.axis_size("depth"))
    state = pltpu.VMEM((shots, columns + 2 * HALO, depth + 2 * ZO, width), F32)
    plane = pltpu.VMEM((columns, depth, width), F32)
    row = pltpu.VMEM((depth, width), F32)
    x_face = pltpu.VMEM((shots, HALO, depth, width), F32)
    z_face = pltpu.VMEM((shots, columns, HALO, width), F32)
    dense = jax.ShapeDtypeStruct((shots, columns, depth, width), F32)
    dma = pltpu.SemaphoreType.DMA
    tile = pltpu.VMEM((shots, columns, 8, width), F32)
    now = pltpu.with_memory_space_constraint(pressure_now, pltpu.HBM)
    before = pltpu.with_memory_space_constraint(pressure_before, pltpu.HBM)
    classes = pltpu.with_memory_space_constraint(class_map, pltpu.HBM)

    def swaps(send_b, send_a, send_near, send_far):
        got = []
        for array, axis, perm in (
            (send_b, "gx", x_b), (send_a, "gx", x_a), (send_near, "depth", z_b), (send_far, "depth", z_a)
        ):
            got.append(lax.ppermute(array, axis, perm))
        return got

    sends = call(open_kernel, [x_face, x_face, z_face, z_face], (now,), [ANY], scratch=[tile, tile, dma((4,))])
    got_b, got_a, got_near, got_far = swaps(*sends)
    u, v, w, sa, bc, spot, amp = call(
        begin_kernel,
        [state, state, plane, plane, row, pltpu.VMEM((8, width), jnp.int32), pltpu.VMEM((ITERS * shots, width), F32)],
        (courant_sq, layer_start, source_cells, source_wavelet, now, before, classes),
        [SMEM] * 4 + [ANY] * 3,
        scratch=[pltpu.VMEM((columns, depth, width), jnp.int32), dma((2 * shots + 1,))],
    )
    v = middle(0, spot, amp, u, v, w, sa, bc, state)
    for step in range(ITERS - 1):
        u, v = call(
            lambda *refs, step=step: ends_kernel(step, *refs),
            [state, state],
            (spot, amp, u, v, got_near, got_far, w, sa, bc),
            [VMEM] * 9,
            {2: 0, 3: 1},
        )
        u, v, send_near, send_far, send_b, send_a = call(
            lambda *refs, step=step: edge_kernel(step, *refs),
            [state, state, z_face, z_face, x_face, x_face],
            (spot, amp, u, v, got_b, got_a, w, sa, bc),
            [VMEM] * 9,
            {2: 0, 3: 1},
        )
        got_b, got_a, got_near, got_far = swaps(send_b, send_a, send_near, send_far)
        u, v = v, u
        v = middle(step + 1, spot, amp, u, v, w, sa, bc, state)
    (prior,) = call(prior_kernel, [dense], (u,), [VMEM], scratch=[dma((shots,))], out_specs=[ANY])
    last = ITERS - 1
    u, v, final = call(
        lambda *refs: ends_kernel(last, *refs),
        [state, state, dense],
        (spot, amp, u, v, got_near, got_far, w, sa, bc),
        [VMEM] * 9,
        {2: 0, 3: 1},
        scratch=[dma((shots,))],
        out_specs=[VMEM, VMEM, ANY],
    )
    _, _, final = call(
        lambda *refs: last_kernel(last, *refs),
        [state, state, dense],
        (spot, amp, u, v, final, got_b, got_a, w, sa, bc),
        [VMEM] * 4 + [ANY] + [VMEM] * 5,
        {2: 0, 3: 1, 4: 2},
        scratch=[dma((2 * shots,))],
        out_specs=[VMEM, VMEM, ANY],
    )
    return final, prior


def middle(step, spot, amp, u, v, w, sa, bc, state):
    return call(lambda *refs: middle_kernel(step, *refs), [state], (spot, amp, u, v, w, sa, bc), [VMEM] * 7, {3: 0})[0]


def solution(mesh):
    placed = (
        P(None, "gx", "depth", None),
        P(None, "gx", "depth", None),
        P("gx", "depth", None),
        P(),
        P(),
        P(),
        P(),
    )
    return jax.shard_map(
        local,
        mesh=mesh,
        in_specs=placed,
        out_specs=(P(None, "gx", "depth", None), P(None, "gx", "depth", None)),
        check_vma=False,
    )
```

time: 229 us -> 129 us (0.56)
  the two profiles are of different devices: /device:TPU:217 before, /device:TPU:1 now
where the time goes in v2:
time: 129 us; the launch traced here: 128 us
  Pallas kernels  57.8 us (45%)
  starting transfers between devices  36.2 us (28%)
  waiting for transfers between devices  30.4 us (24%)
  local copies, waits for them, and re-layouts  2.09 us (2%)
  between operations  1.8 us (1%)
    pallas_call x27, Pallas kernels, call(): pl.pallas_call(kernel, out_shape=out_shape, in_specs=specs, out_specs=out...  57.8 us
    ppermute x32, starting transfers between devices, swaps(): got.append(lax.ppermute(array, axis, perm))  36.2 us
    ppermute x32, waiting for transfers between devices, swaps(): got.append(lax.ppermute(array, axis, perm))  30.4 us
  transfers between devices with their start and end apart: 32, of which 10 were waited for; matrix products, arithmetic and copies ran while one was open for 1% of the time, Pallas kernels for 34%

profile of v2, /device:TPU:1, one launch (start us, length us, event | category | flops | bytes accessed | tf_op | source)
XLA Modules:
  0.0 128.3 jit_solution(1366623075224838093)
XLA Ops:
  0.6 1.4 %shard_map.88 = (f32[4,4,32,128]{3,2,1,0:T(8,128)S(1)}, f32[4,4,32,128]{3,2,1,0:T(8,128)S(1)}, f32[4,32,4,128]{3,2,1,0:T(4,128)S(1)}, f32[4,32,4,128]{3,2,1,0:T(4,128)S(1)}) custom-call(f32[4,32,32,128]{3,2,1,0:T(8,128)} %now.3), custom_call_target="tpu_custom_call" | custom-call | flops 1000000 | bytes 4000000 | tf_op jit(solution)/shard_map/pallas_call | solution.py:272
  2.0 3.1 %collective-permute-start = (f32[4,32,4,128]{3,2,1,0:T(4,128)S(1)}, f32[4,32,4,128]{3,2,1,0:T(4,128)S(1)}, u32[]{:S(2)}, u32[]{:S(2)}) collective-permute-start(f32[4,32,4,128]{3,2,1,0:T(4,128)S(1)} %get-tuple-element.80), channel_id=1, source_target_pairs={{0,240},{16,32},{32,16},{48,64},{64,48},{80,96},{96,80},{112,128},... | collective-permute-start | bytes 786440 | tf_op jit(solution)/shard_map/ppermute | solution.py:312
  5.1 3.8 %collective-permute-start.1 = (f32[4,32,4,128]{3,2,1,0:T(4,128)S(1)}, f32[4,32,4,128]{3,2,1,0:T(4,128)S(1)}, u32[]{:S(2)}, u32[]{:S(2)}) collective-permute-start(f32[4,32,4,128]{3,2,1,0:T(4,128)S(1)} %get-tuple-element.81), channel_id=1, source_target_pairs={{0,16},{16,0},{32,48},{48,32},{64,80},{80,64},{96,112},{112,96},{1... | collective-permute-start | bytes 786440 | tf_op jit(solution)/shard_map/ppermute | solution.py:312
  8.9 4.9 %collective-permute-start.2 = (f32[4,4,32,128]{3,2,1,0:T(8,128)S(1)}, f32[4,4,32,128]{3,2,1,0:T(8,128)S(1)}, u32[]{:S(2)}, u32[]{:S(2)}) collective-permute-start(f32[4,4,32,128]{3,2,1,0:T(8,128)S(1)} %get-tuple-element.84), channel_id=1, source_target_pairs={{0,15},{1,2},{2,1},{3,4},{4,3},{5,6},{6,5},{7,8},{8,7},{9,10},{10,... | collective-permute-start | bytes 786440 | tf_op jit(solution)/shard_map/ppermute | solution.py:312
  14.5 0.8 copy.50.wavelet
  15.3 0.7 copy-done
  15.9 0.7 copy-done.1
  16.6 3.0 %shard_map.86 = (f32[4,40,48,128]{3,2,1,0:T(8,128)S(1)}, f32[4,40,48,128]{3,2,1,0:T(8,128)S(1)}, f32[32,32,128]{2,1,0:T(8,128)S(1)}, f32[32,32,128]{2,1,0:T(8,12...) custom-call(f32[8]{0:T(128)S(1)} %copy-done.1, s32[1]{0:T(128)S(6)} %copy.92.start, ...), custom_call_target="tpu_custom_call" | custom-call | flops 1000000 | bytes 4000000 | tf_op jit(solution)/shard_map/pallas_call | solution.py:272
  19.6 2.3 %shard_map.87.refs_3_ = f32[4,40,48,128]{3,2,1,0:T(8,128)S(1)} custom-call(s32[8,128]{1,0:T(8,128)S(1)} %get-tuple-element.73.refs_0_, f32[32,128]{1,0:T(8,128)S(1)} %get-tuple-element.74.refs_1_, f32[4,40,48,128]{3,2,1,0:T(8,128)S(1)} %get-tuple-element.75.refs_2_, ...), custom_call_target="tpu_custom_call", output_to_operand_aliasing={{}: (3, {})} | custom-call | flops 1000000 | bytes 4000000 | tf_op jit(solution)/shard_map/pallas_call | solution.py:272
  22.0 2.4 %shard_map.89 = (f32[4,40,48,128]{3,2,1,0:T(8,128)S(1)}, f32[4,40,48,128]{3,2,1,0:T(8,128)S(1)}) custom-call(s32[8,128]{1,0:T(8,128)S(1)} %get-tuple-element.73.refs_0_, f32[32,128]{1,0:T(8,128)S(1)} %get-tuple-element.74.refs_1_, f32[4,40,48,128]{3,2,1,0:T(8,128)S(1)} %get-tuple-element.75.refs_2_, ...), custom_call_target="tpu_custom_call", output_to_operand_aliasing={{0}: (2, {}), {1}: (3, {})} | custom-call | flops 1000000 | bytes 4000000 | tf_op jit(solution)/shard_map/pallas_call | solution.py:272
  24.4 1.5 %shard_map.90 = (f32[4,40,48,128]{3,2,1,0:T(8,128)S(1)}, f32[4,40,48,128]{3,2,1,0:T(8,128)S(1)}, f32[4,32,4,128]{3,2,1,0:T(4,128)S(1)}, f32[4,32,4,128]{3,2,1,0:...) custom-call(s32[8,128]{1,0:T(8,128)S(1)} %get-tuple-element.73.refs_, ...), custom_call_target="tpu_custom_call", output_to_operand_aliasing={{0}: (2, {}), {1}: (3, {})} | custom-call | flops 1000000 | bytes 4000000 | tf_op jit(solution)/shard_map/pallas_call | solution.py:272
  25.9 0.1 collective-permute-start.4
  26.0 1.1 collective-permute-start.5
  27.2 1.5 %collective-permute-start.6 = (f32[4,4,32,128]{3,2,1,0:T(8,128)S(1)}, f32[4,4,32,128]{3,2,1,0:T(8,128)S(1)}, u32[]{:S(2)}, u32[]{:S(2)}) collective-permute-start(f32[4,4,32,128]{3,2,1,0:T(8,128)S(1)} %get-tuple-element.92), channel_id=1, source_target_pairs={{0,15},{1,2},{2,1},{3,4},{4,3},{5,6},{6,5},{7,8},{8,7},{9,10},{10,... | collective-permute-start | bytes 786440 | tf_op jit(solution)/shard_map/ppermute | solution.py:312
  28.7 2.3 %shard_map.91.refs_3_ = f32[4,40,48,128]{3,2,1,0:T(8,128)S(1)} custom-call(s32[8,128]{1,0:T(8,128)S(1)} %get-tuple-element.73.refs_0_, f32[32,128]{1,0:T(8,128)S(1)} %get-tuple-element.74.refs_1_, f32[4,40,48,128]{3,2,1,0:T(8,128)S(1)} %get-tuple-element.86.refs_2_, ...), custom_call_target="tpu_custom_call", output_to_operand_aliasing={{}: (3, {})} | custom-call | flops 1000000 | bytes 4000000 | tf_op jit(solution)/shard_map/pallas_call | solution.py:272
  31.0 1.1 collective-permute-done.4.refs_4_
  32.1 2.5 %shard_map.92 = (f32[4,40,48,128]{3,2,1,0:T(8,128)S(1)}, f32[4,40,48,128]{3,2,1,0:T(8,128)S(1)}) custom-call(s32[8,128]{1,0:T(8,128)S(1)} %get-tuple-element.73.refs_0_, f32[32,128]{1,0:T(8,128)S(1)} %get-tuple-element.74.refs_1_, f32[4,40,48,128]{3,2,1,0:T(8,128)S(1)} %get-tuple-element.86.refs_2_, ...), custom_call_target="tpu_custom_call", output_to_operand_aliasing={{0}: (2, {}), {1}: (3, {})} | custom-call | flops 1000000 | bytes 4000000 | tf_op jit(solution)/shard_map/pallas_call | solution.py:272
  34.6 3.7 %collective-permute-done.6.refs_4_ = f32[4,4,32,128]{3,2,1,0:T(8,128)S(1)} collective-permute-done((f32[4,4,32,128]{3,2,1,0:T(8,128)S(1)}, f32[4,4,32,128]{3,2,1,0:T(8,128)S(1)}, u32[]{:S(2)}, u32[]{:S(2)}) %collective-permute-start.6) | collective-permute-done | bytes 262176 | tf_op jit(solution)/shard_map/ppermute | solution.py:312
  38.3 1.5 %shard_map.93 = (f32[4,40,48,128]{3,2,1,0:T(8,128)S(1)}, f32[4,40,48,128]{3,2,1,0:T(8,128)S(1)}, f32[4,32,4,128]{3,2,1,0:T(4,128)S(1)}, f32[4,32,4,128]{3,2,1,0:...) custom-call(s32[8,128]{1,0:T(8,128)S(1)} %get-tuple-element.73.refs_, ...), custom_call_target="tpu_custom_call", output_to_operand_aliasing={{0}: (2, {}), {1}: (3, {})} | custom-call | flops 1000000 | bytes 4000000 | tf_op jit(solution)/shard_map/pallas_call | solution.py:272
  39.8 1.6 %collective-permute-start.8 = (f32[4,32,4,128]{3,2,1,0:T(4,128)S(1)}, f32[4,32,4,128]{3,2,1,0:T(4,128)S(1)}, u32[]{:S(2)}, u32[]{:S(2)}) collective-permute-start(f32[4,32,4,128]{3,2,1,0:T(4,128)S(1)} %get-tuple-element.96), channel_id=1, source_target_pairs={{0,240},{16,32},{32,16},{48,64},{64,48},{80,96},{96,80},{112,128},... | collective-permute-start | bytes 786440 | tf_op jit(solution)/shard_map/ppermute | solution.py:312
  41.4 0.9 collective-permute-start.9
  42.3 1.6 %collective-permute-start.10 = (f32[4,4,32,128]{3,2,1,0:T(8,128)S(1)}, f32[4,4,32,128]{3,2,1,0:T(8,128)S(1)}, u32[]{:S(2)}, u32[]{:S(2)}) collective-permute-start(f32[4,4,32,128]{3,2,1,0:T(8,128)S(1)} %get-tuple-element.100), channel_id=1, source_target_pairs={{0,15},{1,2},{2,1},{3,4},{4,3},{5,6},{6,5},{7,8},{8,7},{9,10},{10,... | collective-permute-start | bytes 786440 | tf_op jit(solution)/shard_map/ppermute | solution.py:312
  43.9 2.3 %shard_map.94.refs_3_ = f32[4,40,48,128]{3,2,1,0:T(8,128)S(1)} custom-call(s32[8,128]{1,0:T(8,128)S(1)} %get-tuple-element.73.refs_0_, f32[32,128]{1,0:T(8,128)S(1)} %get-tuple-element.74.refs_1_, f32[4,40,48,128]{3,2,1,0:T(8,128)S(1)} %get-tuple-element.94.refs_2_, ...), custom_call_target="tpu_custom_call", output_to_operand_aliasing={{}: (3, {})} | custom-call | flops 1000000 | bytes 4000000 | tf_op jit(solution)/shard_map/pallas_call | solution.py:272
  46.2 2.6 %shard_map.95 = (f32[4,40,48,128]{3,2,1,0:T(8,128)S(1)}, f32[4,40,48,128]{3,2,1,0:T(8,128)S(1)}) custom-call(s32[8,128]{1,0:T(8,128)S(1)} %get-tuple-element.73.refs_0_, f32[32,128]{1,0:T(8,128)S(1)} %get-tuple-element.74.refs_1_, f32[4,40,48,128]{3,2,1,0:T(8,128)S(1)} %get-tuple-element.94.refs_2_, ...), custom_call_target="tpu_custom_call", output_to_operand_aliasing={{0}: (2, {}), {1}: (3, {})} | custom-call | flops 1000000 | bytes 4000000 | tf_op jit(solution)/shard_map/pallas_call | solution.py:272
  48.8 4.7 %collective-permute-done.10.refs_4_ = f32[4,4,32,128]{3,2,1,0:T(8,128)S(1)} collective-permute-done((f32[4,4,32,128]{3,2,1,0:T(8,128)S(1)}, f32[4,4,32,128]{3,2,1,0:T(8,128)S(1)}, u32[]{:S(2)}, u32[]{:S(2)}) %collective-permute-start.10) | collective-permute-done | bytes 262176 | tf_op jit(solution)/shard_map/ppermute | solution.py:312
  53.5 1.5 %shard_map.96 = (f32[4,40,48,128]{3,2,1,0:T(8,128)S(1)}, f32[4,40,48,128]{3,2,1,0:T(8,128)S(1)}, f32[4,32,4,128]{3,2,1,0:T(4,128)S(1)}, f32[4,32,4,128]{3,2,1,0:...) custom-call(s32[8,128]{1,0:T(8,128)S(1)} %get-tuple-element.73.refs_, ...), custom_call_target="tpu_custom_call", output_to_operand_aliasing={{0}: (2, {}), {1}: (3, {})} | custom-call | flops 1000000 | bytes 4000000 | tf_op jit(solution)/shard_map/pallas_call | solution.py:272
  55.0 1.1 collective-permute-start.12
  56.1 0.3 collective-permute-start.13
  56.4 1.6 %collective-permute-start.14 = (f32[4,4,32,128]{3,2,1,0:T(8,128)S(1)}, f32[4,4,32,128]{3,2,1,0:T(8,128)S(1)}, u32[]{:S(2)}, u32[]{:S(2)}) collective-permute-start(f32[4,4,32,128]{3,2,1,0:T(8,128)S(1)} %get-tuple-element.108), channel_id=1, source_target_pairs={{0,15},{1,2},{2,1},{3,4},{4,3},{5,6},{6,5},{7,8},{8,7},{9,10},{10,... | collective-permute-start | bytes 786440 | tf_op jit(solution)/shard_map/ppermute | solution.py:312
  58.0 2.3 %shard_map.97.refs_3_ = f32[4,40,48,128]{3,2,1,0:T(8,128)S(1)} custom-call(s32[8,128]{1,0:T(8,128)S(1)} %get-tuple-element.73.refs_0_, f32[32,128]{1,0:T(8,128)S(1)} %get-tuple-element.74.refs_1_, f32[4,40,48,128]{3,2,1,0:T(8,128)S(1)} %get-tuple-element.102.refs_2_, ...), custom_call_target="tpu_custom_call", output_to_operand_aliasing={{}: (3, {})} | custom-call | flops 1000000 | bytes 4000000 | tf_op jit(solution)/shard_map/pallas_call | solution.py:272
  60.3 0.9 collective-permute-done.12.refs_4_
  61.2 2.5 %shard_map.98 = (f32[4,40,48,128]{3,2,1,0:T(8,128)S(1)}, f32[4,40,48,128]{3,2,1,0:T(8,128)S(1)}) custom-call(s32[8,128]{1,0:T(8,128)S(1)} %get-tuple-element.73.refs_0_, f32[32,128]{1,0:T(8,128)S(1)} %get-tuple-element.74.refs_1_, f32[4,40,48,128]{3,2,1,0:T(8,128)S(1)} %get-tuple-element.102.refs_2_, ...), custom_call_target="tpu_custom_call", output_to_operand_aliasing={{0}: (2, {}), {1}: (3, {})} | custom-call | flops 1000000 | bytes 4000000 | tf_op jit(solution)/shard_map/pallas_call | solution.py:272
  63.6 3.8 %collective-permute-done.14.refs_4_ = f32[4,4,32,128]{3,2,1,0:T(8,128)S(1)} collective-permute-done((f32[4,4,32,128]{3,2,1,0:T(8,128)S(1)}, f32[4,4,32,128]{3,2,1,0:T(8,128)S(1)}, u32[]{:S(2)}, u32[]{:S(2)}) %collective-permute-start.14) | collective-permute-done | bytes 262176 | tf_op jit(solution)/shard_map/ppermute | solution.py:312
  67.4 1.5 %shard_map.99 = (f32[4,40,48,128]{3,2,1,0:T(8,128)S(1)}, f32[4,40,48,128]{3,2,1,0:T(8,128)S(1)}, f32[4,32,4,128]{3,2,1,0:T(4,128)S(1)}, f32[4,32,4,128]{3,2,1,0:...) custom-call(s32[8,128]{1,0:T(8,128)S(1)} %get-tuple-element.73.refs_, ...), custom_call_target="tpu_custom_call", output_to_operand_aliasing={{0}: (2, {}), {1}: (3, {})} | custom-call | flops 1000000 | bytes 4000000 | tf_op jit(solution)/shard_map/pallas_call | solution.py:272
  68.9 1.6 %collective-permute-start.16 = (f32[4,32,4,128]{3,2,1,0:T(4,128)S(1)}, f32[4,32,4,128]{3,2,1,0:T(4,128)S(1)}, u32[]{:S(2)}, u32[]{:S(2)}) collective-permute-start(f32[4,32,4,128]{3,2,1,0:T(4,128)S(1)} %get-tuple-element.112), channel_id=1, source_target_pairs={{0,240},{16,32},{32,16},{48,64},{64,48},{80,96},{96,80},{112,128},... | collective-permute-start | bytes 786440 | tf_op jit(solution)/shard_map/ppermute | solution.py:312
  70.5 1.1 collective-permute-start.17
  71.6 1.6 %collective-permute-start.18 = (f32[4,4,32,128]{3,2,1,0:T(8,128)S(1)}, f32[4,4,32,128]{3,2,1,0:T(8,128)S(1)}, u32[]{:S(2)}, u32[]{:S(2)}) collective-permute-start(f32[4,4,32,128]{3,2,1,0:T(8,128)S(1)} %get-tuple-element.116), channel_id=1, source_target_pairs={{0,15},{1,2},{2,1},{3,4},{4,3},{5,6},{6,5},{7,8},{8,7},{9,10},{10,... | collective-permute-start | bytes 786440 | tf_op jit(solution)/shard_map/ppermute | solution.py:312
  73.1 2.3 %shard_map.100.refs_3_ = f32[4,40,48,128]{3,2,1,0:T(8,128)S(1)} custom-call(s32[8,128]{1,0:T(8,128)S(1)} %get-tuple-element.73.refs_0_, f32[32,128]{1,0:T(8,128)S(1)} %get-tuple-element.74.refs_1_, f32[4,40,48,128]{3,2,1,0:T(8,128)S(1)} %get-tuple-element.110.refs_2_, ...), custom_call_target="tpu_custom_call", output_to_operand_aliasing={{}: (3, {})} | custom-call | flops 1000000 | bytes 4000000 | tf_op jit(solution)/shard_map/pallas_call | solution.py:272
  75.5 2.4 %shard_map.101 = (f32[4,40,48,128]{3,2,1,0:T(8,128)S(1)}, f32[4,40,48,128]{3,2,1,0:T(8,128)S(1)}) custom-call(s32[8,128]{1,0:T(8,128)S(1)} %get-tuple-element.73.refs_0_, f32[32,128]{1,0:T(8,128)S(1)} %get-tuple-element.74.refs_1_, f32[4,40,48,128]{3,2,1,0:T(8,128)S(1)} %get-tuple-element.110.refs_2_, ...), custom_call_target="tpu_custom_call", output_to_operand_aliasing={{0}: (2, {}), {1}: (3, {})} | custom-call | flops 1000000 | bytes 4000000 | tf_op jit(solution)/shard_map/pallas_call | solution.py:272
  77.9 4.8 %collective-permute-done.18.refs_4_ = f32[4,4,32,128]{3,2,1,0:T(8,128)S(1)} collective-permute-done((f32[4,4,32,128]{3,2,1,0:T(8,128)S(1)}, f32[4,4,32,128]{3,2,1,0:T(8,128)S(1)}, u32[]{:S(2)}, u32[]{:S(2)}) %collective-permute-start.18) | collective-permute-done | bytes 262176 | tf_op jit(solution)/shard_map/ppermute | solution.py:312
  82.7 1.5 %shard_map.102 = (f32[4,40,48,128]{3,2,1,0:T(8,128)S(1)}, f32[4,40,48,128]{3,2,1,0:T(8,128)S(1)}, f32[4,32,4,128]{3,2,1,0:T(4,128)S(1)}, f32[4,32,4,128]{3,2,1,0...) custom-call(s32[8,128]{1,0:T(8,128)S(1)} %get-tuple-element.73.refs_, ...), custom_call_target="tpu_custom_call", output_to_operand_aliasing={{0}: (2, {}), {1}: (3, {})} | custom-call | flops 1000000 | bytes 4000000 | tf_op jit(solution)/shard_map/pallas_call | solution.py:272
  84.2 1.3 %collective-permute-start.20 = (f32[4,32,4,128]{3,2,1,0:T(4,128)S(1)}, f32[4,32,4,128]{3,2,1,0:T(4,128)S(1)}, u32[]{:S(2)}, u32[]{:S(2)}) collective-permute-start(f32[4,32,4,128]{3,2,1,0:T(4,128)S(1)} %get-tuple-element.120), channel_id=1, source_target_pairs={{0,240},{16,32},{32,16},{48,64},{64,48},{80,96},{96,80},{112,128},... | collective-permute-start | bytes 786440 | tf_op jit(solution)/shard_map/ppermute | solution.py:312
  85.6 0.1 collective-permute-start.21
  85.7 1.6 %collective-permute-start.22 = (f32[4,4,32,128]{3,2,1,0:T(8,128)S(1)}, f32[4,4,32,128]{3,2,1,0:T(8,128)S(1)}, u32[]{:S(2)}, u32[]{:S(2)}) collective-permute-start(f32[4,4,32,128]{3,2,1,0:T(8,128)S(1)} %get-tuple-element.124), channel_id=1, source_target_pairs={{0,15},{1,2},{2,1},{3,4},{4,3},{5,6},{6,5},{7,8},{8,7},{9,10},{10,... | collective-permute-start | bytes 786440 | tf_op jit(solution)/shard_map/ppermute | solution.py:312
  87.2 2.3 %shard_map.103.refs_3_ = f32[4,40,48,128]{3,2,1,0:T(8,128)S(1)} custom-call(s32[8,128]{1,0:T(8,128)S(1)} %get-tuple-element.73.refs_0_, f32[32,128]{1,0:T(8,128)S(1)} %get-tuple-element.74.refs_1_, f32[4,40,48,128]{3,2,1,0:T(8,128)S(1)} %get-tuple-element.118.refs_2_, ...), custom_call_target="tpu_custom_call", output_to_operand_aliasing={{}: (3, {})} | custom-call | flops 1000000 | bytes 4000000 | tf_op jit(solution)/shard_map/pallas_call | solution.py:272
  89.5 0.9 collective-permute-done.20.refs_4_
  90.4 2.5 %shard_map.104 = (f32[4,40,48,128]{3,2,1,0:T(8,128)S(1)}, f32[4,40,48,128]{3,2,1,0:T(8,128)S(1)}) custom-call(s32[8,128]{1,0:T(8,128)S(1)} %get-tuple-element.73.refs_0_, f32[32,128]{1,0:T(8,128)S(1)} %get-tuple-element.74.refs_1_, f32[4,40,48,128]{3,2,1,0:T(8,128)S(1)} %get-tuple-element.118.refs_2_, ...), custom_call_target="tpu_custom_call", output_to_operand_aliasing={{0}: (2, {}), {1}: (3, {})} | custom-call | flops 1000000 | bytes 4000000 | tf_op jit(solution)/shard_map/pallas_call | solution.py:272
  92.9 3.5 %collective-permute-done.22.refs_4_ = f32[4,4,32,128]{3,2,1,0:T(8,128)S(1)} collective-permute-done((f32[4,4,32,128]{3,2,1,0:T(8,128)S(1)}, f32[4,4,32,128]{3,2,1,0:T(8,128)S(1)}, u32[]{:S(2)}, u32[]{:S(2)}) %collective-permute-start.22) | collective-permute-done | bytes 262176 | tf_op jit(solution)/shard_map/ppermute | solution.py:312
  96.4 1.5 %shard_map.105 = (f32[4,40,48,128]{3,2,1,0:T(8,128)S(1)}, f32[4,40,48,128]{3,2,1,0:T(8,128)S(1)}, f32[4,32,4,128]{3,2,1,0:T(4,128)S(1)}, f32[4,32,4,128]{3,2,1,0...) custom-call(s32[8,128]{1,0:T(8,128)S(1)} %get-tuple-element.73.refs_, ...), custom_call_target="tpu_custom_call", output_to_operand_aliasing={{0}: (2, {}), {1}: (3, {})} | custom-call | flops 1000000 | bytes 4000000 | tf_op jit(solution)/shard_map/pallas_call | solution.py:272
  98.0 1.8 %collective-permute-start.24 = (f32[4,32,4,128]{3,2,1,0:T(4,128)S(1)}, f32[4,32,4,128]{3,2,1,0:T(4,128)S(1)}, u32[]{:S(2)}, u32[]{:S(2)}) collective-permute-start(f32[4,32,4,128]{3,2,1,0:T(4,128)S(1)} %get-tuple-element.128), channel_id=1, source_target_pairs={{0,240},{16,32},{32,16},{48,64},{64,48},{80,96},{96,80},{112,128},... | collective-permute-start | bytes 786440 | tf_op jit(solution)/shard_map/ppermute | solution.py:312
  99.7 1.1 collective-permute-start.25
  100.8 1.6 %collective-permute-start.26 = (f32[4,4,32,128]{3,2,1,0:T(8,128)S(1)}, f32[4,4,32,128]{3,2,1,0:T(8,128)S(1)}, u32[]{:S(2)}, u32[]{:S(2)}) collective-permute-start(f32[4,4,32,128]{3,2,1,0:T(8,128)S(1)} %get-tuple-element.132), channel_id=1, source_target_pairs={{0,15},{1,2},{2,1},{3,4},{4,3},{5,6},{6,5},{7,8},{8,7},{9,10},{10,... | collective-permute-start | bytes 786440 | tf_op jit(solution)/shard_map/ppermute | solution.py:312
  102.4 2.3 %shard_map.106.refs_3_ = f32[4,40,48,128]{3,2,1,0:T(8,128)S(1)} custom-call(s32[8,128]{1,0:T(8,128)S(1)} %get-tuple-element.73.refs_0_, f32[32,128]{1,0:T(8,128)S(1)} %get-tuple-element.74.refs_1_, f32[4,40,48,128]{3,2,1,0:T(8,128)S(1)} %get-tuple-element.126.refs_2_, ...), custom_call_target="tpu_custom_call", output_to_operand_aliasing={{}: (3, {})} | custom-call | flops 1000000 | bytes 4000000 | tf_op jit(solution)/shard_map/pallas_call | solution.py:272
  104.7 2.4 %shard_map.107 = (f32[4,40,48,128]{3,2,1,0:T(8,128)S(1)}, f32[4,40,48,128]{3,2,1,0:T(8,128)S(1)}) custom-call(s32[8,128]{1,0:T(8,128)S(1)} %get-tuple-element.73.refs_0_, f32[32,128]{1,0:T(8,128)S(1)} %get-tuple-element.74.refs_1_, f32[4,40,48,128]{3,2,1,0:T(8,128)S(1)} %get-tuple-element.126.refs_2_, ...), custom_call_target="tpu_custom_call", output_to_operand_aliasing={{0}: (2, {}), {1}: (3, {})} | custom-call | flops 1000000 | bytes 4000000 | tf_op jit(solution)/shard_map/pallas_call | solution.py:272
  107.1 4.8 %collective-permute-done.26.refs_4_ = f32[4,4,32,128]{3,2,1,0:T(8,128)S(1)} collective-permute-done((f32[4,4,32,128]{3,2,1,0:T(8,128)S(1)}, f32[4,4,32,128]{3,2,1,0:T(8,128)S(1)}, u32[]{:S(2)}, u32[]{:S(2)}) %collective-permute-start.26) | collective-permute-done | bytes 262176 | tf_op jit(solution)/shard_map/ppermute | solution.py:312
  112.0 1.5 %shard_map.108 = (f32[4,40,48,128]{3,2,1,0:T(8,128)S(1)}, f32[4,40,48,128]{3,2,1,0:T(8,128)S(1)}, f32[4,32,4,128]{3,2,1,0:T(4,128)S(1)}, f32[4,32,4,128]{3,2,1,0...) custom-call(s32[8,128]{1,0:T(8,128)S(1)} %get-tuple-element.73.refs_, ...), custom_call_target="tpu_custom_call", output_to_operand_aliasing={{0}: (2, {}), {1}: (3, {})} | custom-call | flops 1000000 | bytes 4000000 | tf_op jit(solution)/shard_map/pallas_call | solution.py:272
  113.5 0.9 collective-permute-start.28
  114.4 0.5 collective-permute-start.29
  114.9 1.6 %collective-permute-start.30 = (f32[4,4,32,128]{3,2,1,0:T(8,128)S(1)}, f32[4,4,32,128]{3,2,1,0:T(8,128)S(1)}, u32[]{:S(2)}, u32[]{:S(2)}) collective-permute-start(f32[4,4,32,128]{3,2,1,0:T(8,128)S(1)} %get-tuple-element.141), channel_id=1, source_target_pairs={{0,15},{1,2},{2,1},{3,4},{4,3},{5,6},{6,5},{7,8},{8,7},{9,10},{10,... | collective-permute-start | bytes 786440 | tf_op jit(solution)/shard_map/ppermute | solution.py:312
  116.5 1.3 %shard_map.112 = f32[4,32,32,128]{3,2,1,0:T(8,128)} custom-call(f32[4,40,48,128]{3,2,1,0:T(8,128)S(1)} %get-tuple-element.134.refs_2_.u), custom_call_target="tpu_custom_call" | custom-call | flops 1000000 | bytes 4000000 | tf_op jit(solution)/shard_map/pallas_call | solution.py:272
  117.8 2.3 %shard_map.109.refs_3_ = f32[4,40,48,128]{3,2,1,0:T(8,128)S(1)} custom-call(s32[8,128]{1,0:T(8,128)S(1)} %get-tuple-element.73.refs_0_, f32[32,128]{1,0:T(8,128)S(1)} %get-tuple-element.74.refs_1_, f32[4,40,48,128]{3,2,1,0:T(8,128)S(1)} %get-tuple-element.134.refs_2_.u, ...), custom_call_target="tpu_custom_call", output_to_operand_aliasing={{}: (3, {})} | custom-call | flops 1000000 | bytes 4000000 | tf_op jit(solution)/shard_map/pallas_call | solution.py:272
  120.2 3.6 %shard_map.110 = (f32[4,40,48,128]{3,2,1,0:T(8,128)S(1)}, f32[4,40,48,128]{3,2,1,0:T(8,128)S(1)}, f32[4,32,32,128]{3,2,1,0:T(8,128)}) custom-call(s32[8,128]{1,0:T(8,128)S(1)} %get-tuple-element.73.refs_0_, f32[32,128]{1,0:T(8,128)S(1)} %get-tuple-element.74.refs_1_, ...), custom_call_target="tpu_custom_call", output_to_operand_aliasing={{0}: (2, {}), {1}: (3, {})} | custom-call | flops 1000000 | bytes 4000000 | tf_op jit(solution)/shard_map/pallas_call | solution.py:272
  123.8 2.2 %collective-permute-done.30.refs_5_ = f32[4,4,32,128]{3,2,1,0:T(8,128)S(1)} collective-permute-done((f32[4,4,32,128]{3,2,1,0:T(8,128)S(1)}, f32[4,4,32,128]{3,2,1,0:T(8,128)S(1)}, u32[]{:S(2)}, u32[]{:S(2)}) %collective-permute-start.30) | collective-permute-done | bytes 262176 | tf_op jit(solution)/shard_map/ppermute | solution.py:312
  126.0 2.2 %shard_map.111 = (f32[4,40,48,128]{3,2,1,0:T(8,128)S(1)}, f32[4,40,48,128]{3,2,1,0:T(8,128)S(1)}, f32[4,32,32,128]{3,2,1,0:T(8,128)}) custom-call(s32[8,128]{1,0:T(8,128)S(1)} %get-tuple-element.73.refs_0_, f32[32,128]{1,0:T(8,128)S(1)} %get-tuple-element.74.refs_1_, ...), custom_call_target="tpu_custom_call", output_to_operand_aliasing={{0}: (2, {}), {1}: (3, {}), {2}: (4, {})} | custom-call | flops 1000000 | bytes 4000000 | tf_op jit(solution)/shard_map/pallas_call | solution.py:272
  (32 shorter events, 0.1 us)
Async XLA Ops:
  2.0 19.9 %collective-permute-start = (f32[4,32,4,128]{3,2,1,0:T(4,128)S(1)}, f32[4,32,4,128]{3,2,1,0:T(4,128)S(1)}, u32[]{:S(2)}, u32[]{:S(2)}) collective-permute-start(f32[4,32,4,128]{3,2,1,0:T(4,128)S(1)} %get-tuple-element.80), channel_id=1, source_target_pairs={{0,240},{16,32},{32,16},{48,64},{64,48},{80,96},{96,80},{112,128},... | collective-permute-start | bytes 786440 | tf_op jit(solution)/shard_map/ppermute | solution.py:312
  5.1 16.8 %collective-permute-start.1 = (f32[4,32,4,128]{3,2,1,0:T(4,128)S(1)}, f32[4,32,4,128]{3,2,1,0:T(4,128)S(1)}, u32[]{:S(2)}, u32[]{:S(2)}) collective-permute-start(f32[4,32,4,128]{3,2,1,0:T(4,128)S(1)} %get-tuple-element.81), channel_id=1, source_target_pairs={{0,16},{16,0},{32,48},{48,32},{64,80},{80,64},{96,112},{112,96},{1... | collective-permute-start | bytes 786440 | tf_op jit(solution)/shard_map/ppermute | solution.py:312
  8.9 15.5 %collective-permute-start.2 = (f32[4,4,32,128]{3,2,1,0:T(8,128)S(1)}, f32[4,4,32,128]{3,2,1,0:T(8,128)S(1)}, u32[]{:S(2)}, u32[]{:S(2)}) collective-permute-start(f32[4,4,32,128]{3,2,1,0:T(8,128)S(1)} %get-tuple-element.84), channel_id=1, source_target_pairs={{0,15},{1,2},{2,1},{3,4},{4,3},{5,6},{6,5},{7,8},{8,7},{9,10},{10,... | collective-permute-start | bytes 786440 | tf_op jit(solution)/shard_map/ppermute | solution.py:312
  13.8 10.6 %collective-permute-start.3 = (f32[4,4,32,128]{3,2,1,0:T(8,128)S(1)}, f32[4,4,32,128]{3,2,1,0:T(8,128)S(1)}, u32[]{:S(2)}, u32[]{:S(2)}) collective-permute-start(f32[4,4,32,128]{3,2,1,0:T(8,128)S(1)} %get-tuple-element.85), channel_id=1, source_target_pairs={{0,1},{1,0},{2,3},{3,2},{4,5},{5,4},{6,7},{7,6},{8,9},{9,8},{10,11... | collective-permute-start | bytes 786440 | tf_op jit(solution)/shard_map/ppermute | solution.py:312
  15.3 0.7 copy-start
  15.9 0.7 copy-start.1
  25.9 6.2 %collective-permute-start.4 = (f32[4,32,4,128]{3,2,1,0:T(4,128)S(1)}, f32[4,32,4,128]{3,2,1,0:T(4,128)S(1)}, u32[]{:S(2)}, u32[]{:S(2)}) collective-permute-start(f32[4,32,4,128]{3,2,1,0:T(4,128)S(1)} %get-tuple-element.88), channel_id=1, source_target_pairs={{0,240},{16,32},{32,16},{48,64},{64,48},{80,96},{96,80},{112,128},... | collective-permute-start | bytes 786440 | tf_op jit(solution)/shard_map/ppermute | solution.py:312
  26.0 6.1 %collective-permute-start.5 = (f32[4,32,4,128]{3,2,1,0:T(4,128)S(1)}, f32[4,32,4,128]{3,2,1,0:T(4,128)S(1)}, u32[]{:S(2)}, u32[]{:S(2)}) collective-permute-start(f32[4,32,4,128]{3,2,1,0:T(4,128)S(1)} %get-tuple-element.89), channel_id=1, source_target_pairs={{0,16},{16,0},{32,48},{48,32},{64,80},{80,64},{96,112},{112,96},{1... | collective-permute-start | bytes 786440 | tf_op jit(solution)/shard_map/ppermute | solution.py:312
  27.2 11.1 %collective-permute-start.6 = (f32[4,4,32,128]{3,2,1,0:T(8,128)S(1)}, f32[4,4,32,128]{3,2,1,0:T(8,128)S(1)}, u32[]{:S(2)}, u32[]{:S(2)}) collective-permute-start(f32[4,4,32,128]{3,2,1,0:T(8,128)S(1)} %get-tuple-element.92), channel_id=1, source_target_pairs={{0,15},{1,2},{2,1},{3,4},{4,3},{5,6},{6,5},{7,8},{8,7},{9,10},{10,... | collective-permute-start | bytes 786440 | tf_op jit(solution)/shard_map/ppermute | solution.py:312
  28.7 9.6 %collective-permute-start.7 = (f32[4,4,32,128]{3,2,1,0:T(8,128)S(1)}, f32[4,4,32,128]{3,2,1,0:T(8,128)S(1)}, u32[]{:S(2)}, u32[]{:S(2)}) collective-permute-start(f32[4,4,32,128]{3,2,1,0:T(8,128)S(1)} %get-tuple-element.93), channel_id=1, source_target_pairs={{0,1},{1,0},{2,3},{3,2},{4,5},{5,4},{6,7},{7,6},{8,9},{9,8},{10,11... | collective-permute-start | bytes 786440 | tf_op jit(solution)/shard_map/ppermute | solution.py:312
  39.8 6.4 %collective-permute-start.8 = (f32[4,32,4,128]{3,2,1,0:T(4,128)S(1)}, f32[4,32,4,128]{3,2,1,0:T(4,128)S(1)}, u32[]{:S(2)}, u32[]{:S(2)}) collective-permute-start(f32[4,32,4,128]{3,2,1,0:T(4,128)S(1)} %get-tuple-element.96), channel_id=1, source_target_pairs={{0,240},{16,32},{32,16},{48,64},{64,48},{80,96},{96,80},{112,128},... | collective-permute-start | bytes 786440 | tf_op jit(solution)/shard_map/ppermute | solution.py:312
  41.4 4.8 %collective-permute-start.9 = (f32[4,32,4,128]{3,2,1,0:T(4,128)S(1)}, f32[4,32,4,128]{3,2,1,0:T(4,128)S(1)}, u32[]{:S(2)}, u32[]{:S(2)}) collective-permute-start(f32[4,32,4,128]{3,2,1,0:T(4,128)S(1)} %get-tuple-element.97), channel_id=1, source_target_pairs={{0,16},{16,0},{32,48},{48,32},{64,80},{80,64},{96,112},{112,96},{1... | collective-permute-start | bytes 786440 | tf_op jit(solution)/shard_map/ppermute | solution.py:312
  42.3 11.2 %collective-permute-start.10 = (f32[4,4,32,128]{3,2,1,0:T(8,128)S(1)}, f32[4,4,32,128]{3,2,1,0:T(8,128)S(1)}, u32[]{:S(2)}, u32[]{:S(2)}) collective-permute-start(f32[4,4,32,128]{3,2,1,0:T(8,128)S(1)} %get-tuple-element.100), channel_id=1, source_target_pairs={{0,15},{1,2},{2,1},{3,4},{4,3},{5,6},{6,5},{7,8},{8,7},{9,10},{10,... | collective-permute-start | bytes 786440 | tf_op jit(solution)/shard_map/ppermute | solution.py:312
  43.9 9.6 %collective-permute-start.11 = (f32[4,4,32,128]{3,2,1,0:T(8,128)S(1)}, f32[4,4,32,128]{3,2,1,0:T(8,128)S(1)}, u32[]{:S(2)}, u32[]{:S(2)}) collective-permute-start(f32[4,4,32,128]{3,2,1,0:T(8,128)S(1)} %get-tuple-element.101), channel_id=1, source_target_pairs={{0,1},{1,0},{2,3},{3,2},{4,5},{5,4},{6,7},{7,6},{8,9},{9,8},{10,11... | collective-permute-start | bytes 786440 | tf_op jit(solution)/shard_map/ppermute | solution.py:312
  55.0 6.2 %collective-permute-start.12 = (f32[4,32,4,128]{3,2,1,0:T(4,128)S(1)}, f32[4,32,4,128]{3,2,1,0:T(4,128)S(1)}, u32[]{:S(2)}, u32[]{:S(2)}) collective-permute-start(f32[4,32,4,128]{3,2,1,0:T(4,128)S(1)} %get-tuple-element.104), channel_id=1, source_target_pairs={{0,240},{16,32},{32,16},{48,64},{64,48},{80,96},{96,80},{112,128},... | collective-permute-start | bytes 786440 | tf_op jit(solution)/shard_map/ppermute | solution.py:312
  56.1 5.1 %collective-permute-start.13 = (f32[4,32,4,128]{3,2,1,0:T(4,128)S(1)}, f32[4,32,4,128]{3,2,1,0:T(4,128)S(1)}, u32[]{:S(2)}, u32[]{:S(2)}) collective-permute-start(f32[4,32,4,128]{3,2,1,0:T(4,128)S(1)} %get-tuple-element.105), channel_id=1, source_target_pairs={{0,16},{16,0},{32,48},{48,32},{64,80},{80,64},{96,112},{112,96},{1... | collective-permute-start | bytes 786440 | tf_op jit(solution)/shard_map/ppermute | solution.py:312
  56.4 11.0 %collective-permute-start.14 = (f32[4,4,32,128]{3,2,1,0:T(8,128)S(1)}, f32[4,4,32,128]{3,2,1,0:T(8,128)S(1)}, u32[]{:S(2)}, u32[]{:S(2)}) collective-permute-start(f32[4,4,32,128]{3,2,1,0:T(8,128)S(1)} %get-tuple-element.108), channel_id=1, source_target_pairs={{0,15},{1,2},{2,1},{3,4},{4,3},{5,6},{6,5},{7,8},{8,7},{9,10},{10,... | collective-permute-start | bytes 786440 | tf_op jit(solution)/shard_map/ppermute | solution.py:312
  58.0 9.4 %collective-permute-start.15 = (f32[4,4,32,128]{3,2,1,0:T(8,128)S(1)}, f32[4,4,32,128]{3,2,1,0:T(8,128)S(1)}, u32[]{:S(2)}, u32[]{:S(2)}) collective-permute-start(f32[4,4,32,128]{3,2,1,0:T(8,128)S(1)} %get-tuple-element.109), channel_id=1, source_target_pairs={{0,1},{1,0},{2,3},{3,2},{4,5},{5,4},{6,7},{7,6},{8,9},{9,8},{10,11... | collective-permute-start | bytes 786440 | tf_op jit(solution)/shard_map/ppermute | solution.py:312
  68.9 6.5 %collective-permute-start.16 = (f32[4,32,4,128]{3,2,1,0:T(4,128)S(1)}, f32[4,32,4,128]{3,2,1,0:T(4,128)S(1)}, u32[]{:S(2)}, u32[]{:S(2)}) collective-permute-start(f32[4,32,4,128]{3,2,1,0:T(4,128)S(1)} %get-tuple-element.112), channel_id=1, source_target_pairs={{0,240},{16,32},{32,16},{48,64},{64,48},{80,96},{96,80},{112,128},... | collective-permute-start | bytes 786440 | tf_op jit(solution)/shard_map/ppermute | solution.py:312
  70.5 5.0 %collective-permute-start.17 = (f32[4,32,4,128]{3,2,1,0:T(4,128)S(1)}, f32[4,32,4,128]{3,2,1,0:T(4,128)S(1)}, u32[]{:S(2)}, u32[]{:S(2)}) collective-permute-start(f32[4,32,4,128]{3,2,1,0:T(4,128)S(1)} %get-tuple-element.113), channel_id=1, source_target_pairs={{0,16},{16,0},{32,48},{48,32},{64,80},{80,64},{96,112},{112,96},{1... | collective-permute-start | bytes 786440 | tf_op jit(solution)/shard_map/ppermute | solution.py:312
  71.6 11.2 %collective-permute-start.18 = (f32[4,4,32,128]{3,2,1,0:T(8,128)S(1)}, f32[4,4,32,128]{3,2,1,0:T(8,128)S(1)}, u32[]{:S(2)}, u32[]{:S(2)}) collective-permute-start(f32[4,4,32,128]{3,2,1,0:T(8,128)S(1)} %get-tuple-element.116), channel_id=1, source_target_pairs={{0,15},{1,2},{2,1},{3,4},{4,3},{5,6},{6,5},{7,8},{8,7},{9,10},{10,... | collective-permute-start | bytes 786440 | tf_op jit(solution)/shard_map/ppermute | solution.py:312
  73.1 9.6 %collective-permute-start.19 = (f32[4,4,32,128]{3,2,1,0:T(8,128)S(1)}, f32[4,4,32,128]{3,2,1,0:T(8,128)S(1)}, u32[]{:S(2)}, u32[]{:S(2)}) collective-permute-start(f32[4,4,32,128]{3,2,1,0:T(8,128)S(1)} %get-tuple-element.117), channel_id=1, source_target_pairs={{0,1},{1,0},{2,3},{3,2},{4,5},{5,4},{6,7},{7,6},{8,9},{9,8},{10,11... | collective-permute-start | bytes 786440 | tf_op jit(solution)/shard_map/ppermute | solution.py:312
  84.2 6.2 %collective-permute-start.20 = (f32[4,32,4,128]{3,2,1,0:T(4,128)S(1)}, f32[4,32,4,128]{3,2,1,0:T(4,128)S(1)}, u32[]{:S(2)}, u32[]{:S(2)}) collective-permute-start(f32[4,32,4,128]{3,2,1,0:T(4,128)S(1)} %get-tuple-element.120), channel_id=1, source_target_pairs={{0,240},{16,32},{32,16},{48,64},{64,48},{80,96},{96,80},{112,128},... | collective-permute-start | bytes 786440 | tf_op jit(solution)/shard_map/ppermute | solution.py:312
  85.6 4.9 %collective-permute-start.21 = (f32[4,32,4,128]{3,2,1,0:T(4,128)S(1)}, f32[4,32,4,128]{3,2,1,0:T(4,128)S(1)}, u32[]{:S(2)}, u32[]{:S(2)}) collective-permute-start(f32[4,32,4,128]{3,2,1,0:T(4,128)S(1)} %get-tuple-element.121), channel_id=1, source_target_pairs={{0,16},{16,0},{32,48},{48,32},{64,80},{80,64},{96,112},{112,96},{1... | collective-permute-start | bytes 786440 | tf_op jit(solution)/shard_map/ppermute | solution.py:312
  85.7 10.8 %collective-permute-start.22 = (f32[4,4,32,128]{3,2,1,0:T(8,128)S(1)}, f32[4,4,32,128]{3,2,1,0:T(8,128)S(1)}, u32[]{:S(2)}, u32[]{:S(2)}) collective-permute-start(f32[4,4,32,128]{3,2,1,0:T(8,128)S(1)} %get-tuple-element.124), channel_id=1, source_target_pairs={{0,15},{1,2},{2,1},{3,4},{4,3},{5,6},{6,5},{7,8},{8,7},{9,10},{10,... | collective-permute-start | bytes 786440 | tf_op jit(solution)/shard_map/ppermute | solution.py:312
  87.2 9.2 %collective-permute-start.23 = (f32[4,4,32,128]{3,2,1,0:T(8,128)S(1)}, f32[4,4,32,128]{3,2,1,0:T(8,128)S(1)}, u32[]{:S(2)}, u32[]{:S(2)}) collective-permute-start(f32[4,4,32,128]{3,2,1,0:T(8,128)S(1)} %get-tuple-element.125), channel_id=1, source_target_pairs={{0,1},{1,0},{2,3},{3,2},{4,5},{5,4},{6,7},{7,6},{8,9},{9,8},{10,11... | collective-permute-start | bytes 786440 | tf_op jit(solution)/shard_map/ppermute | solution.py:312
  98.0 6.7 %collective-permute-start.24 = (f32[4,32,4,128]{3,2,1,0:T(4,128)S(1)}, f32[4,32,4,128]{3,2,1,0:T(4,128)S(1)}, u32[]{:S(2)}, u32[]{:S(2)}) collective-permute-start(f32[4,32,4,128]{3,2,1,0:T(4,128)S(1)} %get-tuple-element.128), channel_id=1, source_target_pairs={{0,240},{16,32},{32,16},{48,64},{64,48},{80,96},{96,80},{112,128},... | collective-permute-start | bytes 786440 | tf_op jit(solution)/shard_map/ppermute | solution.py:312
  99.7 5.0 %collective-permute-start.25 = (f32[4,32,4,128]{3,2,1,0:T(4,128)S(1)}, f32[4,32,4,128]{3,2,1,0:T(4,128)S(1)}, u32[]{:S(2)}, u32[]{:S(2)}) collective-permute-start(f32[4,32,4,128]{3,2,1,0:T(4,128)S(1)} %get-tuple-element.129), channel_id=1, source_target_pairs={{0,16},{16,0},{32,48},{48,32},{64,80},{80,64},{96,112},{112,96},{1... | collective-permute-start | bytes 786440 | tf_op jit(solution)/shard_map/ppermute | solution.py:312
  100.8 11.2 %collective-permute-start.26 = (f32[4,4,32,128]{3,2,1,0:T(8,128)S(1)}, f32[4,4,32,128]{3,2,1,0:T(8,128)S(1)}, u32[]{:S(2)}, u32[]{:S(2)}) collective-permute-start(f32[4,4,32,128]{3,2,1,0:T(8,128)S(1)} %get-tuple-element.132), channel_id=1, source_target_pairs={{0,15},{1,2},{2,1},{3,4},{4,3},{5,6},{6,5},{7,8},{8,7},{9,10},{10,... | collective-permute-start | bytes 786440 | tf_op jit(solution)/shard_map/ppermute | solution.py:312
  102.4 9.6 %collective-permute-start.27 = (f32[4,4,32,128]{3,2,1,0:T(8,128)S(1)}, f32[4,4,32,128]{3,2,1,0:T(8,128)S(1)}, u32[]{:S(2)}, u32[]{:S(2)}) collective-permute-start(f32[4,4,32,128]{3,2,1,0:T(8,128)S(1)} %get-tuple-element.133), channel_id=1, source_target_pairs={{0,1},{1,0},{2,3},{3,2},{4,5},{5,4},{6,7},{7,6},{8,9},{9,8},{10,11... | collective-permute-start | bytes 786440 | tf_op jit(solution)/shard_map/ppermute | solution.py:312
  113.5 6.6 %collective-permute-start.28 = (f32[4,32,4,128]{3,2,1,0:T(4,128)S(1)}, f32[4,32,4,128]{3,2,1,0:T(4,128)S(1)}, u32[]{:S(2)}, u32[]{:S(2)}) collective-permute-start(f32[4,32,4,128]{3,2,1,0:T(4,128)S(1)} %get-tuple-element.136), channel_id=1, source_target_pairs={{0,240},{16,32},{32,16},{48,64},{64,48},{80,96},{96,80},{112,128},... | collective-permute-start | bytes 786440 | tf_op jit(solution)/shard_map/ppermute | solution.py:312
  114.4 5.7 %collective-permute-start.29 = (f32[4,32,4,128]{3,2,1,0:T(4,128)S(1)}, f32[4,32,4,128]{3,2,1,0:T(4,128)S(1)}, u32[]{:S(2)}, u32[]{:S(2)}) collective-permute-start(f32[4,32,4,128]{3,2,1,0:T(4,128)S(1)} %get-tuple-element.137), channel_id=1, source_target_pairs={{0,16},{16,0},{32,48},{48,32},{64,80},{80,64},{96,112},{112,96},{1... | collective-permute-start | bytes 786440 | tf_op jit(solution)/shard_map/ppermute | solution.py:312
  114.9 11.1 %collective-permute-start.30 = (f32[4,4,32,128]{3,2,1,0:T(8,128)S(1)}, f32[4,4,32,128]{3,2,1,0:T(8,128)S(1)}, u32[]{:S(2)}, u32[]{:S(2)}) collective-permute-start(f32[4,4,32,128]{3,2,1,0:T(8,128)S(1)} %get-tuple-element.141), channel_id=1, source_target_pairs={{0,15},{1,2},{2,1},{3,4},{4,3},{5,6},{6,5},{7,8},{8,7},{9,10},{10,... | collective-permute-start | bytes 786440 | tf_op jit(solution)/shard_map/ppermute | solution.py:312
  116.5 9.5 %collective-permute-start.31 = (f32[4,4,32,128]{3,2,1,0:T(8,128)S(1)}, f32[4,4,32,128]{3,2,1,0:T(8,128)S(1)}, u32[]{:S(2)}, u32[]{:S(2)}) collective-permute-start(f32[4,4,32,128]{3,2,1,0:T(8,128)S(1)} %get-tuple-element.142), channel_id=1, source_target_pairs={{0,1},{1,0},{2,3},{3,2},{4,5},{5,4},{6,7},{7,6},{8,9},{9,8},{10,11... | collective-permute-start | bytes 786440 | tf_op jit(solution)/shard_map/ppermute | solution.py:312

commit v3 on v2

--- a/solution.py
+++ b/solution.py
@@ -1,5 +1,6 @@
 import jax
 import jax.numpy as jnp
+import numpy as np
 from jax import lax
 from jax.experimental import pallas as pl
 from jax.experimental.pallas import tpu as pltpu
@@ -18,24 +19,56 @@
     return lax.broadcasted_iota(jnp.int32, (rows, width), 1)
 
 
-def stencil(u, v, w, sa, bc, s, x, z, count):
-    width = u.shape[3]
+def stencil(u, v, y, w, sa, bc, s, x, z, count):
     at = ZO + z
     center = u[s, HALO + x, at : at + count, :]
-    lane = lanes(count, width)
     total = None
     for k in range(1, HALO + 1):
         pair = u[s, HALO + x + k, at : at + count, :] + u[s, HALO + x - k, at : at + count, :]
         pair = pair + (u[s, HALO + x, at + k : at + k + count, :] + u[s, HALO + x, at - k : at - k + count, :])
-        low = jnp.where(lane >= k, pltpu.roll(center, k, 1), 0.0)
-        high = jnp.where(lane < width - k, pltpu.roll(center, width - k, 1), 0.0)
-        pair = pair + (low + high)
+        if k == 1:
+            pair = pair + y[s, x, z : z + count, :]
         total = COEFFS[k] * pair if total is None else total + COEFFS[k] * pair
     return (
         w[x, z : z + count, :] * center
         + sa[x, z : z + count, :] * total
         - bc[z : z + count, :] * v[s, HALO + x, at : at + count, :]
     )
+
+
+def halves(number):
+    kind = np.dtype(jnp.bfloat16)
+    high = float(np.asarray(number).astype(kind))
+    return high, float(np.asarray(number - high).astype(kind))
+
+
+def fill_band(band):
+    size = band.shape[0]
+    width = size // 2
+    i = lax.broadcasted_iota(jnp.int32, (size, size), 0)
+    j = lax.broadcasted_iota(jnp.int32, (size, size), 1)
+    right, below = j >= width, i >= width
+    apart = jnp.abs(jnp.where(below, i - width, i) - jnp.where(right, j - width, j))
+    high, low = jnp.zeros((size, size), F32), jnp.zeros((size, size), F32)
+    for k in range(1, HALO + 1):
+        parts = halves(COEFFS[k] / COEFFS[1])
+        high = jnp.where(apart == k, parts[0], high)
+        low = jnp.where(apart == k, parts[1], low)
+    band[...] = jnp.where(right, jnp.where(below, 0.0, low), high).astype(jnp.bfloat16)
+
+
+def lateral(u, band, y):
+    shots, columns, depth, width = y.shape
+
+    def shot(s, carry):
+        now = u[s, HALO : HALO + columns, ZO : ZO + depth, :].reshape(columns * depth, width)
+        high = now.astype(jnp.bfloat16)
+        low = (now - high.astype(F32)).astype(jnp.bfloat16)
+        both = jnp.dot(jnp.concatenate([high, low], axis=1), band[...], preferred_element_type=F32)
+        y[s] = (both[:, :width] + both[:, width:]).reshape(columns, depth, width)
+        return carry
+
+    lax.fori_loop(0, shots, shot, 0)
 
 
 def inject(step, spot, amp, v, spans, send=None, send_at=None):
@@ -109,37 +142,38 @@
     lax.fori_loop(0, columns, face, 0, unroll=8)
 
 
-def span_loop(u, v, w, sa, bc, tiles, group):
+def span_loop(u, v, y, w, sa, bc, tiles, group):
     inner = w.shape[0] - 2 * HALO
 
     def some(i, carry):
         s, x = i // (inner // group), HALO + group * lax.rem(i, inner // group)
         for j in range(group):
             for z, count in tiles:
-                v[s, HALO + x + j, ZO + z : ZO + z + count, :] = stencil(u, v, w, sa, bc, s, x + j, z, count)
+                v[s, HALO + x + j, ZO + z : ZO + z + count, :] = stencil(u, v, y, w, sa, bc, s, x + j, z, count)
         return carry
 
     lax.fori_loop(0, v.shape[0] * (inner // group), some, 0)
 
 
-def ends_kernel(step, spot, amp, u_in, v_in, z_near, z_far, w, sa, bc, u, v, *out):
+def ends_kernel(step, spot, amp, u_in, v_in, z_near, z_far, y, w, sa, bc, u, v, *out):
     del u_in, v_in
     columns, depth = w.shape[0], w.shape[1]
     fill_depth(u, z_near, z_far, columns, depth)
-    span_loop(u, v, w, sa, bc, ((0, 8), (depth - 8, 8)), 12)
+    span_loop(u, v, y, w, sa, bc, ((0, 8), (depth - 8, 8)), 12)
     inject(step, spot, amp, v, ((HALO, columns - HALO, 0, 8), (HALO, columns - HALO, depth - 8, depth)))
     if step == ITERS - 1:
         to_hbm(v, *out, ((HALO, columns - 2 * HALO),))
 
 
-def middle_kernel(step, spot, amp, u, v_in, w, sa, bc, v):
+def middle_kernel(step, spot, amp, u, v_in, band, w, sa, bc, v, y):
     del v_in
+    lateral(u, band, y)
     columns, depth = w.shape[0], w.shape[1]
-    span_loop(u, v, w, sa, bc, ((8, depth - 16),), 12)
+    span_loop(u, v, y, w, sa, bc, ((8, depth - 16),), 12)
     inject(step, spot, amp, v, ((HALO, columns - HALO, 8, depth - 8),))
 
 
-def edge_kernel(step, spot, amp, u_in, v_in, got_b, got_a, w, sa, bc, u, v, near, far, send_b, send_a):
+def edge_kernel(step, spot, amp, u_in, v_in, got_b, got_a, y, w, sa, bc, u, v, near, far, send_b, send_a):
     del u_in, v_in
     columns, depth = w.shape[0], w.shape[1]
     fill_x(0, u, got_b, columns, depth)
@@ -148,7 +182,7 @@
         for x in range(HALO):
             for side, send in ((0, send_b), (1, send_a)):
                 at = at_high_x(side) * (columns - HALO) + x
-                new = stencil(u, v, w, sa, bc, s, at, 0, depth)
+                new = stencil(u, v, y, w, sa, bc, s, at, 0, depth)
                 v[s, HALO + at, ZO : ZO + depth, :] = new
                 send[s, x] = new
     for side, send in ((0, send_b), (1, send_a)):
@@ -157,7 +191,7 @@
     depth_faces(v, near, far, columns, depth)
 
 
-def last_kernel(step, spot, amp, u_in, v_in, out_in, got_b, got_a, w, sa, bc, u, v, out, sem):
+def last_kernel(step, spot, amp, u_in, v_in, out_in, got_b, got_a, y, w, sa, bc, u, v, out, sem):
     del u_in, v_in, out_in
     columns, depth = w.shape[0], w.shape[1]
     fill_x(0, u, got_b, columns, depth)
@@ -165,7 +199,7 @@
     for s in range(u.shape[0]):
         for x in range(HALO):
             for at in (x, columns - HALO + x):
-                v[s, HALO + at, ZO : ZO + depth, :] = stencil(u, v, w, sa, bc, s, at, 0, depth)
+                v[s, HALO + at, ZO : ZO + depth, :] = stencil(u, v, y, w, sa, bc, s, at, 0, depth)
     inject(step, spot, amp, v, ((0, HALO, 0, depth), (columns - HALO, columns, 0, depth)))
     to_hbm(v, out, sem, ((0, HALO), (columns - HALO, HALO)))
 
@@ -215,7 +249,7 @@
     copies[3].wait()
 
 
-def begin_kernel(speeds, start, cells, wavelet, now, before, classes, u, v, w, sa, bc, spot, amp, kinds, sem):
+def begin_kernel(speeds, start, cells, wavelet, now, before, classes, u, v, w, sa, bc, spot, amp, band, kinds, sem):
     shots, columns, depth, width = now.shape
     copies = [pltpu.make_async_copy(classes, kinds, sem.at[2 * shots])]
     for i, (source, state) in enumerate(((now, u), (before, v))):
@@ -246,6 +280,7 @@
         for step in range(wavelet.shape[0]):
             amp[step * shots + s : step * shots + s + 1, :] = wavelet[step, s] * scale
     spot[shots : shots + 1, :] = jnp.broadcast_to(some, (1, width))
+    fill_band(band)
     copies[0].wait()
 
     def column(x, carry):
@@ -293,6 +328,7 @@
     x_b, x_a = pairs(lax.axis_size("gx"))
     z_b, z_a = pairs(lax.axis_size("depth"))
     state = pltpu.VMEM((shots, columns + 2 * HALO, depth + 2 * ZO, width), F32)
+    lateral_sums = pltpu.VMEM((shots, columns, depth, width), F32)
     plane = pltpu.VMEM((columns, depth, width), F32)
     row = pltpu.VMEM((depth, width), F32)
     x_face = pltpu.VMEM((shots, HALO, depth, width), F32)
@@ -314,39 +350,48 @@
 
     sends = call(open_kernel, [x_face, x_face, z_face, z_face], (now,), [ANY], scratch=[tile, tile, dma((4,))])
     got_b, got_a, got_near, got_far = swaps(*sends)
-    u, v, w, sa, bc, spot, amp = call(
+    u, v, w, sa, bc, spot, amp, band = call(
         begin_kernel,
-        [state, state, plane, plane, row, pltpu.VMEM((8, width), jnp.int32), pltpu.VMEM((ITERS * shots, width), F32)],
+        [
+            state,
+            state,
+            plane,
+            plane,
+            row,
+            pltpu.VMEM((8, width), jnp.int32),
+            pltpu.VMEM((ITERS * shots, width), F32),
+            pltpu.VMEM((2 * width, 2 * width), jnp.bfloat16),
+        ],
         (courant_sq, layer_start, source_cells, source_wavelet, now, before, classes),
         [SMEM] * 4 + [ANY] * 3,
         scratch=[pltpu.VMEM((columns, depth, width), jnp.int32), dma((2 * shots + 1,))],
     )
-    v = middle(0, spot, amp, u, v, w, sa, bc, state)
+    v, y = middle(0, spot, amp, u, v, band, w, sa, bc, state, lateral_sums)
     for step in range(ITERS - 1):
         u, v = call(
             lambda *refs, step=step: ends_kernel(step, *refs),
             [state, state],
-            (spot, amp, u, v, got_near, got_far, w, sa, bc),
-            [VMEM] * 9,
+            (spot, amp, u, v, got_near, got_far, y, w, sa, bc),
+            [VMEM] * 10,
             {2: 0, 3: 1},
         )
         u, v, send_near, send_far, send_b, send_a = call(
             lambda *refs, step=step: edge_kernel(step, *refs),
             [state, state, z_face, z_face, x_face, x_face],
-            (spot, amp, u, v, got_b, got_a, w, sa, bc),
-            [VMEM] * 9,
+            (spot, amp, u, v, got_b, got_a, y, w, sa, bc),
+            [VMEM] * 10,
             {2: 0, 3: 1},
         )
         got_b, got_a, got_near, got_far = swaps(send_b, send_a, send_near, send_far)
         u, v = v, u
-        v = middle(step + 1, spot, amp, u, v, w, sa, bc, state)
+        v, y = middle(step + 1, spot, amp, u, v, band, w, sa, bc, state, lateral_sums)
     (prior,) = call(prior_kernel, [dense], (u,), [VMEM], scratch=[dma((shots,))], out_specs=[ANY])
     last = ITERS - 1
     u, v, final = call(
         lambda *refs: ends_kernel(last, *refs),
         [state, state, dense],
-        (spot, amp, u, v, got_near, got_far, w, sa, bc),
-        [VMEM] * 9,
+        (spot, amp, u, v, got_near, got_far, y, w, sa, bc),
+        [VMEM] * 10,
         {2: 0, 3: 1},
         scratch=[dma((shots,))],
         out_specs=[VMEM, VMEM, ANY],
@@ -354,8 +399,8 @@
     _, _, final = call(
         lambda *refs: last_kernel(last, *refs),
         [state, state, dense],
-        (spot, amp, u, v, final, got_b, got_a, w, sa, bc),
-        [VMEM] * 4 + [ANY] + [VMEM] * 5,
+        (spot, amp, u, v, final, got_b, got_a, y, w, sa, bc),
+        [VMEM] * 4 + [ANY] + [VMEM] * 6,
         {2: 0, 3: 1, 4: 2},
         scratch=[dma((2 * shots,))],
         out_specs=[VMEM, VMEM, ANY],
@@ -363,8 +408,14 @@
     return final, prior
 
 
-def middle(step, spot, amp, u, v, w, sa, bc, state):
-    return call(lambda *refs: middle_kernel(step, *refs), [state], (spot, amp, u, v, w, sa, bc), [VMEM] * 7, {3: 0})[0]
+def middle(step, spot, amp, u, v, band, w, sa, bc, state, lateral_sums):
+    return call(
+        lambda *refs: middle_kernel(step, *refs),
+        [state, lateral_sums],
+        (spot, amp, u, v, band, w, sa, bc),
+        [VMEM] * 8,
+        {3: 0},
+    )
 
 
 def solution(mesh):

time: 129 us -> 121 us (0.938)
  Pallas kernels: 57.8 us -> 40.3 us
  starting transfers between devices: 36.2 us -> 41.5 us
  waiting for transfers between devices: 30.4 us -> 35.5 us
    pallas_call x27, Pallas kernels: 57.8 us -> 40.3 us  [call(): pl.pallas_call(kernel, out_shape=out_shape, in_specs=specs, out_specs=out...]
    ppermute x32, starting transfers between devices: 36.2 us -> 41.5 us  [swaps(): got.append(lax.ppermute(array, axis, perm))]
    ppermute x32, waiting for transfers between devices: 30.4 us -> 35.5 us  [swaps(): got.append(lax.ppermute(array, axis, perm))]
  transfers between devices with their start and end apart: 32 -> 32, of which waited for: 10 -> 10; matrix products, arithmetic and copies ran while one was open for 1% -> 1% of each run, Pallas kernels for 34% -> 26%
where the time goes in v3:
time: 121 us
  starting transfers between devices  41.5 us (34%)
  Pallas kernels  40.3 us (33%)
  waiting for transfers between devices  35.5 us (29%)
  local copies, waits for them, and re-layouts  2.09 us (2%)
  between operations  1.8 us (1%)
    ppermute x32, starting transfers between devices, swaps(): got.append(lax.ppermute(array, axis, perm))  41.5 us
    pallas_call x27, Pallas kernels, call(): pl.pallas_call(kernel, out_shape=out_shape, in_specs=specs, out_specs=out...  40.3 us
    ppermute x32, waiting for transfers between devices, swaps(): got.append(lax.ppermute(array, axis, perm))  35.5 us
  transfers between devices with their start and end apart: 32, of which 10 were waited for; matrix products, arithmetic and copies ran while one was open for 1% of the time, Pallas kernels for 26%

profile of v3, /device:TPU:1, one launch (start us, length us, event | category | flops | bytes accessed | tf_op | source)
XLA Modules:
  0.0 121.3 jit_solution(16446440628300346988)
XLA Ops:
  0.6 1.4 %shard_map.88 = (f32[4,4,32,128]{3,2,1,0:T(8,128)S(1)}, f32[4,4,32,128]{3,2,1,0:T(8,128)S(1)}, f32[4,32,4,128]{3,2,1,0:T(4,128)S(1)}, f32[4,32,4,128]{3,2,1,0:T(4,128)S(1)}) custom-call(f32[4,32,32,128]{3,2,1,0:T(8,128)} %now.3), custom_call_target="tpu_custom_call" | custom-call | flops 1000000 | bytes 4000000 | tf_op jit(solution)/shard_map/pallas_call | solution.py:307
  2.0 3.1 %collective-permute-start = (f32[4,32,4,128]{3,2,1,0:T(4,128)S(1)}, f32[4,32,4,128]{3,2,1,0:T(4,128)S(1)}, u32[]{:S(2)}, u32[]{:S(2)}) collective-permute-start(f32[4,32,4,128]{3,2,1,0:T(4,128)S(1)} %get-tuple-element.99), channel_id=1, source_target_pairs={{0,240},{16,32},{32,16},{48,64},{64,48},{80,96},{96,80},{112,128},... | collective-permute-start | bytes 786440 | tf_op jit(solution)/shard_map/ppermute | solution.py:348
  5.1 3.8 %collective-permute-start.1 = (f32[4,32,4,128]{3,2,1,0:T(4,128)S(1)}, f32[4,32,4,128]{3,2,1,0:T(4,128)S(1)}, u32[]{:S(2)}, u32[]{:S(2)}) collective-permute-start(f32[4,32,4,128]{3,2,1,0:T(4,128)S(1)} %get-tuple-element.100), channel_id=1, source_target_pairs={{0,16},{16,0},{32,48},{48,32},{64,80},{80,64},{96,112},{112,96},{1... | collective-permute-start | bytes 786440 | tf_op jit(solution)/shard_map/ppermute | solution.py:348
  8.9 4.9 %collective-permute-start.2 = (f32[4,4,32,128]{3,2,1,0:T(8,128)S(1)}, f32[4,4,32,128]{3,2,1,0:T(8,128)S(1)}, u32[]{:S(2)}, u32[]{:S(2)}) collective-permute-start(f32[4,4,32,128]{3,2,1,0:T(8,128)S(1)} %get-tuple-element.104), channel_id=1, source_target_pairs={{0,15},{1,2},{2,1},{3,4},{4,3},{5,6},{6,5},{7,8},{8,7},{9,10},{10,... | collective-permute-start | bytes 786440 | tf_op jit(solution)/shard_map/ppermute | solution.py:348
  14.5 0.8 copy.50.wavelet
  15.3 0.7 copy-done
  15.9 0.7 copy-done.1
  16.6 3.0 %shard_map.86 = (f32[4,40,48,128]{3,2,1,0:T(8,128)S(1)}, f32[4,40,48,128]{3,2,1,0:T(8,128)S(1)}, f32[32,32,128]{2,1,0:T(8,128)S(1)}, f32[32,32,128]{2,1,0:T(8,12...) custom-call(f32[8]{0:T(128)S(1)} %copy-done.1, ...), custom_call_target="tpu_custom_call" | custom-call | flops 1000000 | bytes 4000000 | tf_op jit(solution)/shard_map/pallas_call | solution.py:307
  19.6 2.2 %shard_map.87 = (f32[4,40,48,128]{3,2,1,0:T(8,128)S(1)}, f32[4,32,32,128]{3,2,1,0:T(8,128)S(1)}) custom-call(s32[8,128]{1,0:T(8,128)S(1)} %get-tuple-element.90.refs_0_, f32[32,128]{1,0:T(8,128)S(1)} %get-tuple-element.91.refs_1_, f32[4,40,48,128]{3,2,1,0:T(8,128)S(1)} %get-tuple-element.92.refs_2_, ...), custom_call_target="tpu_custom_call", output_to_operand_aliasing={{0}: (3, {})} | custom-call | flops 1000000 | bytes 4000000 | tf_op jit(solution)/shard_map/pallas_call | solution.py:307
  21.8 1.0 shard_map.89
  22.9 0.8 shard_map.90
  23.7 0.1 collective-permute-start.4
  23.8 1.1 collective-permute-start.5
  24.9 2.5 %collective-permute-start.6 = (f32[4,4,32,128]{3,2,1,0:T(8,128)S(1)}, f32[4,4,32,128]{3,2,1,0:T(8,128)S(1)}, u32[]{:S(2)}, u32[]{:S(2)}) collective-permute-start(f32[4,4,32,128]{3,2,1,0:T(8,128)S(1)} %get-tuple-element.114), channel_id=1, source_target_pairs={{0,15},{1,2},{2,1},{3,4},{4,3},{5,6},{6,5},{7,8},{8,7},{9,10},{10,... | collective-permute-start | bytes 786440 | tf_op jit(solution)/shard_map/ppermute | solution.py:348
  27.4 2.2 %shard_map.91 = (f32[4,40,48,128]{3,2,1,0:T(8,128)S(1)}, f32[4,32,32,128]{3,2,1,0:T(8,128)S(1)}) custom-call(s32[8,128]{1,0:T(8,128)S(1)} %get-tuple-element.90.refs_0_, f32[32,128]{1,0:T(8,128)S(1)} %get-tuple-element.91.refs_1_, f32[4,40,48,128]{3,2,1,0:T(8,128)S(1)} %get-tuple-element.106.refs_2_, ...), custom_call_target="tpu_custom_call", output_to_operand_aliasing={{0}: (3, {})} | custom-call | flops 1000000 | bytes 4000000 | tf_op jit(solution)/shard_map/pallas_call | solution.py:307
  29.6 0.2 collective-permute-done.4.refs_4_
  29.8 1.1 shard_map.92
  31.0 5.0 %collective-permute-done.6.refs_4_ = f32[4,4,32,128]{3,2,1,0:T(8,128)S(1)} collective-permute-done((f32[4,4,32,128]{3,2,1,0:T(8,128)S(1)}, f32[4,4,32,128]{3,2,1,0:T(8,128)S(1)}, u32[]{:S(2)}, u32[]{:S(2)}) %collective-permute-start.6) | collective-permute-done | bytes 262176 | tf_op jit(solution)/shard_map/ppermute | solution.py:348
  36.0 0.8 shard_map.93
  36.8 1.6 %collective-permute-start.8 = (f32[4,32,4,128]{3,2,1,0:T(4,128)S(1)}, f32[4,32,4,128]{3,2,1,0:T(4,128)S(1)}, u32[]{:S(2)}, u32[]{:S(2)}) collective-permute-start(f32[4,32,4,128]{3,2,1,0:T(4,128)S(1)} %get-tuple-element.119), channel_id=1, source_target_pairs={{0,240},{16,32},{32,16},{48,64},{64,48},{80,96},{96,80},{112,128},... | collective-permute-start | bytes 786440 | tf_op jit(solution)/shard_map/ppermute | solution.py:348
  38.4 0.9 collective-permute-start.9
  39.3 2.3 %collective-permute-start.10 = (f32[4,4,32,128]{3,2,1,0:T(8,128)S(1)}, f32[4,4,32,128]{3,2,1,0:T(8,128)S(1)}, u32[]{:S(2)}, u32[]{:S(2)}) collective-permute-start(f32[4,4,32,128]{3,2,1,0:T(8,128)S(1)} %get-tuple-element.124), channel_id=1, source_target_pairs={{0,15},{1,2},{2,1},{3,4},{4,3},{5,6},{6,5},{7,8},{8,7},{9,10},{10,... | collective-permute-start | bytes 786440 | tf_op jit(solution)/shard_map/ppermute | solution.py:348
  41.6 2.2 %shard_map.94 = (f32[4,40,48,128]{3,2,1,0:T(8,128)S(1)}, f32[4,32,32,128]{3,2,1,0:T(8,128)S(1)}) custom-call(s32[8,128]{1,0:T(8,128)S(1)} %get-tuple-element.90.refs_0_, f32[32,128]{1,0:T(8,128)S(1)} %get-tuple-element.91.refs_1_, f32[4,40,48,128]{3,2,1,0:T(8,128)S(1)} %get-tuple-element.116.refs_2_, ...), custom_call_target="tpu_custom_call", output_to_operand_aliasing={{0}: (3, {})} | custom-call | flops 1000000 | bytes 4000000 | tf_op jit(solution)/shard_map/pallas_call | solution.py:307
  43.8 1.0 shard_map.95
  44.9 5.6 %collective-permute-done.10.refs_4_ = f32[4,4,32,128]{3,2,1,0:T(8,128)S(1)} collective-permute-done((f32[4,4,32,128]{3,2,1,0:T(8,128)S(1)}, f32[4,4,32,128]{3,2,1,0:T(8,128)S(1)}, u32[]{:S(2)}, u32[]{:S(2)}) %collective-permute-start.10) | collective-permute-done | bytes 262176 | tf_op jit(solution)/shard_map/ppermute | solution.py:348
  50.5 0.8 shard_map.96
  51.3 1.1 collective-permute-start.12
  52.4 0.5 collective-permute-start.13
  52.9 2.3 %collective-permute-start.14 = (f32[4,4,32,128]{3,2,1,0:T(8,128)S(1)}, f32[4,4,32,128]{3,2,1,0:T(8,128)S(1)}, u32[]{:S(2)}, u32[]{:S(2)}) collective-permute-start(f32[4,4,32,128]{3,2,1,0:T(8,128)S(1)} %get-tuple-element.134), channel_id=1, source_target_pairs={{0,15},{1,2},{2,1},{3,4},{4,3},{5,6},{6,5},{7,8},{8,7},{9,10},{10,... | collective-permute-start | bytes 786440 | tf_op jit(solution)/shard_map/ppermute | solution.py:348
  55.2 2.2 %shard_map.97 = (f32[4,40,48,128]{3,2,1,0:T(8,128)S(1)}, f32[4,32,32,128]{3,2,1,0:T(8,128)S(1)}) custom-call(s32[8,128]{1,0:T(8,128)S(1)} %get-tuple-element.90.refs_0_, f32[32,128]{1,0:T(8,128)S(1)} %get-tuple-element.91.refs_1_, f32[4,40,48,128]{3,2,1,0:T(8,128)S(1)} %get-tuple-element.126.refs_2_, ...), custom_call_target="tpu_custom_call", output_to_operand_aliasing={{0}: (3, {})} | custom-call | flops 1000000 | bytes 4000000 | tf_op jit(solution)/shard_map/pallas_call | solution.py:307
  57.4 0.1 collective-permute-done.12.refs_4_
  57.5 1.1 shard_map.98
  58.6 5.4 %collective-permute-done.14.refs_4_ = f32[4,4,32,128]{3,2,1,0:T(8,128)S(1)} collective-permute-done((f32[4,4,32,128]{3,2,1,0:T(8,128)S(1)}, f32[4,4,32,128]{3,2,1,0:T(8,128)S(1)}, u32[]{:S(2)}, u32[]{:S(2)}) %collective-permute-start.14) | collective-permute-done | bytes 262176 | tf_op jit(solution)/shard_map/ppermute | solution.py:348
  64.0 0.8 shard_map.99
  64.8 1.3 %collective-permute-start.16 = (f32[4,32,4,128]{3,2,1,0:T(4,128)S(1)}, f32[4,32,4,128]{3,2,1,0:T(4,128)S(1)}, u32[]{:S(2)}, u32[]{:S(2)}) collective-permute-start(f32[4,32,4,128]{3,2,1,0:T(4,128)S(1)} %get-tuple-element.139), channel_id=1, source_target_pairs={{0,240},{16,32},{32,16},{48,64},{64,48},{80,96},{96,80},{112,128},... | collective-permute-start | bytes 786440 | tf_op jit(solution)/shard_map/ppermute | solution.py:348
  66.0 1.1 collective-permute-start.17
  67.1 2.3 %collective-permute-start.18 = (f32[4,4,32,128]{3,2,1,0:T(8,128)S(1)}, f32[4,4,32,128]{3,2,1,0:T(8,128)S(1)}, u32[]{:S(2)}, u32[]{:S(2)}) collective-permute-start(f32[4,4,32,128]{3,2,1,0:T(8,128)S(1)} %get-tuple-element.144), channel_id=1, source_target_pairs={{0,15},{1,2},{2,1},{3,4},{4,3},{5,6},{6,5},{7,8},{8,7},{9,10},{10,... | collective-permute-start | bytes 786440 | tf_op jit(solution)/shard_map/ppermute | solution.py:348
  69.4 2.2 %shard_map.100 = (f32[4,40,48,128]{3,2,1,0:T(8,128)S(1)}, f32[4,32,32,128]{3,2,1,0:T(8,128)S(1)}) custom-call(s32[8,128]{1,0:T(8,128)S(1)} %get-tuple-element.90.refs_0_, f32[32,128]{1,0:T(8,128)S(1)} %get-tuple-element.91.refs_1_, f32[4,40,48,128]{3,2,1,0:T(8,128)S(1)} %get-tuple-element.136.refs_2_, ...), custom_call_target="tpu_custom_call", output_to_operand_aliasing={{0}: (3, {})} | custom-call | flops 1000000 | bytes 4000000 | tf_op jit(solution)/shard_map/pallas_call | solution.py:307
  71.6 1.0 shard_map.101
  72.7 5.6 %collective-permute-done.18.refs_4_ = f32[4,4,32,128]{3,2,1,0:T(8,128)S(1)} collective-permute-done((f32[4,4,32,128]{3,2,1,0:T(8,128)S(1)}, f32[4,4,32,128]{3,2,1,0:T(8,128)S(1)}, u32[]{:S(2)}, u32[]{:S(2)}) %collective-permute-start.18) | collective-permute-done | bytes 262176 | tf_op jit(solution)/shard_map/ppermute | solution.py:348
  78.3 0.8 shard_map.102
  79.1 1.3 %collective-permute-start.20 = (f32[4,32,4,128]{3,2,1,0:T(4,128)S(1)}, f32[4,32,4,128]{3,2,1,0:T(4,128)S(1)}, u32[]{:S(2)}, u32[]{:S(2)}) collective-permute-start(f32[4,32,4,128]{3,2,1,0:T(4,128)S(1)} %get-tuple-element.149), channel_id=1, source_target_pairs={{0,240},{16,32},{32,16},{48,64},{64,48},{80,96},{96,80},{112,128},... | collective-permute-start | bytes 786440 | tf_op jit(solution)/shard_map/ppermute | solution.py:348
  80.4 0.3 collective-permute-start.21
  80.7 2.3 %collective-permute-start.22 = (f32[4,4,32,128]{3,2,1,0:T(8,128)S(1)}, f32[4,4,32,128]{3,2,1,0:T(8,128)S(1)}, u32[]{:S(2)}, u32[]{:S(2)}) collective-permute-start(f32[4,4,32,128]{3,2,1,0:T(8,128)S(1)} %get-tuple-element.154), channel_id=1, source_target_pairs={{0,15},{1,2},{2,1},{3,4},{4,3},{5,6},{6,5},{7,8},{8,7},{9,10},{10,... | collective-permute-start | bytes 786440 | tf_op jit(solution)/shard_map/ppermute | solution.py:348
  83.0 2.2 %shard_map.103 = (f32[4,40,48,128]{3,2,1,0:T(8,128)S(1)}, f32[4,32,32,128]{3,2,1,0:T(8,128)S(1)}) custom-call(s32[8,128]{1,0:T(8,128)S(1)} %get-tuple-element.90.refs_0_, f32[32,128]{1,0:T(8,128)S(1)} %get-tuple-element.91.refs_1_, f32[4,40,48,128]{3,2,1,0:T(8,128)S(1)} %get-tuple-element.146.refs_2_, ...), custom_call_target="tpu_custom_call", output_to_operand_aliasing={{0}: (3, {})} | custom-call | flops 1000000 | bytes 4000000 | tf_op jit(solution)/shard_map/pallas_call | solution.py:307
  85.2 0.1 collective-permute-done.20.refs_4_
  85.2 1.1 shard_map.104
  86.4 5.2 %collective-permute-done.22.refs_4_ = f32[4,4,32,128]{3,2,1,0:T(8,128)S(1)} collective-permute-done((f32[4,4,32,128]{3,2,1,0:T(8,128)S(1)}, f32[4,4,32,128]{3,2,1,0:T(8,128)S(1)}, u32[]{:S(2)}, u32[]{:S(2)}) %collective-permute-start.22) | collective-permute-done | bytes 262176 | tf_op jit(solution)/shard_map/ppermute | solution.py:348
  91.6 0.8 shard_map.105
  92.4 1.4 %collective-permute-start.24 = (f32[4,32,4,128]{3,2,1,0:T(4,128)S(1)}, f32[4,32,4,128]{3,2,1,0:T(4,128)S(1)}, u32[]{:S(2)}, u32[]{:S(2)}) collective-permute-start(f32[4,32,4,128]{3,2,1,0:T(4,128)S(1)} %get-tuple-element.159), channel_id=1, source_target_pairs={{0,240},{16,32},{32,16},{48,64},{64,48},{80,96},{96,80},{112,128},... | collective-permute-start | bytes 786440 | tf_op jit(solution)/shard_map/ppermute | solution.py:348
  93.8 1.1 collective-permute-start.25
  94.9 2.3 %collective-permute-start.26 = (f32[4,4,32,128]{3,2,1,0:T(8,128)S(1)}, f32[4,4,32,128]{3,2,1,0:T(8,128)S(1)}, u32[]{:S(2)}, u32[]{:S(2)}) collective-permute-start(f32[4,4,32,128]{3,2,1,0:T(8,128)S(1)} %get-tuple-element.164), channel_id=1, source_target_pairs={{0,15},{1,2},{2,1},{3,4},{4,3},{5,6},{6,5},{7,8},{8,7},{9,10},{10,... | collective-permute-start | bytes 786440 | tf_op jit(solution)/shard_map/ppermute | solution.py:348
  97.2 2.4 %shard_map.106 = (f32[4,40,48,128]{3,2,1,0:T(8,128)S(1)}, f32[4,32,32,128]{3,2,1,0:T(8,128)S(1)}) custom-call(s32[8,128]{1,0:T(8,128)S(1)} %get-tuple-element.90.refs_0_, f32[32,128]{1,0:T(8,128)S(1)} %get-tuple-element.91.refs_1_, f32[4,40,48,128]{3,2,1,0:T(8,128)S(1)} %get-tuple-element.156.refs_2_, ...), custom_call_target="tpu_custom_call", output_to_operand_aliasing={{0}: (3, {})} | custom-call | flops 1000000 | bytes 4000000 | tf_op jit(solution)/shard_map/pallas_call | solution.py:307
  99.7 1.0 shard_map.107
  100.7 5.4 %collective-permute-done.26.refs_4_ = f32[4,4,32,128]{3,2,1,0:T(8,128)S(1)} collective-permute-done((f32[4,4,32,128]{3,2,1,0:T(8,128)S(1)}, f32[4,4,32,128]{3,2,1,0:T(8,128)S(1)}, u32[]{:S(2)}, u32[]{:S(2)}) %collective-permute-start.26) | collective-permute-done | bytes 262176 | tf_op jit(solution)/shard_map/ppermute | solution.py:348
  106.1 0.8 shard_map.108
  106.9 1.0 collective-permute-start.28
  107.8 0.6 collective-permute-start.29
  108.4 2.3 %collective-permute-start.30 = (f32[4,4,32,128]{3,2,1,0:T(8,128)S(1)}, f32[4,4,32,128]{3,2,1,0:T(8,128)S(1)}, u32[]{:S(2)}, u32[]{:S(2)}) collective-permute-start(f32[4,4,32,128]{3,2,1,0:T(8,128)S(1)} %get-tuple-element.175), channel_id=1, source_target_pairs={{0,15},{1,2},{2,1},{3,4},{4,3},{5,6},{6,5},{7,8},{8,7},{9,10},{10,... | collective-permute-start | bytes 786440 | tf_op jit(solution)/shard_map/ppermute | solution.py:348
  110.7 1.3 %shard_map.112 = f32[4,32,32,128]{3,2,1,0:T(8,128)} custom-call(f32[4,40,48,128]{3,2,1,0:T(8,128)S(1)} %get-tuple-element.166.refs_2_.u), custom_call_target="tpu_custom_call" | custom-call | flops 1000000 | bytes 4000000 | tf_op jit(solution)/shard_map/pallas_call | solution.py:307
  112.1 2.2 %shard_map.109 = (f32[4,40,48,128]{3,2,1,0:T(8,128)S(1)}, f32[4,32,32,128]{3,2,1,0:T(8,128)S(1)}) custom-call(s32[8,128]{1,0:T(8,128)S(1)} %get-tuple-element.90.refs_0_, f32[32,128]{1,0:T(8,128)S(1)} %get-tuple-element.91.refs_1_, f32[4,40,48,128]{3,2,1,0:T(8,128)S(1)} %get-tuple-element.166.refs_2_.u, ...), custom_call_target="tpu_custom_call", output_to_operand_aliasing={{0}: (3, {})} | custom-call | flops 1000000 | bytes 4000000 | tf_op jit(solution)/shard_map/pallas_call | solution.py:307
  114.4 2.3 %shard_map.110 = (f32[4,40,48,128]{3,2,1,0:T(8,128)S(1)}, f32[4,40,48,128]{3,2,1,0:T(8,128)S(1)}, f32[4,32,32,128]{3,2,1,0:T(8,128)}) custom-call(s32[8,128]{1,0:T(8,128)S(1)} %get-tuple-element.90.refs_0_, f32[32,128]{1,0:T(8,128)S(1)} %get-tuple-element.91.refs_1_, ...), custom_call_target="tpu_custom_call", output_to_operand_aliasing={{0}: (2, {}), {1}: (3, {})} | custom-call | flops 1000000 | bytes 4000000 | tf_op jit(solution)/shard_map/pallas_call | solution.py:307
  116.7 2.9 %collective-permute-done.30.refs_5_ = f32[4,4,32,128]{3,2,1,0:T(8,128)S(1)} collective-permute-done((f32[4,4,32,128]{3,2,1,0:T(8,128)S(1)}, f32[4,4,32,128]{3,2,1,0:T(8,128)S(1)}, u32[]{:S(2)}, u32[]{:S(2)}) %collective-permute-start.30) | collective-permute-done | bytes 262176 | tf_op jit(solution)/shard_map/ppermute | solution.py:348
  119.6 1.5 %shard_map.111 = (f32[4,40,48,128]{3,2,1,0:T(8,128)S(1)}, f32[4,40,48,128]{3,2,1,0:T(8,128)S(1)}, f32[4,32,32,128]{3,2,1,0:T(8,128)}) custom-call(s32[8,128]{1,0:T(8,128)S(1)} %get-tuple-element.90.refs_0_, f32[32,128]{1,0:T(8,128)S(1)} %get-tuple-element.91.refs_1_, ...), custom_call_target="tpu_custom_call", output_to_operand_aliasing={{0}: (2, {}), {1}: (3, {}), {2}: (4, {})} | custom-call | flops 1000000 | bytes 4000000 | tf_op jit(solution)/shard_map/pallas_call | solution.py:307
  (32 shorter events, 0.1 us)
Async XLA Ops:
  2.0 19.8 %collective-permute-start = (f32[4,32,4,128]{3,2,1,0:T(4,128)S(1)}, f32[4,32,4,128]{3,2,1,0:T(4,128)S(1)}, u32[]{:S(2)}, u32[]{:S(2)}) collective-permute-start(f32[4,32,4,128]{3,2,1,0:T(4,128)S(1)} %get-tuple-element.99), channel_id=1, source_target_pairs={{0,240},{16,32},{32,16},{48,64},{64,48},{80,96},{96,80},{112,128},... | collective-permute-start | bytes 786440 | tf_op jit(solution)/shard_map/ppermute | solution.py:348
  5.1 16.7 %collective-permute-start.1 = (f32[4,32,4,128]{3,2,1,0:T(4,128)S(1)}, f32[4,32,4,128]{3,2,1,0:T(4,128)S(1)}, u32[]{:S(2)}, u32[]{:S(2)}) collective-permute-start(f32[4,32,4,128]{3,2,1,0:T(4,128)S(1)} %get-tuple-element.100), channel_id=1, source_target_pairs={{0,16},{16,0},{32,48},{48,32},{64,80},{80,64},{96,112},{112,96},{1... | collective-permute-start | bytes 786440 | tf_op jit(solution)/shard_map/ppermute | solution.py:348
  8.9 14.0 %collective-permute-start.2 = (f32[4,4,32,128]{3,2,1,0:T(8,128)S(1)}, f32[4,4,32,128]{3,2,1,0:T(8,128)S(1)}, u32[]{:S(2)}, u32[]{:S(2)}) collective-permute-start(f32[4,4,32,128]{3,2,1,0:T(8,128)S(1)} %get-tuple-element.104), channel_id=1, source_target_pairs={{0,15},{1,2},{2,1},{3,4},{4,3},{5,6},{6,5},{7,8},{8,7},{9,10},{10,... | collective-permute-start | bytes 786440 | tf_op jit(solution)/shard_map/ppermute | solution.py:348
  13.8 9.0 %collective-permute-start.3 = (f32[4,4,32,128]{3,2,1,0:T(8,128)S(1)}, f32[4,4,32,128]{3,2,1,0:T(8,128)S(1)}, u32[]{:S(2)}, u32[]{:S(2)}) collective-permute-start(f32[4,4,32,128]{3,2,1,0:T(8,128)S(1)} %get-tuple-element.105), channel_id=1, source_target_pairs={{0,1},{1,0},{2,3},{3,2},{4,5},{5,4},{6,7},{7,6},{8,9},{9,8},{10,11... | collective-permute-start | bytes 786440 | tf_op jit(solution)/shard_map/ppermute | solution.py:348
  15.3 0.7 copy-start
  15.9 0.7 copy-start.1
  23.7 6.2 %collective-permute-start.4 = (f32[4,32,4,128]{3,2,1,0:T(4,128)S(1)}, f32[4,32,4,128]{3,2,1,0:T(4,128)S(1)}, u32[]{:S(2)}, u32[]{:S(2)}) collective-permute-start(f32[4,32,4,128]{3,2,1,0:T(4,128)S(1)} %get-tuple-element.109), channel_id=1, source_target_pairs={{0,240},{16,32},{32,16},{48,64},{64,48},{80,96},{96,80},{112,128},... | collective-permute-start | bytes 786440 | tf_op jit(solution)/shard_map/ppermute | solution.py:348
  23.8 6.1 %collective-permute-start.5 = (f32[4,32,4,128]{3,2,1,0:T(4,128)S(1)}, f32[4,32,4,128]{3,2,1,0:T(4,128)S(1)}, u32[]{:S(2)}, u32[]{:S(2)}) collective-permute-start(f32[4,32,4,128]{3,2,1,0:T(4,128)S(1)} %get-tuple-element.110), channel_id=1, source_target_pairs={{0,16},{16,0},{32,48},{48,32},{64,80},{80,64},{96,112},{112,96},{1... | collective-permute-start | bytes 786440 | tf_op jit(solution)/shard_map/ppermute | solution.py:348
  24.9 11.1 %collective-permute-start.6 = (f32[4,4,32,128]{3,2,1,0:T(8,128)S(1)}, f32[4,4,32,128]{3,2,1,0:T(8,128)S(1)}, u32[]{:S(2)}, u32[]{:S(2)}) collective-permute-start(f32[4,4,32,128]{3,2,1,0:T(8,128)S(1)} %get-tuple-element.114), channel_id=1, source_target_pairs={{0,15},{1,2},{2,1},{3,4},{4,3},{5,6},{6,5},{7,8},{8,7},{9,10},{10,... | collective-permute-start | bytes 786440 | tf_op jit(solution)/shard_map/ppermute | solution.py:348
  27.4 8.6 %collective-permute-start.7 = (f32[4,4,32,128]{3,2,1,0:T(8,128)S(1)}, f32[4,4,32,128]{3,2,1,0:T(8,128)S(1)}, u32[]{:S(2)}, u32[]{:S(2)}) collective-permute-start(f32[4,4,32,128]{3,2,1,0:T(8,128)S(1)} %get-tuple-element.115), channel_id=1, source_target_pairs={{0,1},{1,0},{2,3},{3,2},{4,5},{5,4},{6,7},{7,6},{8,9},{9,8},{10,11... | collective-permute-start | bytes 786440 | tf_op jit(solution)/shard_map/ppermute | solution.py:348
  36.8 7.0 %collective-permute-start.8 = (f32[4,32,4,128]{3,2,1,0:T(4,128)S(1)}, f32[4,32,4,128]{3,2,1,0:T(4,128)S(1)}, u32[]{:S(2)}, u32[]{:S(2)}) collective-permute-start(f32[4,32,4,128]{3,2,1,0:T(4,128)S(1)} %get-tuple-element.119), channel_id=1, source_target_pairs={{0,240},{16,32},{32,16},{48,64},{64,48},{80,96},{96,80},{112,128},... | collective-permute-start | bytes 786440 | tf_op jit(solution)/shard_map/ppermute | solution.py:348
  38.4 5.4 %collective-permute-start.9 = (f32[4,32,4,128]{3,2,1,0:T(4,128)S(1)}, f32[4,32,4,128]{3,2,1,0:T(4,128)S(1)}, u32[]{:S(2)}, u32[]{:S(2)}) collective-permute-start(f32[4,32,4,128]{3,2,1,0:T(4,128)S(1)} %get-tuple-element.120), channel_id=1, source_target_pairs={{0,16},{16,0},{32,48},{48,32},{64,80},{80,64},{96,112},{112,96},{1... | collective-permute-start | bytes 786440 | tf_op jit(solution)/shard_map/ppermute | solution.py:348
  39.3 11.2 %collective-permute-start.10 = (f32[4,4,32,128]{3,2,1,0:T(8,128)S(1)}, f32[4,4,32,128]{3,2,1,0:T(8,128)S(1)}, u32[]{:S(2)}, u32[]{:S(2)}) collective-permute-start(f32[4,4,32,128]{3,2,1,0:T(8,128)S(1)} %get-tuple-element.124), channel_id=1, source_target_pairs={{0,15},{1,2},{2,1},{3,4},{4,3},{5,6},{6,5},{7,8},{8,7},{9,10},{10,... | collective-permute-start | bytes 786440 | tf_op jit(solution)/shard_map/ppermute | solution.py:348
  41.6 8.9 %collective-permute-start.11 = (f32[4,4,32,128]{3,2,1,0:T(8,128)S(1)}, f32[4,4,32,128]{3,2,1,0:T(8,128)S(1)}, u32[]{:S(2)}, u32[]{:S(2)}) collective-permute-start(f32[4,4,32,128]{3,2,1,0:T(8,128)S(1)} %get-tuple-element.125), channel_id=1, source_target_pairs={{0,1},{1,0},{2,3},{3,2},{4,5},{5,4},{6,7},{7,6},{8,9},{9,8},{10,11... | collective-permute-start | bytes 786440 | tf_op jit(solution)/shard_map/ppermute | solution.py:348
  51.3 6.2 %collective-permute-start.12 = (f32[4,32,4,128]{3,2,1,0:T(4,128)S(1)}, f32[4,32,4,128]{3,2,1,0:T(4,128)S(1)}, u32[]{:S(2)}, u32[]{:S(2)}) collective-permute-start(f32[4,32,4,128]{3,2,1,0:T(4,128)S(1)} %get-tuple-element.129), channel_id=1, source_target_pairs={{0,240},{16,32},{32,16},{48,64},{64,48},{80,96},{96,80},{112,128},... | collective-permute-start | bytes 786440 | tf_op jit(solution)/shard_map/ppermute | solution.py:348
  52.4 5.1 %collective-permute-start.13 = (f32[4,32,4,128]{3,2,1,0:T(4,128)S(1)}, f32[4,32,4,128]{3,2,1,0:T(4,128)S(1)}, u32[]{:S(2)}, u32[]{:S(2)}) collective-permute-start(f32[4,32,4,128]{3,2,1,0:T(4,128)S(1)} %get-tuple-element.130), channel_id=1, source_target_pairs={{0,16},{16,0},{32,48},{48,32},{64,80},{80,64},{96,112},{112,96},{1... | collective-permute-start | bytes 786440 | tf_op jit(solution)/shard_map/ppermute | solution.py:348
  52.9 11.1 %collective-permute-start.14 = (f32[4,4,32,128]{3,2,1,0:T(8,128)S(1)}, f32[4,4,32,128]{3,2,1,0:T(8,128)S(1)}, u32[]{:S(2)}, u32[]{:S(2)}) collective-permute-start(f32[4,4,32,128]{3,2,1,0:T(8,128)S(1)} %get-tuple-element.134), channel_id=1, source_target_pairs={{0,15},{1,2},{2,1},{3,4},{4,3},{5,6},{6,5},{7,8},{8,7},{9,10},{10,... | collective-permute-start | bytes 786440 | tf_op jit(solution)/shard_map/ppermute | solution.py:348
  55.2 8.8 %collective-permute-start.15 = (f32[4,4,32,128]{3,2,1,0:T(8,128)S(1)}, f32[4,4,32,128]{3,2,1,0:T(8,128)S(1)}, u32[]{:S(2)}, u32[]{:S(2)}) collective-permute-start(f32[4,4,32,128]{3,2,1,0:T(8,128)S(1)} %get-tuple-element.135), channel_id=1, source_target_pairs={{0,1},{1,0},{2,3},{3,2},{4,5},{5,4},{6,7},{7,6},{8,9},{9,8},{10,11... | collective-permute-start | bytes 786440 | tf_op jit(solution)/shard_map/ppermute | solution.py:348
  64.8 6.9 %collective-permute-start.16 = (f32[4,32,4,128]{3,2,1,0:T(4,128)S(1)}, f32[4,32,4,128]{3,2,1,0:T(4,128)S(1)}, u32[]{:S(2)}, u32[]{:S(2)}) collective-permute-start(f32[4,32,4,128]{3,2,1,0:T(4,128)S(1)} %get-tuple-element.139), channel_id=1, source_target_pairs={{0,240},{16,32},{32,16},{48,64},{64,48},{80,96},{96,80},{112,128},... | collective-permute-start | bytes 786440 | tf_op jit(solution)/shard_map/ppermute | solution.py:348
  66.0 5.6 %collective-permute-start.17 = (f32[4,32,4,128]{3,2,1,0:T(4,128)S(1)}, f32[4,32,4,128]{3,2,1,0:T(4,128)S(1)}, u32[]{:S(2)}, u32[]{:S(2)}) collective-permute-start(f32[4,32,4,128]{3,2,1,0:T(4,128)S(1)} %get-tuple-element.140), channel_id=1, source_target_pairs={{0,16},{16,0},{32,48},{48,32},{64,80},{80,64},{96,112},{112,96},{1... | collective-permute-start | bytes 786440 | tf_op jit(solution)/shard_map/ppermute | solution.py:348
  67.1 11.2 %collective-permute-start.18 = (f32[4,4,32,128]{3,2,1,0:T(8,128)S(1)}, f32[4,4,32,128]{3,2,1,0:T(8,128)S(1)}, u32[]{:S(2)}, u32[]{:S(2)}) collective-permute-start(f32[4,4,32,128]{3,2,1,0:T(8,128)S(1)} %get-tuple-element.144), channel_id=1, source_target_pairs={{0,15},{1,2},{2,1},{3,4},{4,3},{5,6},{6,5},{7,8},{8,7},{9,10},{10,... | collective-permute-start | bytes 786440 | tf_op jit(solution)/shard_map/ppermute | solution.py:348
  69.4 8.9 %collective-permute-start.19 = (f32[4,4,32,128]{3,2,1,0:T(8,128)S(1)}, f32[4,4,32,128]{3,2,1,0:T(8,128)S(1)}, u32[]{:S(2)}, u32[]{:S(2)}) collective-permute-start(f32[4,4,32,128]{3,2,1,0:T(8,128)S(1)} %get-tuple-element.145), channel_id=1, source_target_pairs={{0,1},{1,0},{2,3},{3,2},{4,5},{5,4},{6,7},{7,6},{8,9},{9,8},{10,11... | collective-permute-start | bytes 786440 | tf_op jit(solution)/shard_map/ppermute | solution.py:348
  79.1 6.2 %collective-permute-start.20 = (f32[4,32,4,128]{3,2,1,0:T(4,128)S(1)}, f32[4,32,4,128]{3,2,1,0:T(4,128)S(1)}, u32[]{:S(2)}, u32[]{:S(2)}) collective-permute-start(f32[4,32,4,128]{3,2,1,0:T(4,128)S(1)} %get-tuple-element.149), channel_id=1, source_target_pairs={{0,240},{16,32},{32,16},{48,64},{64,48},{80,96},{96,80},{112,128},... | collective-permute-start | bytes 786440 | tf_op jit(solution)/shard_map/ppermute | solution.py:348
  80.4 4.8 %collective-permute-start.21 = (f32[4,32,4,128]{3,2,1,0:T(4,128)S(1)}, f32[4,32,4,128]{3,2,1,0:T(4,128)S(1)}, u32[]{:S(2)}, u32[]{:S(2)}) collective-permute-start(f32[4,32,4,128]{3,2,1,0:T(4,128)S(1)} %get-tuple-element.150), channel_id=1, source_target_pairs={{0,16},{16,0},{32,48},{48,32},{64,80},{80,64},{96,112},{112,96},{1... | collective-permute-start | bytes 786440 | tf_op jit(solution)/shard_map/ppermute | solution.py:348
  80.7 10.9 %collective-permute-start.22 = (f32[4,4,32,128]{3,2,1,0:T(8,128)S(1)}, f32[4,4,32,128]{3,2,1,0:T(8,128)S(1)}, u32[]{:S(2)}, u32[]{:S(2)}) collective-permute-start(f32[4,4,32,128]{3,2,1,0:T(8,128)S(1)} %get-tuple-element.154), channel_id=1, source_target_pairs={{0,15},{1,2},{2,1},{3,4},{4,3},{5,6},{6,5},{7,8},{8,7},{9,10},{10,... | collective-permute-start | bytes 786440 | tf_op jit(solution)/shard_map/ppermute | solution.py:348
  83.0 8.6 %collective-permute-start.23 = (f32[4,4,32,128]{3,2,1,0:T(8,128)S(1)}, f32[4,4,32,128]{3,2,1,0:T(8,128)S(1)}, u32[]{:S(2)}, u32[]{:S(2)}) collective-permute-start(f32[4,4,32,128]{3,2,1,0:T(8,128)S(1)} %get-tuple-element.155), channel_id=1, source_target_pairs={{0,1},{1,0},{2,3},{3,2},{4,5},{5,4},{6,7},{7,6},{8,9},{9,8},{10,11... | collective-permute-start | bytes 786440 | tf_op jit(solution)/shard_map/ppermute | solution.py:348
  92.4 7.2 %collective-permute-start.24 = (f32[4,32,4,128]{3,2,1,0:T(4,128)S(1)}, f32[4,32,4,128]{3,2,1,0:T(4,128)S(1)}, u32[]{:S(2)}, u32[]{:S(2)}) collective-permute-start(f32[4,32,4,128]{3,2,1,0:T(4,128)S(1)} %get-tuple-element.159), channel_id=1, source_target_pairs={{0,240},{16,32},{32,16},{48,64},{64,48},{80,96},{96,80},{112,128},... | collective-permute-start | bytes 786440 | tf_op jit(solution)/shard_map/ppermute | solution.py:348
  93.8 5.8 %collective-permute-start.25 = (f32[4,32,4,128]{3,2,1,0:T(4,128)S(1)}, f32[4,32,4,128]{3,2,1,0:T(4,128)S(1)}, u32[]{:S(2)}, u32[]{:S(2)}) collective-permute-start(f32[4,32,4,128]{3,2,1,0:T(4,128)S(1)} %get-tuple-element.160), channel_id=1, source_target_pairs={{0,16},{16,0},{32,48},{48,32},{64,80},{80,64},{96,112},{112,96},{1... | collective-permute-start | bytes 786440 | tf_op jit(solution)/shard_map/ppermute | solution.py:348
  94.9 11.2 %collective-permute-start.26 = (f32[4,4,32,128]{3,2,1,0:T(8,128)S(1)}, f32[4,4,32,128]{3,2,1,0:T(8,128)S(1)}, u32[]{:S(2)}, u32[]{:S(2)}) collective-permute-start(f32[4,4,32,128]{3,2,1,0:T(8,128)S(1)} %get-tuple-element.164), channel_id=1, source_target_pairs={{0,15},{1,2},{2,1},{3,4},{4,3},{5,6},{6,5},{7,8},{8,7},{9,10},{10,... | collective-permute-start | bytes 786440 | tf_op jit(solution)/shard_map/ppermute | solution.py:348
  97.2 8.9 %collective-permute-start.27 = (f32[4,4,32,128]{3,2,1,0:T(8,128)S(1)}, f32[4,4,32,128]{3,2,1,0:T(8,128)S(1)}, u32[]{:S(2)}, u32[]{:S(2)}) collective-permute-start(f32[4,4,32,128]{3,2,1,0:T(8,128)S(1)} %get-tuple-element.165), channel_id=1, source_target_pairs={{0,1},{1,0},{2,3},{3,2},{4,5},{5,4},{6,7},{7,6},{8,9},{9,8},{10,11... | collective-permute-start | bytes 786440 | tf_op jit(solution)/shard_map/ppermute | solution.py:348
  106.9 7.5 %collective-permute-start.28 = (f32[4,32,4,128]{3,2,1,0:T(4,128)S(1)}, f32[4,32,4,128]{3,2,1,0:T(4,128)S(1)}, u32[]{:S(2)}, u32[]{:S(2)}) collective-permute-start(f32[4,32,4,128]{3,2,1,0:T(4,128)S(1)} %get-tuple-element.169), channel_id=1, source_target_pairs={{0,240},{16,32},{32,16},{48,64},{64,48},{80,96},{96,80},{112,128},... | collective-permute-start | bytes 786440 | tf_op jit(solution)/shard_map/ppermute | solution.py:348
  107.8 6.5 %collective-permute-start.29 = (f32[4,32,4,128]{3,2,1,0:T(4,128)S(1)}, f32[4,32,4,128]{3,2,1,0:T(4,128)S(1)}, u32[]{:S(2)}, u32[]{:S(2)}) collective-permute-start(f32[4,32,4,128]{3,2,1,0:T(4,128)S(1)} %get-tuple-element.170), channel_id=1, source_target_pairs={{0,16},{16,0},{32,48},{48,32},{64,80},{80,64},{96,112},{112,96},{1... | collective-permute-start | bytes 786440 | tf_op jit(solution)/shard_map/ppermute | solution.py:348
  108.4 11.2 %collective-permute-start.30 = (f32[4,4,32,128]{3,2,1,0:T(8,128)S(1)}, f32[4,4,32,128]{3,2,1,0:T(8,128)S(1)}, u32[]{:S(2)}, u32[]{:S(2)}) collective-permute-start(f32[4,4,32,128]{3,2,1,0:T(8,128)S(1)} %get-tuple-element.175), channel_id=1, source_target_pairs={{0,15},{1,2},{2,1},{3,4},{4,3},{5,6},{6,5},{7,8},{8,7},{9,10},{10,... | collective-permute-start | bytes 786440 | tf_op jit(solution)/shard_map/ppermute | solution.py:348
  110.7 8.9 %collective-permute-start.31 = (f32[4,4,32,128]{3,2,1,0:T(8,128)S(1)}, f32[4,4,32,128]{3,2,1,0:T(8,128)S(1)}, u32[]{:S(2)}, u32[]{:S(2)}) collective-permute-start(f32[4,4,32,128]{3,2,1,0:T(8,128)S(1)} %get-tuple-element.176), channel_id=1, source_target_pairs={{0,1},{1,0},{2,3},{3,2},{4,5},{5,4},{6,7},{7,6},{8,9},{9,8},{10,11... | collective-permute-start | bytes 786440 | tf_op jit(solution)/shard_map/ppermute | solution.py:348
